TPU v7x, 32 devices: a whole 2x2x4 slice. The times are simulated.
32 devices in a mesh: dp: 2 (over x), tp: 4 (over z), cp: 4 (over y, core).
Axes of the slice: x: 2, y: 2, z: 4, core: 2. Of those that a mesh axis runs over, the one named last changes fastest.
Arguments:
- x_in: bfloat16 [2, 4096, 2048], P('dp', 'cp'), parts along dimension 0
- w_q: bfloat16 [2048, 16, 128], P(None, 'tp')
- w_k: bfloat16 [2048, 16, 128], P(None, 'tp')
- w_v: bfloat16 [2048, 16, 128], P(None, 'tp')
- w_o: bfloat16 [16, 128, 2048], P('tp')
- q_norm_w: float32 [16, 128], P('tp')
- k_norm_w: float32 [16, 128], P('tp')
- post_norm_w: float32 [2048], replicated
- grad_y: bfloat16 [2, 4096, 2048], P('dp', 'cp'), parts along dimension 0
Outputs:
- output 1: bfloat16 [2, 4096, 2048], P('dp', 'cp'), parts along dimension 0
- output 2: bfloat16 [2, 4096, 2048], P('dp', 'cp'), parts along dimension 0
- output 3: float32 [4096, 16, 128], P('dp', 'tp'), parts along dimension 0
- output 4: float32 [4096, 16, 128], P('dp', 'tp'), parts along dimension 0
- output 5: float32 [4096, 16, 128], P('dp', 'tp'), parts along dimension 0
- output 6: float32 [32, 128, 2048], P(('dp', 'tp')), parts along dimension 0
- output 7: float32 [32, 128], P(('dp', 'tp')), parts along dimension 0
- output 8: float32 [32, 128], P(('dp', 'tp')), parts along dimension 0
- output 9: float32 [4096], P('dp'), parts along dimension 0
There are 2 independent parts. A program takes and returns all parts, laid end to end along the dimension named above; an argument that names none is the same for every part.
All inputs are finite; a program needn't handle non-finite values.
Results may differ from a plain program's by a relative error of at most 0.0159639.
Values are sent between devices in bfloat16 or wider.
A program may use at most 1 GiB of HBM per device.

v0:
```python
import jax
import jax.numpy as jnp
from jax import lax
from jax.sharding import PartitionSpec as P

ROPE_THETA = 500000.0
NORM_EPS = 1e-6
MASK_VALUE = -1e30


def rope_tables(start_pos, seq_rows, head_dim):
    half_dim = head_dim // 2
    inv_freq = ROPE_THETA ** (-2.0 * jnp.arange(half_dim, dtype=jnp.float32) / head_dim)
    positions = (start_pos + jnp.arange(seq_rows)).astype(jnp.float32)
    angles = positions[:, None] * inv_freq[None, :]
    return jnp.cos(angles), jnp.sin(angles)


def apply_rope(values, cos_tab, sin_tab):
    half_dim = values.shape[-1] // 2
    low_half = values[..., :half_dim]
    high_half = values[..., half_dim:]
    cos_rows = cos_tab[:, None, :]
    sin_rows = sin_tab[:, None, :]
    return jnp.concatenate([low_half * cos_rows - high_half * sin_rows, high_half * cos_rows + low_half * sin_rows], axis=-1)


def rope_back(grad_in, cos_tab, sin_tab):
    half_dim = grad_in.shape[-1] // 2
    low_half = grad_in[..., :half_dim]
    high_half = grad_in[..., half_dim:]
    cos_rows = cos_tab[:, None, :]
    sin_rows = sin_tab[:, None, :]
    return jnp.concatenate([low_half * cos_rows + high_half * sin_rows, high_half * cos_rows - low_half * sin_rows], axis=-1)


def whole_norm(lin_out, weight, width):
    sq_sum = lax.psum(jnp.sum(lin_out * lin_out, axis=(2, 3)), "tp")
    inv_rms = lax.rsqrt(sq_sum / width + NORM_EPS)[:, :, None, None]
    normed = lin_out * inv_rms
    return normed * weight, normed, inv_rms


def whole_norm_back(grad_out, normed, inv_rms, weight, width):
    grad_weight = jnp.sum(grad_out * normed, axis=(0, 1))
    grad_normed = grad_out * weight
    dot_sum = lax.psum(jnp.sum(grad_normed * normed, axis=(2, 3)), "tp")
    grad_lin = inv_rms * (grad_normed - normed * (dot_sum / width)[:, :, None, None])
    return grad_lin, grad_weight


def attend_block(q_rot, k_blk, v_blk, stats_in, score_scale, causal):
    row_max, row_sum, out_acc = stats_in
    scores = jnp.einsum("blkgd,bmkd->bklgm", q_rot, k_blk, preferred_element_type=jnp.float32) * score_scale
    if causal:
        block_len = q_rot.shape[1]
        lower_tri = jnp.arange(block_len)[:, None] >= jnp.arange(block_len)[None, :]
        scores = jnp.where(lower_tri[:, None, :], scores, MASK_VALUE)
    new_max = jnp.maximum(row_max, jnp.max(scores, axis=-1))
    prob_blk = jnp.exp(scores - new_max[..., None])
    rescale = jnp.exp(row_max - new_max)
    new_sum = row_sum * rescale + jnp.sum(prob_blk, axis=-1)
    new_acc = out_acc * rescale[..., None] + jnp.einsum("bklgm,bmkd->bklgd", prob_blk.astype(jnp.bfloat16), v_blk, preferred_element_type=jnp.float32)
    return new_max, new_sum, new_acc


def attend_block_back(q_rot, k_blk, v_blk, grad_o, log_sum, row_delta, score_scale, causal):
    scores = jnp.einsum("blkgd,bmkd->bklgm", q_rot, k_blk, preferred_element_type=jnp.float32) * score_scale
    if causal:
        block_len = q_rot.shape[1]
        lower_tri = jnp.arange(block_len)[:, None] >= jnp.arange(block_len)[None, :]
        scores = jnp.where(lower_tri[:, None, :], scores, MASK_VALUE)
    prob_blk = jnp.exp(scores - log_sum[..., None])
    grad_v = jnp.einsum("bklgm,blkgd->bkmd", prob_blk.astype(jnp.bfloat16), grad_o, preferred_element_type=jnp.float32)
    grad_p = jnp.einsum("blkgd,bmkd->bklgm", grad_o, v_blk, preferred_element_type=jnp.float32)
    grad_s = (prob_blk * (grad_p - row_delta[..., None]) * score_scale).astype(jnp.bfloat16)
    grad_q = jnp.einsum("bklgm,bmkd->bklgd", grad_s, k_blk, preferred_element_type=jnp.float32)
    grad_k = jnp.einsum("bklgm,blkgd->bkmd", grad_s, q_rot, preferred_element_type=jnp.float32)
    return grad_q, grad_k, grad_v


def solution(mesh):
    tp_size = mesh.shape["tp"]
    cp_size = mesh.shape["cp"]
    perm_next = [(src_dev, (src_dev + 1) % cp_size) for src_dev in range(cp_size)]
    act_spec = P("dp", "cp", None)
    col_spec = P(None, "tp", None)
    part_col = P("dp", "tp", None)
    in_specs = (act_spec, col_spec, col_spec, col_spec, P("tp", None, None), P("tp", None), P("tp", None), P(None), act_spec)
    out_specs = (act_spec, act_spec, part_col, part_col, part_col, P(("dp", "tp"), None, None), P(("dp", "tp"), None), P(("dp", "tp"), None), P("dp"))

    def local_run(x_in, w_q, w_k, w_v, w_o, q_norm_w, k_norm_w, post_norm_w, grad_y):
        n_batch = x_in.shape[0]
        block_len = x_in.shape[1]
        heads_loc = w_q.shape[1]
        kv_loc = w_k.shape[1]
        head_dim = w_q.shape[2]
        group_size = heads_loc // kv_loc
        q_width = heads_loc * head_dim * tp_size
        k_width = kv_loc * head_dim * tp_size
        score_scale = head_dim ** -0.5
        cp_index = lax.axis_index("cp")
        cos_tab, sin_tab = rope_tables(cp_index * block_len, block_len, head_dim)

        q_lin = jnp.einsum("bld,dhe->blhe", x_in, w_q, preferred_element_type=jnp.float32)
        k_lin = jnp.einsum("bld,dhe->blhe", x_in, w_k, preferred_element_type=jnp.float32)
        v_lin = jnp.einsum("bld,dhe->blhe", x_in, w_v, preferred_element_type=jnp.float32)
        q_scaled, q_hat, q_inv = whole_norm(q_lin, q_norm_w, q_width)
        k_scaled, k_hat, k_inv = whole_norm(k_lin, k_norm_w, k_width)
        q_rot = apply_rope(q_scaled, cos_tab, sin_tab).astype(jnp.bfloat16).reshape(n_batch, block_len, kv_loc, group_size, head_dim)
        k_rot = apply_rope(k_scaled, cos_tab, sin_tab).astype(jnp.bfloat16)
        v_val = v_lin.astype(jnp.bfloat16)

        stat_shape = (n_batch, kv_loc, block_len, group_size)
        first_state = (jnp.full(stat_shape, MASK_VALUE, jnp.float32), jnp.zeros(stat_shape, jnp.float32), jnp.zeros(stat_shape + (head_dim,), jnp.float32))
        soft_state = attend_block(q_rot, k_rot, v_val, first_state, score_scale, True)

        def fwd_step(step_idx, loop_state):
            k_cur, v_cur, stats_in = loop_state
            k_cur, v_cur = lax.ppermute((k_cur, v_cur), "cp", perm_next)

            def use_block(stats_now):
                return attend_block(q_rot, k_cur, v_cur, stats_now, score_scale, False)

            def keep_block(stats_now):
                return stats_now

            stats_out = lax.cond(step_idx <= cp_index, use_block, keep_block, stats_in)
            return k_cur, v_cur, stats_out

        row_max, row_sum, out_acc = lax.fori_loop(1, cp_size, fwd_step, (k_rot, v_val, soft_state))[2]
        attn_out = (out_acc / row_sum[..., None]).astype(jnp.bfloat16).transpose(0, 2, 1, 3, 4).reshape(n_batch, block_len, heads_loc, head_dim)
        log_sum = row_max + jnp.log(row_sum)

        proj = lax.psum(jnp.einsum("blhe,hed->bld", attn_out, w_o, preferred_element_type=jnp.float32), "tp")
        post_inv = lax.rsqrt(jnp.mean(proj * proj, axis=-1, keepdims=True) + NORM_EPS)
        post_hat = proj * post_inv
        y_out = (x_in + post_hat * post_norm_w).astype(jnp.bfloat16)

        grad_f = grad_y.astype(jnp.float32)
        grad_post = jnp.sum(grad_f * post_hat, axis=(0, 1))
        grad_hat = grad_f * post_norm_w
        grad_proj = (post_inv * (grad_hat - post_hat * jnp.mean(grad_hat * post_hat, axis=-1, keepdims=True))).astype(jnp.bfloat16)
        grad_w_o = jnp.einsum("blhe,bld->hed", attn_out, grad_proj, preferred_element_type=jnp.float32)
        grad_attn = jnp.einsum("bld,hed->blhe", grad_proj, w_o, preferred_element_type=jnp.float32)
        row_delta = jnp.sum(grad_attn * attn_out, axis=-1).reshape(n_batch, block_len, kv_loc, group_size).transpose(0, 2, 1, 3)
        grad_o = grad_attn.astype(jnp.bfloat16).reshape(n_batch, block_len, kv_loc, group_size, head_dim)

        diag_q, diag_k, diag_v = attend_block_back(q_rot, k_rot, v_val, grad_o, log_sum, row_delta, score_scale, True)

        def bwd_step(step_idx, loop_state):
            k_cur, v_cur, dk_cur, dv_cur, dq_cur = loop_state
            k_cur, v_cur, dk_cur, dv_cur = lax.ppermute((k_cur, v_cur, dk_cur, dv_cur), "cp", perm_next)

            def use_block(acc_in):
                part_q, part_k, part_v = attend_block_back(q_rot, k_cur, v_cur, grad_o, log_sum, row_delta, score_scale, False)
                return acc_in[0] + part_q, acc_in[1] + part_k, acc_in[2] + part_v

            def keep_block(acc_in):
                return acc_in

            dq_cur, dk_cur, dv_cur = lax.cond(step_idx <= cp_index, use_block, keep_block, (dq_cur, dk_cur, dv_cur))
            return k_cur, v_cur, dk_cur, dv_cur, dq_cur

        back_state = lax.fori_loop(1, cp_size, bwd_step, (k_rot, v_val, diag_k, diag_v, diag_q))
        dk_home, dv_home = lax.ppermute((back_state[2], back_state[3]), "cp", perm_next)
        grad_q_rot = back_state[4].transpose(0, 2, 1, 3, 4).reshape(n_batch, block_len, heads_loc, head_dim)
        grad_k_rot = dk_home.transpose(0, 2, 1, 3)
        grad_v16 = dv_home.transpose(0, 2, 1, 3).astype(jnp.bfloat16)

        grad_q_lin, grad_q_norm = whole_norm_back(rope_back(grad_q_rot, cos_tab, sin_tab), q_hat, q_inv, q_norm_w, q_width)
        grad_k_lin, grad_k_norm = whole_norm_back(rope_back(grad_k_rot, cos_tab, sin_tab), k_hat, k_inv, k_norm_w, k_width)
        grad_q16 = grad_q_lin.astype(jnp.bfloat16)
        grad_k16 = grad_k_lin.astype(jnp.bfloat16)
        grad_w_q = jnp.einsum("bld,blhe->dhe", x_in, grad_q16, preferred_element_type=jnp.float32)
        grad_w_k = jnp.einsum("bld,blhe->dhe", x_in, grad_k16, preferred_element_type=jnp.float32)
        grad_w_v = jnp.einsum("bld,blhe->dhe", x_in, grad_v16, preferred_element_type=jnp.float32)
        grad_x_part = (jnp.einsum("blhe,dhe->bld", grad_q16, w_q, preferred_element_type=jnp.float32)
                       + jnp.einsum("blhe,dhe->bld", grad_k16, w_k, preferred_element_type=jnp.float32)
                       + jnp.einsum("blhe,dhe->bld", grad_v16, w_v, preferred_element_type=jnp.float32))
        grad_x = (grad_f + lax.psum(grad_x_part, "tp")).astype(jnp.bfloat16)
        weight_grads = lax.psum((grad_w_q, grad_w_k, grad_w_v, grad_w_o, grad_q_norm, grad_k_norm, grad_post), "cp")
        return (y_out, grad_x) + tuple(weight_grads)

    return jax.shard_map(local_run, mesh=mesh, in_specs=in_specs, out_specs=out_specs, check_vma=False)
```

profile of v0, /device:TPU:0, one launch (start us, length us, event | category | flops | bytes accessed | tf_op | source)
XLA Modules:
  0.0 1609.0 jit_solution(1544178895626987065)
XLA Ops:
  8.5 6.2 fusion.76
  17.0 4.3 copy.23
  21.3 4.3 copy.21
  25.6 6.7 multiply_reduce_fusion.8
  37.0 13.9 all-reduce.3
  65.8 8.7 fusion.94
  74.5 8.0 fusion.31
  82.5 8.9 add_bitcast_fusion
  91.4 140.3 %while.42 = (s32[]{:T(128)}, bf16[1,1024,4,128]{3,1,2,0:T(8,128)(2,1)}, bf16[1,1024,4,128]{3,1,2,0:T(8,128)(2,1)}, f32[1,4,1024,1]{2,1,3,0:T(4,128)S(1)}, f32[1,...) while((s32[]{:T(128)}, ...), condition=%wide.region_11.12_spmd, body=%wide.region_6.11_spmd.sunk | while | flops 2182098944 | bytes 70517024 | solution.py:131
  93.3 12.6 collective-permute-done.1
  105.9 11.2 collective-permute-done
  121.7 26.7 %collective-permute-start.1 = (bf16[1,1024,4,128]{3,1,2,0:T(8,128)(2,1)}, bf16[1,1024,4,128]{3,1,2,0:T(8,128)(2,1)}, u32[]{:S(2)}, u32[]{:S(2)}) collective-permute-start(bf16[1,1024,4,128]{3,1,2,0:T(8,128)(2,1)} %get-tuple-element.684), channel_id=1, source_target_pairs={{0,1},{1,2},{2,3},{3,0},{4,5},{5,6},{6,7},{7,4},{8,9},{9,10},{10,1... | collective-permute-start | bytes 3145736 | tf_op jit(solution)/shard_map/while/body/eval_jaxpr/ppermute | solution.py:120
  150.8 10.1 collective-permute-done.1
  160.9 11.2 collective-permute-done
  178.3 30.0 %collective-permute-start = (bf16[1,1024,4,128]{3,1,2,0:T(8,128)(2,1)}, bf16[1,1024,4,128]{3,1,2,0:T(8,128)(2,1)}, u32[]{:S(2)}, u32[]{:S(2)}) collective-permute-start(bf16[1,1024,4,128]{3,1,2,0:T(8,128)(2,1)} %get-tuple-element.683), channel_id=1, source_target_pairs={{0,1},{1,2},{2,3},{3,0},{4,5},{5,6},{6,7},{7,4},{8,9},{9,10},{10,1... | collective-permute-start | bytes 3145736 | tf_op jit(solution)/shard_map/while/body/eval_jaxpr/ppermute | solution.py:120
  208.3 7.6 collective-permute-done.1
  215.9 11.2 collective-permute-done
  234.6 7.2 convolution_bitcast_fusion
  241.9 312.3 %all-reduce.8.cloned.1.call-done = f32[1,1024,2048]{2,1,0:T(8,128)} async-done(((f32[1,1024,2048]{2,1,0:T(8,128)}), f32[1,1024,2048]{2,1,0:T(8,128)}) %all-reduce.8.cloned.1.call-update) | async-done | bytes 8388624 | tf_op jit(solution)/shard_map/psum | solution.py:135
  560.0 5.6 fusion.39
  565.6 5.0 fusion.47
  570.6 4.7 fusion.95
  575.9 9.6 fusion.71
  585.4 8.2 multiply_convert_fusion.1
  593.7 4.5 convolution_bitcast_fusion.1
  602.6 302.2 %while.43 = (s32[]{:T(128)}, bf16[1,1024,4,128]{3,1,2,0:T(8,128)(2,1)}, bf16[1,1024,4,128]{3,1,2,0:T(8,128)(2,1)}, f32[1,4,1024,128]{3,2,1,0:T(8,128)}, f32[1,4,...) while((s32[]{:T(128)}, ...), condition=%wide.region_19.0_spmd, body=%wide.region_16.19_spmd.sunk | while | flops 5408030720 | bytes 149996000 | solution.py:165
  605.1 56.9 %collective-permute-done.3 = bf16[1,1024,4,128]{3,1,2,0:T(8,128)(2,1)} collective-permute-done((bf16[1,1024,4,128]{3,1,2,0:T(8,128)(2,1)}, bf16[1,1024,4,128]{3,1,2,0:T(8,128)(2,1)}, u32[]{:S(2)}, u32[]{:S(2)}) %collective-permute-start.3) | collective-permute-done | bytes 1048608 | tf_op jit(solution)/shard_map/while/body/eval_jaxpr/ppermute | solution.py:153
  664.2 9.0 collective-permute-done.2
  680.3 36.2 %collective-permute-start.5 = (f32[1,4,1024,128]{3,2,1,0:T(8,128)}, f32[1,4,1024,128]{3,2,1,0:T(8,128)}, u32[]{:S(2)}, u32[]{:S(2)}) collective-permute-start(f32[1,4,1024,128]{3,2,1,0:T(8,128)} %get-tuple-element.716), channel_id=1, source_target_pairs={{0,1},{1,2},{2,3},{3,0},{4,5},{5,6},{6,7},{7,4},{8,9},{9,10},{10,1... | collective-permute-start | bytes 6291464 | tf_op jit(solution)/shard_map/while/body/eval_jaxpr/ppermute | solution.py:153
  719.0 55.0 %collective-permute-done.3 = bf16[1,1024,4,128]{3,1,2,0:T(8,128)(2,1)} collective-permute-done((bf16[1,1024,4,128]{3,1,2,0:T(8,128)(2,1)}, bf16[1,1024,4,128]{3,1,2,0:T(8,128)(2,1)}, u32[]{:S(2)}, u32[]{:S(2)}) %collective-permute-start.3) | collective-permute-done | bytes 1048608 | tf_op jit(solution)/shard_map/while/body/eval_jaxpr/ppermute | solution.py:153
  776.3 9.0 collective-permute-done.2
  794.0 39.6 %collective-permute-start.4 = (f32[1,4,1024,128]{3,2,1,0:T(8,128)}, f32[1,4,1024,128]{3,2,1,0:T(8,128)}, u32[]{:S(2)}, u32[]{:S(2)}) collective-permute-start(f32[1,4,1024,128]{3,2,1,0:T(8,128)} %get-tuple-element.715), channel_id=1, source_target_pairs={{0,1},{1,2},{2,3},{3,0},{4,5},{5,6},{6,7},{7,4},{8,9},{9,10},{10,1... | collective-permute-start | bytes 6291464 | tf_op jit(solution)/shard_map/while/body/eval_jaxpr/ppermute | solution.py:153
  833.6 52.5 %collective-permute-done.3 = bf16[1,1024,4,128]{3,1,2,0:T(8,128)(2,1)} collective-permute-done((bf16[1,1024,4,128]{3,1,2,0:T(8,128)(2,1)}, bf16[1,1024,4,128]{3,1,2,0:T(8,128)(2,1)}, u32[]{:S(2)}, u32[]{:S(2)}) %collective-permute-start.3) | collective-permute-done | bytes 1048608 | tf_op jit(solution)/shard_map/while/body/eval_jaxpr/ppermute | solution.py:153
  888.4 9.0 collective-permute-done.2
  918.9 7.3 fusion.83
  926.2 52.7 %collective-permute-done.7 = bf16[1,4,1024,128]{3,2,1,0:T(8,128)(2,1)S(1)} collective-permute-done((bf16[1,4,1024,128]{3,2,1,0:T(8,128)(2,1)}, bf16[1,4,1024,128]{3,2,1,0:T(8,128)(2,1)S(1)}, u32[]{:S(2)}, u32[]{:S(2)}) %collective-permute-start.7) | collective-permute-done | bytes 1048608 | tf_op jit(solution)/shard_map/ppermute | solution.py:166
  979.0 4.5 fusion.66
  989.3 10.2 all-reduce.2
  1004.8 4.4 fusion.60
  1009.2 4.4 fusion.63
  1020.4 5.8 fusion.44
  1026.8 11.8 all-reduce
  1038.7 260.6 %all-reduce.12.cloned.1.call-done = (f32[2048,4,128]{0,2,1:T(8,128)}, f32[2048,4,128]{0,2,1:T(8,128)}, f32[2048,4,128]{0,2,1:T(8,128)}, f32[4,128,2048]{2,1,0:T(8,128)}) async-done(((f32[2048,4,128]{0,2,1:T(8,128)}, f32[2048,4,128]{0,2,1:T(8,128)}, f32[2048,4,128]{0,2,1:T(8,128)}, f32[4,128,2048]{2,1,0:T(8,128)}), (f32[2048,4,128]{0,2,1:T(8,128)}, f32[2048,4,128]{0,2,1:T(8,128)}, f32[2048,4,128]{0,2,1:T(8,128)}, ...) | async-done | bytes 16777232 | tf_op jit(solution)/shard_map/psum | solution.py:182
  1299.2 5.2 copy.48
  1304.4 5.2 copy.49
  1309.7 5.2 copy.50
  1314.9 275.6 %all-reduce.10.cloned.1.call-done = f32[1,1024,2048]{2,1,0:T(8,128)} async-done(((f32[1,1024,2048]{2,1,0:T(8,128)}), f32[1,1024,2048]{2,1,0:T(8,128)}) %all-reduce.10.cloned.1.call-update) | async-done | bytes 8388624 | tf_op jit(solution)/shard_map/psum | solution.py:181
  1590.5 8.4 fusion.38
  (201 shorter events, 126.5 us)
Async XLA Ops:
  7.2 227.4 %copy-start = (bf16[4,128,2048]{2,1,0:T(8,128)(2,1)S(1)}, bf16[4,128,2048]{2,1,0:T(8,128)(2,1)}, u32[]{:S(2)}) copy-start(bf16[4,128,2048]{2,1,0:T(8,128)(2,1)} %param.21) | copy-start | bytes 6291460
  7.2 547.0 %all-reduce.8.cloned.1.call-start = ((), (), s32[]{:S(2)}) async-start(), calls=%async_computation | async-start | bytes 16777216 | tf_op jit(solution)/shard_map/psum | solution.py:135
  25.6 6.7 copy-start.10
  25.6 6.7 copy-start.28
  32.3 18.7 %copy-start.53 = (f32[4,128]{1,0:T(4,128)S(1)}, f32[4,128]{1,0:T(4,128)}, u32[]{:S(2)}) copy-start(f32[4,128]{1,0:T(4,128)} %param.23) | copy-start | bytes 6148
  37.0 16.4 %copy-start.23 = (f32[1024,64]{0,1:T(8,128)}, f32[1024,64]{0,1:T(8,128)S(1)}, u32[]{:S(2)}) copy-start(f32[1024,64]{0,1:T(8,128)S(1)} %get-tuple-element.523) | copy-start | bytes 786436
  37.0 16.4 %copy-start.25 = (f32[1024,64]{0,1:T(8,128)}, f32[1024,64]{0,1:T(8,128)S(1)}, u32[]{:S(2)}) copy-start(f32[1024,64]{0,1:T(8,128)S(1)} %get-tuple-element.524) | copy-start | bytes 786436
  91.6 14.3 collective-permute-start.1
  91.7 25.4 %collective-permute-start = (bf16[1,1024,4,128]{3,1,2,0:T(8,128)(2,1)}, bf16[1,1024,4,128]{3,1,2,0:T(8,128)(2,1)}, u32[]{:S(2)}, u32[]{:S(2)}) collective-permute-start(bf16[1,1024,4,128]{3,1,2,0:T(8,128)(2,1)} %get-tuple-element.683), channel_id=1, source_target_pairs={{0,1},{1,2},{2,3},{3,0},{4,5},{5,6},{6,7},{7,4},{8,9},{9,10},{10,1... | collective-permute-start | bytes 3145736 | tf_op jit(solution)/shard_map/while/body/eval_jaxpr/ppermute | solution.py:120
  121.7 39.3 %collective-permute-start.1 = (bf16[1,1024,4,128]{3,1,2,0:T(8,128)(2,1)}, bf16[1,1024,4,128]{3,1,2,0:T(8,128)(2,1)}, u32[]{:S(2)}, u32[]{:S(2)}) collective-permute-start(bf16[1,1024,4,128]{3,1,2,0:T(8,128)(2,1)} %get-tuple-element.684), channel_id=1, source_target_pairs={{0,1},{1,2},{2,3},{3,0},{4,5},{5,6},{6,7},{7,4},{8,9},{9,10},{10,1... | collective-permute-start | bytes 3145736 | tf_op jit(solution)/shard_map/while/body/eval_jaxpr/ppermute | solution.py:120
  148.3 23.8 %collective-permute-start = (bf16[1,1024,4,128]{3,1,2,0:T(8,128)(2,1)}, bf16[1,1024,4,128]{3,1,2,0:T(8,128)(2,1)}, u32[]{:S(2)}, u32[]{:S(2)}) collective-permute-start(bf16[1,1024,4,128]{3,1,2,0:T(8,128)(2,1)} %get-tuple-element.683), channel_id=1, source_target_pairs={{0,1},{1,2},{2,3},{3,0},{4,5},{5,6},{6,7},{7,4},{8,9},{9,10},{10,1... | collective-permute-start | bytes 3145736 | tf_op jit(solution)/shard_map/while/body/eval_jaxpr/ppermute | solution.py:120
  176.7 39.3 %collective-permute-start.1 = (bf16[1,1024,4,128]{3,1,2,0:T(8,128)(2,1)}, bf16[1,1024,4,128]{3,1,2,0:T(8,128)(2,1)}, u32[]{:S(2)}, u32[]{:S(2)}) collective-permute-start(bf16[1,1024,4,128]{3,1,2,0:T(8,128)(2,1)} %get-tuple-element.684), channel_id=1, source_target_pairs={{0,1},{1,2},{2,3},{3,0},{4,5},{5,6},{6,7},{7,4},{8,9},{9,10},{10,1... | collective-permute-start | bytes 3145736 | tf_op jit(solution)/shard_map/while/body/eval_jaxpr/ppermute | solution.py:120
  178.3 48.9 %collective-permute-start = (bf16[1,1024,4,128]{3,1,2,0:T(8,128)(2,1)}, bf16[1,1024,4,128]{3,1,2,0:T(8,128)(2,1)}, u32[]{:S(2)}, u32[]{:S(2)}) collective-permute-start(bf16[1,1024,4,128]{3,1,2,0:T(8,128)(2,1)} %get-tuple-element.683), channel_id=1, source_target_pairs={{0,1},{1,2},{2,3},{3,0},{4,5},{5,6},{6,7},{7,4},{8,9},{9,10},{10,1... | collective-permute-start | bytes 3145736 | tf_op jit(solution)/shard_map/while/body/eval_jaxpr/ppermute | solution.py:120
  231.7 343.6 %copy-start.41 = (f32[1,4,1024,1]{2,1,3,0:T(4,128)}, f32[1,4,1024,1]{2,1,3,0:T(4,128)S(1)}, u32[]{:S(2)}) copy-start(f32[1,4,1024,1]{2,1,3,0:T(4,128)S(1)} %get-tuple-element.412) | copy-start | bytes 49156
  241.8 1057.4 %all-reduce.12.cloned.1.call-start = ((), (), s32[]{:S(2)}) async-start(), calls=%async_computation.2 | async-start | bytes 33554432 | tf_op jit(solution)/shard_map/psum | solution.py:182
  241.9 316.5 %copy-start.51 = (f32[2048]{0:T(1024)S(1)}, f32[2048]{0:T(1024)}, u32[]{:S(2)}) copy-start(f32[2048]{0:T(1024)} %param.24) | copy-start | bytes 24580
  554.2 5.8 copy-start.5
  560.0 5.6 copy-start.6
  560.0 5.6 copy-start.11
  570.6 4.7 copy-start.19
  585.4 8.2 copy-start.38
  585.4 8.2 copy-start.40
  593.7 4.5 copy-start.33
  593.7 4.5 copy-start.36
  602.7 71.4 %collective-permute-start.5 = (f32[1,4,1024,128]{3,2,1,0:T(8,128)}, f32[1,4,1024,128]{3,2,1,0:T(8,128)}, u32[]{:S(2)}, u32[]{:S(2)}) collective-permute-start(f32[1,4,1024,128]{3,2,1,0:T(8,128)} %get-tuple-element.716), channel_id=1, source_target_pairs={{0,1},{1,2},{2,3},{3,0},{4,5},{5,6},{6,7},{7,4},{8,9},{9,10},{10,1... | collective-permute-start | bytes 6291464 | tf_op jit(solution)/shard_map/while/body/eval_jaxpr/ppermute | solution.py:153
  602.8 71.4 %collective-permute-start.4 = (f32[1,4,1024,128]{3,2,1,0:T(8,128)}, f32[1,4,1024,128]{3,2,1,0:T(8,128)}, u32[]{:S(2)}, u32[]{:S(2)}) collective-permute-start(f32[1,4,1024,128]{3,2,1,0:T(8,128)} %get-tuple-element.715), channel_id=1, source_target_pairs={{0,1},{1,2},{2,3},{3,0},{4,5},{5,6},{6,7},{7,4},{8,9},{9,10},{10,1... | collective-permute-start | bytes 6291464 | tf_op jit(solution)/shard_map/while/body/eval_jaxpr/ppermute | solution.py:153
  604.4 57.6 %collective-permute-start.3 = (bf16[1,1024,4,128]{3,1,2,0:T(8,128)(2,1)}, bf16[1,1024,4,128]{3,1,2,0:T(8,128)(2,1)}, u32[]{:S(2)}, u32[]{:S(2)}) collective-permute-start(bf16[1,1024,4,128]{3,1,2,0:T(8,128)(2,1)} %get-tuple-element.714), channel_id=1, source_target_pairs={{0,1},{1,2},{2,3},{3,0},{4,5},{5,6},{6,7},{7,4},{8,9},{9,10},{10,1... | collective-permute-start | bytes 3145736 | tf_op jit(solution)/shard_map/while/body/eval_jaxpr/ppermute | solution.py:153
  604.4 68.8 %collective-permute-start.2 = (bf16[1,1024,4,128]{3,1,2,0:T(8,128)(2,1)}, bf16[1,1024,4,128]{3,1,2,0:T(8,128)(2,1)S(1)}, u32[]{:S(2)}, u32[]{:S(2)}) collective-permute-start(bf16[1,1024,4,128]{3,1,2,0:T(8,128)(2,1)} %get-tuple-element.713), channel_id=1, source_target_pairs={{0,1},{1,2},{2,3},{3,0},{4,5},{5,6},{6,7},{7,4},{8,9},{9,10},{10,1... | collective-permute-start | bytes 3145736 | tf_op jit(solution)/shard_map/while/body/eval_jaxpr/ppermute | solution.py:153
  680.3 106.0 %collective-permute-start.5 = (f32[1,4,1024,128]{3,2,1,0:T(8,128)}, f32[1,4,1024,128]{3,2,1,0:T(8,128)}, u32[]{:S(2)}, u32[]{:S(2)}) collective-permute-start(f32[1,4,1024,128]{3,2,1,0:T(8,128)} %get-tuple-element.716), channel_id=1, source_target_pairs={{0,1},{1,2},{2,3},{3,0},{4,5},{5,6},{6,7},{7,4},{8,9},{9,10},{10,1... | collective-permute-start | bytes 6291464 | tf_op jit(solution)/shard_map/while/body/eval_jaxpr/ppermute | solution.py:153
  716.5 69.8 %collective-permute-start.4 = (f32[1,4,1024,128]{3,2,1,0:T(8,128)}, f32[1,4,1024,128]{3,2,1,0:T(8,128)}, u32[]{:S(2)}, u32[]{:S(2)}) collective-permute-start(f32[1,4,1024,128]{3,2,1,0:T(8,128)} %get-tuple-element.715), channel_id=1, source_target_pairs={{0,1},{1,2},{2,3},{3,0},{4,5},{5,6},{6,7},{7,4},{8,9},{9,10},{10,1... | collective-permute-start | bytes 6291464 | tf_op jit(solution)/shard_map/while/body/eval_jaxpr/ppermute | solution.py:153
  719.0 55.1 %collective-permute-start.3 = (bf16[1,1024,4,128]{3,1,2,0:T(8,128)(2,1)}, bf16[1,1024,4,128]{3,1,2,0:T(8,128)(2,1)}, u32[]{:S(2)}, u32[]{:S(2)}) collective-permute-start(bf16[1,1024,4,128]{3,1,2,0:T(8,128)(2,1)} %get-tuple-element.714), channel_id=1, source_target_pairs={{0,1},{1,2},{2,3},{3,0},{4,5},{5,6},{6,7},{7,4},{8,9},{9,10},{10,1... | collective-permute-start | bytes 3145736 | tf_op jit(solution)/shard_map/while/body/eval_jaxpr/ppermute | solution.py:153
  719.0 66.3 %collective-permute-start.2 = (bf16[1,1024,4,128]{3,1,2,0:T(8,128)(2,1)}, bf16[1,1024,4,128]{3,1,2,0:T(8,128)(2,1)S(1)}, u32[]{:S(2)}, u32[]{:S(2)}) collective-permute-start(bf16[1,1024,4,128]{3,1,2,0:T(8,128)(2,1)} %get-tuple-element.713), channel_id=1, source_target_pairs={{0,1},{1,2},{2,3},{3,0},{4,5},{5,6},{6,7},{7,4},{8,9},{9,10},{10,1... | collective-permute-start | bytes 3145736 | tf_op jit(solution)/shard_map/while/body/eval_jaxpr/ppermute | solution.py:153
  792.4 106.0 %collective-permute-start.5 = (f32[1,4,1024,128]{3,2,1,0:T(8,128)}, f32[1,4,1024,128]{3,2,1,0:T(8,128)}, u32[]{:S(2)}, u32[]{:S(2)}) collective-permute-start(f32[1,4,1024,128]{3,2,1,0:T(8,128)} %get-tuple-element.716), channel_id=1, source_target_pairs={{0,1},{1,2},{2,3},{3,0},{4,5},{5,6},{6,7},{7,4},{8,9},{9,10},{10,1... | collective-permute-start | bytes 6291464 | tf_op jit(solution)/shard_map/while/body/eval_jaxpr/ppermute | solution.py:153
  794.0 104.4 %collective-permute-start.4 = (f32[1,4,1024,128]{3,2,1,0:T(8,128)}, f32[1,4,1024,128]{3,2,1,0:T(8,128)}, u32[]{:S(2)}, u32[]{:S(2)}) collective-permute-start(f32[1,4,1024,128]{3,2,1,0:T(8,128)} %get-tuple-element.715), channel_id=1, source_target_pairs={{0,1},{1,2},{2,3},{3,0},{4,5},{5,6},{6,7},{7,4},{8,9},{9,10},{10,1... | collective-permute-start | bytes 6291464 | tf_op jit(solution)/shard_map/while/body/eval_jaxpr/ppermute | solution.py:153
  833.6 52.6 %collective-permute-start.3 = (bf16[1,1024,4,128]{3,1,2,0:T(8,128)(2,1)}, bf16[1,1024,4,128]{3,1,2,0:T(8,128)(2,1)}, u32[]{:S(2)}, u32[]{:S(2)}) collective-permute-start(bf16[1,1024,4,128]{3,1,2,0:T(8,128)(2,1)} %get-tuple-element.714), channel_id=1, source_target_pairs={{0,1},{1,2},{2,3},{3,0},{4,5},{5,6},{6,7},{7,4},{8,9},{9,10},{10,1... | collective-permute-start | bytes 3145736 | tf_op jit(solution)/shard_map/while/body/eval_jaxpr/ppermute | solution.py:153
  833.6 63.8 %collective-permute-start.2 = (bf16[1,1024,4,128]{3,1,2,0:T(8,128)(2,1)}, bf16[1,1024,4,128]{3,1,2,0:T(8,128)(2,1)S(1)}, u32[]{:S(2)}, u32[]{:S(2)}) collective-permute-start(bf16[1,1024,4,128]{3,1,2,0:T(8,128)(2,1)} %get-tuple-element.713), channel_id=1, source_target_pairs={{0,1},{1,2},{2,3},{3,0},{4,5},{5,6},{6,7},{7,4},{8,9},{9,10},{10,1... | collective-permute-start | bytes 3145736 | tf_op jit(solution)/shard_map/while/body/eval_jaxpr/ppermute | solution.py:153
  907.7 9.3 copy-start.4
  907.7 75.7 %collective-permute-start.6 = (f32[1,4,1024,128]{2,3,1,0:T(8,128)}, f32[1,4,1024,128]{2,3,1,0:T(8,128)}, u32[]{:S(2)}, u32[]{:S(2)}) collective-permute-start(f32[1,4,1024,128]{2,3,1,0:T(8,128)} %copy.43), channel_id=1, source_target_pairs={{0,1},{1,2},{2,3},{3,0},{4,5},{5,6},{6,7},{7,4},{8,9},{9,10},{10,1... | collective-permute-start | bytes 6291464 | tf_op jit(solution)/shard_map/ppermute | solution.py:166
  914.5 64.5 %collective-permute-start.7 = (bf16[1,4,1024,128]{3,2,1,0:T(8,128)(2,1)}, bf16[1,4,1024,128]{3,2,1,0:T(8,128)(2,1)S(1)}, u32[]{:S(2)}, u32[]{:S(2)}) collective-permute-start(bf16[1,4,1024,128]{3,2,1,0:T(8,128)(2,1)} %convert.38), channel_id=1, source_target_pairs={{0,1},{1,2},{2,3},{3,0},{4,5},{5,6},{6,7},{7,4},{8,9},{9,10},{10,1... | collective-permute-start | bytes 3145736 | tf_op jit(solution)/shard_map/ppermute | solution.py:166
  918.9 60.1 %copy-start.12 = (bf16[1,1024,2048]{2,1,0:T(8,128)(2,1)S(1)}, bf16[1,1024,2048]{2,1,0:T(8,128)(2,1)}, u32[]{:S(2)}) copy-start(bf16[1,1024,2048]{2,1,0:T(8,128)(2,1)} %param.17) | copy-start | bytes 12582916
  926.2 57.2 %copy-start.18 = (f32[1,4,1024,1,128]{2,4,1,3,0:T(8,128)S(1)}, f32[1,4,1024,1,128]{2,4,1,3,0:T(8,128)}, u32[]{:S(2)}) copy-start(f32[1,4,1024,1,128]{2,4,1,3,0:T(8,128)} %copy.40) | copy-start | bytes 6291460
  926.2 57.2 %copy-start.24 = (f32[1024,64]{0,1:T(8,128)S(1)}, f32[1024,64]{0,1:T(8,128)}, u32[]{:S(2)}) copy-start(f32[1024,64]{0,1:T(8,128)} %copy-done.23) | copy-start | bytes 786436
  926.2 57.2 %copy-start.26 = (f32[1024,64]{0,1:T(8,128)S(1)}, f32[1024,64]{0,1:T(8,128)}, u32[]{:S(2)}) copy-start(f32[1024,64]{0,1:T(8,128)} %copy-done.25) | copy-start | bytes 786436
  979.0 4.5 copy-start.20
  1002.2 7.0 copy-start.43
  1004.8 4.4 copy-start.45
  1013.6 576.9 %all-reduce.10.cloned.1.call-start = ((), (), s32[]{:S(2)}) async-start(), calls=%async_computation.1 | async-start | bytes 16777216 | tf_op jit(solution)/shard_map/psum | solution.py:181
  1590.5 8.5 copy-start.22
  (30 other events, 63.8 us)
Sparse Core Ops, SparseCore 0:
  242.0 312.2 all-reduce.7
  1013.7 285.4 all-reduce.11
  1301.7 288.7 all-reduce.9
where the time goes:
time: 1620 us; the launch traced here: 1610 us
  waiting for transfers between devices  1160 us (72%)
  starting transfers between devices  152 us (9%)
  matrix products  103 us (6%)
  local copies, waits for them, and re-layouts  95.4 us (6%)
  other arithmetic  50.8 us (3%)
  blocking collectives  35.9 us (2%)
    psum x1, waiting for transfers between devices, local_run(): lax.psum(jnp.einsum('blhe,hed->bld', attn_out, w_o, preferred_element_typ...  312 us
    psum x1, waiting for transfers between devices, local_run(): grad_x = (grad_f + lax.psum(grad_x_part, 'tp')).astype(jnp.bfloat16)  276 us
    psum x1, waiting for transfers between devices, local_run(): lax.psum((grad_w_q, grad_w_k, grad_w_v, grad_w_o, grad_q_norm, grad_k_nor...  261 us
    ppermute x12, waiting for transfers between devices, bwd_step(): lax.ppermute((k_cur, v_cur, dk_cur, dv_cur), 'cp', perm_next)  191 us
    ppermute x12, starting transfers between devices, bwd_step(): lax.ppermute((k_cur, v_cur, dk_cur, dv_cur), 'cp', perm_next)  82.2 us
    ppermute x6, waiting for transfers between devices, fwd_step(): k_cur, v_cur = lax.ppermute((k_cur, v_cur), 'cp', perm_next)  64 us
    ppermute x6, starting transfers between devices, fwd_step(): k_cur, v_cur = lax.ppermute((k_cur, v_cur), 'cp', perm_next)  62.5 us
    ppermute x2, waiting for transfers between devices, local_run(): lax.ppermute((back_state[2], back_state[3]), 'cp', perm_next)  52.7 us
  transfers between devices with their start and end apart: 23, of which 16 were waited for; matrix products, arithmetic and copies ran while one was open for 3% of the time, Pallas kernels for 0%

commit v1 on v0

v1 whole, which is shorter than its diff:
```python
import functools

import jax
import jax.numpy as jnp
from jax import lax
from jax.experimental import pallas as pl
from jax.experimental.pallas import tpu as pltpu
from jax.sharding import PartitionSpec as P

ROPE_THETA = 500000.0
NORM_EPS = 1e-6
MASK_VALUE = -1e30
LOG2E = 1.4426950408889634
MESH = pl.DeviceIdType.MESH
VMEM_SPEC = pl.BlockSpec(memory_space=pltpu.VMEM)
VMEM_LIMIT = 60 * 1024 * 1024
NT = (((1,), (1,)), ((), ()))
TN = (((0,), (0,)), ((), ()))


def dot_nt(a, b):
    return lax.dot_general(a, b, NT, preferred_element_type=jnp.float32)


def dot_tn(a, b):
    return lax.dot_general(a, b, TN, preferred_element_type=jnp.float32)


def dot_nn(a, b):
    return jnp.dot(a, b, preferred_element_type=jnp.float32)


def rope_tables(start_pos, seq_rows, head_dim):
    half_dim = head_dim // 2
    inv_freq = ROPE_THETA ** (-2.0 * jnp.arange(half_dim, dtype=jnp.float32) / head_dim)
    positions = (start_pos + jnp.arange(seq_rows)).astype(jnp.float32)
    angles = positions[:, None] * inv_freq[None, :]
    return jnp.cos(angles), jnp.sin(angles)


def rope(values, cos_tab, sin_tab, sign):
    half_dim = values.shape[-1] // 2
    low_half = values[..., :half_dim]
    high_half = values[..., half_dim:]
    sin_tab = sign * sin_tab
    return jnp.concatenate([low_half * cos_tab - high_half * sin_tab, high_half * cos_tab + low_half * sin_tab], axis=-1)


def entry_barrier(axis, size):
    me = lax.axis_index(axis)
    barrier = pltpu.get_barrier_semaphore()
    for shift in range(1, size):
        pl.semaphore_signal(barrier, inc=1, device_id={axis: lax.rem(me + shift, size)}, device_id_type=MESH)
    pl.semaphore_wait(barrier, size - 1)


def exchange_kernel(axis, size, count, *refs):
    ins = refs[:count]
    outs = refs[count:2 * count]
    send_sem, recv_sem = refs[2 * count:]
    me = lax.axis_index(axis)
    entry_barrier(axis, size)
    copies = []
    for idx in range(count):
        for shift in (2, 1, 3) if size == 4 else range(1, size):
            dst = lax.rem(me + shift, size)
            copy = pltpu.make_async_remote_copy(
                src_ref=ins[idx].at[dst], dst_ref=outs[idx].at[me],
                send_sem=send_sem.at[idx, shift - 1], recv_sem=recv_sem.at[idx, shift - 1],
                device_id={axis: dst}, device_id_type=MESH)
            copy.start()
            copies.append(copy)
    for idx in range(count):
        outs[idx][me] = ins[idx][me]
    for copy in copies:
        copy.wait()


def exchange(axis, size, collective_id, *arrays):
    count = len(arrays)
    return pl.pallas_call(
        functools.partial(exchange_kernel, axis, size, count),
        out_shape=tuple(jax.ShapeDtypeStruct(a.shape, a.dtype) for a in arrays),
        in_specs=[VMEM_SPEC] * count,
        out_specs=tuple([VMEM_SPEC] * count),
        scratch_shapes=[pltpu.SemaphoreType.DMA((count, size - 1)), pltpu.SemaphoreType.DMA((count, size - 1))],
        compiler_params=pltpu.CompilerParams(collective_id=collective_id, has_side_effects=True, vmem_limit_bytes=VMEM_LIMIT),
        name="exchange_" + str(collective_id),
    )(*arrays)


def sum_kernel(axis, size, in_ref, out_ref, slots, send_sem, recv_sem):
    me = lax.axis_index(axis)
    entry_barrier(axis, size)
    copies = []
    for shift in range(1, size):
        copy = pltpu.make_async_remote_copy(
            src_ref=in_ref, dst_ref=slots.at[me],
            send_sem=send_sem.at[shift - 1], recv_sem=recv_sem.at[shift - 1],
            device_id={axis: lax.rem(me + shift, size)}, device_id_type=MESH)
        copy.start()
        copies.append(copy)
    slots[me] = in_ref[...]
    for copy in copies:
        copy.wait()
    total = slots[0]
    for idx in range(1, size):
        total = total + slots[idx]
    out_ref[...] = total


def small_sum(axis, size, collective_id, array):
    return pl.pallas_call(
        functools.partial(sum_kernel, axis, size),
        out_shape=jax.ShapeDtypeStruct(array.shape, array.dtype),
        in_specs=[VMEM_SPEC],
        out_specs=VMEM_SPEC,
        scratch_shapes=[pltpu.VMEM((size,) + array.shape, array.dtype), pltpu.SemaphoreType.DMA((size - 1,)), pltpu.SemaphoreType.DMA((size - 1,))],
        compiler_params=pltpu.CompilerParams(collective_id=collective_id, has_side_effects=True),
        name="small_sum_" + str(collective_id),
    )(array)


def causal_mask(scores):
    key_pos = lax.broadcasted_iota(jnp.int32, scores.shape, 0)
    query_pos = lax.broadcasted_iota(jnp.int32, scores.shape, 1)
    return jnp.where(key_pos <= query_pos, scores, MASK_VALUE)


def attend_kernel(block, factor, q_ref, k_ref, v_ref, o_ref, lse_ref):
    blk = pl.program_id(0)
    q_blk = q_ref[...]

    def scores_of(idx):
        rows = pl.ds(pl.multiple_of(idx * block, block), block)
        return dot_nt(k_ref[rows, :], q_blk), v_ref[rows, :]

    scores, v_blk = scores_of(blk)
    scores = causal_mask(scores)
    top = jnp.max(scores, axis=0, keepdims=True)
    probs = jnp.exp2((scores - top) * factor)
    norm = jnp.sum(probs, axis=0, keepdims=True)
    acc = dot_tn(v_blk, probs.astype(jnp.bfloat16))

    def step(idx, state):
        top, norm, acc = state
        scores, v_blk = scores_of(idx)
        new_top = jnp.maximum(top, jnp.max(scores, axis=0, keepdims=True))
        probs = jnp.exp2((scores - new_top) * factor)
        rescale = jnp.exp2((top - new_top) * factor)
        norm = norm * rescale + jnp.sum(probs, axis=0, keepdims=True)
        acc = acc * rescale + dot_tn(v_blk, probs.astype(jnp.bfloat16))
        return new_top, norm, acc

    top, norm, acc = lax.fori_loop(0, blk, step, (top, norm, acc))
    o_ref[...] = (acc / norm).T.astype(jnp.bfloat16)
    lse_ref[...] = top * factor + jnp.log2(norm)


def attend(q, k, v):
    rows, head_dim = q.shape
    block = min(512, rows // 4)
    whole = pl.BlockSpec((rows, head_dim), lambda i: (0, 0))
    part = pl.BlockSpec((block, head_dim), lambda i: (i, 0))
    return pl.pallas_call(
        functools.partial(attend_kernel, block, head_dim ** -0.5 * LOG2E),
        grid=(rows // block,),
        out_shape=(jax.ShapeDtypeStruct(q.shape, jnp.bfloat16), jax.ShapeDtypeStruct((1, rows), jnp.float32)),
        in_specs=[part, whole, whole],
        out_specs=(part, pl.BlockSpec((1, block), lambda i: (0, i))),
        compiler_params=pltpu.CompilerParams(vmem_limit_bytes=VMEM_LIMIT),
        cost_estimate=pl.CostEstimate(flops=2 * rows * rows * head_dim, bytes_accessed=8 * rows * head_dim, transcendentals=rows * rows // 2),
        name="attend",
    )(q, k, v)


def attend_back_kernel(block, scale, q_ref, k_ref, v_ref, o_ref, do_ref, lse_ref, dq_ref, dk_ref, dv_ref, delta_ref, dk_acc, dv_acc):
    blk = pl.program_id(0)
    n_blk = pl.num_programs(0)
    factor = scale * LOG2E

    @pl.when(blk == 0)
    def _():
        def prepare(idx, carry):
            rows = pl.ds(pl.multiple_of(idx * block, block), block)
            prod = do_ref[rows, :].astype(jnp.float32) * o_ref[rows, :].astype(jnp.float32)
            delta_ref[:, rows] = jnp.sum(prod.T, axis=0, keepdims=True)
            dq_ref[rows, :] = jnp.zeros((block, dq_ref.shape[1]), jnp.float32)
            return carry
        lax.fori_loop(0, n_blk, prepare, 0)

    k_blk = k_ref[...]
    v_blk = v_ref[...]

    def one(idx, masked):
        rows = pl.ds(pl.multiple_of(idx * block, block), block)
        q_blk = q_ref[rows, :]
        do_blk = do_ref[rows, :]
        scores = dot_nt(k_blk, q_blk)
        if masked:
            scores = causal_mask(scores)
        probs = jnp.exp2(scores * factor - lse_ref[:, rows])
        grad_v = dot_nn(probs.astype(jnp.bfloat16), do_blk)
        grad_p = dot_nt(v_blk, do_blk)
        grad_s = (probs * ((grad_p - delta_ref[:, rows]) * scale)).astype(jnp.bfloat16)
        dq_ref[rows, :] += dot_tn(grad_s, k_blk)
        return dot_nn(grad_s, q_blk), grad_v

    dk_acc[...], dv_acc[...] = one(blk, True)

    def step(idx, carry):
        grad_k, grad_v = one(idx, False)
        dk_acc[...] += grad_k
        dv_acc[...] += grad_v
        return carry

    lax.fori_loop(blk + 1, n_blk, step, 0)
    dk_ref[...] = dk_acc[...]
    dv_ref[...] = dv_acc[...].astype(jnp.bfloat16)


def attend_back(q, k, v, o, do, lse):
    rows, head_dim = q.shape
    block = min(512, rows // 4)
    whole = pl.BlockSpec((rows, head_dim), lambda i: (0, 0))
    part = pl.BlockSpec((block, head_dim), lambda i: (i, 0))
    stat = pl.BlockSpec((1, rows), lambda i: (0, 0))
    return pl.pallas_call(
        functools.partial(attend_back_kernel, block, head_dim ** -0.5),
        grid=(rows // block,),
        out_shape=(jax.ShapeDtypeStruct(q.shape, jnp.float32), jax.ShapeDtypeStruct(q.shape, jnp.float32), jax.ShapeDtypeStruct(q.shape, jnp.bfloat16)),
        in_specs=[whole, part, part, whole, whole, stat],
        out_specs=(whole, part, part),
        scratch_shapes=[pltpu.VMEM((1, rows), jnp.float32), pltpu.VMEM((block, head_dim), jnp.float32), pltpu.VMEM((block, head_dim), jnp.float32)],
        compiler_params=pltpu.CompilerParams(vmem_limit_bytes=VMEM_LIMIT),
        cost_estimate=pl.CostEstimate(flops=5 * rows * rows * head_dim, bytes_accessed=20 * rows * head_dim, transcendentals=rows * rows // 2),
        name="attend_back",
    )(q, k, v, o, do, lse)


def post_kernel(tp_size, o_ref, wo_ref, wown_ref, x_ref, gy_ref, pw_ref, y_ref, gp_ref, do_ref, gpost_ref):
    proj = dot_nn(o_ref[0], wo_ref[0])
    for idx in range(1, tp_size):
        proj = proj + dot_nn(o_ref[idx], wo_ref[idx])
    gain = pw_ref[...]
    inv = lax.rsqrt(jnp.mean(proj * proj, axis=-1, keepdims=True) + NORM_EPS)
    hat = proj * inv
    y_ref[...] = (x_ref[...].astype(jnp.float32) + hat * gain).astype(jnp.bfloat16)
    grad = gy_ref[...].astype(jnp.float32)
    gpost = jnp.sum(grad * hat, axis=0, keepdims=True)
    grad_hat = grad * gain
    grad_proj = (inv * (grad_hat - hat * jnp.mean(grad_hat * hat, axis=-1, keepdims=True))).astype(jnp.bfloat16)
    gp_ref[...] = grad_proj
    grad_o = dot_nt(grad_proj, wown_ref[...]).astype(jnp.bfloat16)
    head_dim = do_ref.shape[2]
    for idx in range(do_ref.shape[0]):
        do_ref[idx] = grad_o[:, idx * head_dim:(idx + 1) * head_dim]

    @pl.when(pl.program_id(0) == 0)
    def _():
        gpost_ref[...] = jnp.zeros_like(gpost_ref)

    gpost_ref[...] += gpost


def post(o_all, wo_all, w_own, x, gy, gain, heads, head_dim):
    tp_size, rows, width = o_all.shape
    d_model = x.shape[1]
    block = min(256, rows)
    act = pl.BlockSpec((block, d_model), lambda i: (i, 0))
    return pl.pallas_call(
        functools.partial(post_kernel, tp_size),
        grid=(rows // block,),
        out_shape=(jax.ShapeDtypeStruct((rows, d_model), jnp.bfloat16), jax.ShapeDtypeStruct((rows, d_model), jnp.bfloat16),
                   jax.ShapeDtypeStruct((heads, rows, head_dim), jnp.bfloat16), jax.ShapeDtypeStruct((1, d_model), jnp.float32)),
        in_specs=[pl.BlockSpec((tp_size, block, width), lambda i: (0, i, 0)), pl.BlockSpec(wo_all.shape, lambda i: (0, 0, 0)),
                  pl.BlockSpec(w_own.shape, lambda i: (0, 0)), act, act, pl.BlockSpec((1, d_model), lambda i: (0, 0))],
        out_specs=(act, act, pl.BlockSpec((heads, block, head_dim), lambda i: (0, i, 0)), pl.BlockSpec((1, d_model), lambda i: (0, 0))),
        compiler_params=pltpu.CompilerParams(vmem_limit_bytes=VMEM_LIMIT),
        cost_estimate=pl.CostEstimate(flops=2 * rows * d_model * (d_model + width), bytes_accessed=4 * d_model * d_model, transcendentals=rows),
        name="post",
    )(o_all, wo_all, w_own, x, gy, gain)


def chain_kernel(size, n_chunk, lag, part_ref, gy_ref, out_ref, sums_a, sums_b, rs_send, rs_recv, ag_send, ag_recv):
    me = lax.axis_index("tp")
    entry_barrier("tp", size)
    half = part_ref.shape[0] // 2
    rows = half // n_chunk
    last = size - 1

    def parts(side, chunk):
        local = pl.ds(pl.multiple_of(chunk * rows, rows), rows)
        glob = pl.ds(pl.multiple_of(side * half + chunk * rows, rows), rows)
        sums = (sums_a, sums_b)[side]
        return local, glob, sums

    def toward(side):
        return jnp.maximum(me - 1, 0) if side == 0 else jnp.minimum(me + 1, last)

    def away(side):
        return jnp.minimum(me + 1, last) if side == 0 else jnp.maximum(me - 1, 0)

    def rs_copy(side, chunk, first):
        local, glob, sums = parts(side, chunk)
        return pltpu.make_async_remote_copy(
            src_ref=part_ref.at[glob] if first else sums.at[local], dst_ref=sums.at[local],
            send_sem=rs_send.at[side, chunk], recv_sem=rs_recv.at[side, chunk],
            device_id={"tp": toward(side)}, device_id_type=MESH)

    def ag_copy(side, chunk):
        local, glob, sums = parts(side, chunk)
        return pltpu.make_async_remote_copy(
            src_ref=out_ref.at[glob], dst_ref=out_ref.at[glob],
            send_sem=ag_send.at[side, chunk], recv_sem=ag_recv.at[side, chunk],
            device_id={"tp": away(side)}, device_id_type=MESH)

    def step(idx, carry):
        for side in (0, 1):
            pos = me if side == 0 else last - me
            local, glob, sums = parts(side, idx)

            @pl.when((idx < n_chunk) & (pos == last))
            def _(side=side):
                rs_copy(side, idx, True).start()

            @pl.when((idx < n_chunk) & (pos > 0) & (pos < last))
            def _(side=side, local=local, glob=glob, sums=sums):
                rs_copy(side, idx, False).wait_recv()
                sums[local] = sums[local] + part_ref[glob]
                rs_copy(side, idx, False).start()

            @pl.when((idx < n_chunk) & (pos == 0))
            def _(side=side, local=local, glob=glob, sums=sums):
                rs_copy(side, idx, False).wait_recv()
                out_ref[glob] = (gy_ref[glob].astype(jnp.float32) + (sums[local] + part_ref[glob])).astype(jnp.bfloat16)
                ag_copy(side, idx).start()

            @pl.when((idx >= lag) & (pos > 0))
            def _(side=side):
                ag_copy(side, idx - lag).wait_recv()

            @pl.when((idx >= lag) & (pos > 0) & (pos < last))
            def _(side=side):
                ag_copy(side, idx - lag).start()
        return carry

    lax.fori_loop(0, n_chunk + lag, step, 0)

    def drain(idx, carry):
        for side in (0, 1):
            pos = me if side == 0 else last - me

            @pl.when(pos > 0)
            def _(side=side):
                rs_copy(side, idx, False).wait_send()

            @pl.when(pos < last)
            def _(side=side):
                ag_copy(side, idx).wait_send()
        return carry

    lax.fori_loop(0, n_chunk, drain, 0)


def chain_sum(size, collective_id, part, gy):
    rows, d_model = part.shape
    n_chunk = 16 if rows >= 512 else 2
    sems = [pltpu.SemaphoreType.DMA((2, n_chunk))] * 4
    return pl.pallas_call(
        functools.partial(chain_kernel, size, n_chunk, min(6, n_chunk)),
        out_shape=jax.ShapeDtypeStruct((rows, d_model), jnp.bfloat16),
        in_specs=[VMEM_SPEC, VMEM_SPEC],
        out_specs=VMEM_SPEC,
        scratch_shapes=[pltpu.VMEM((rows // 2, d_model), jnp.float32), pltpu.VMEM((rows // 2, d_model), jnp.float32)] + sems,
        compiler_params=pltpu.CompilerParams(collective_id=collective_id, has_side_effects=True, vmem_limit_bytes=VMEM_LIMIT),
        cost_estimate=pl.CostEstimate(flops=10 ** 11, bytes_accessed=16 * rows * d_model, transcendentals=0),
        name="chain_sum",
    )(part, gy)


def solution(mesh):
    tp_size = mesh.shape["tp"]
    cp_size = mesh.shape["cp"]
    act_spec = P("dp", "cp", None)
    col_spec = P(None, "tp", None)
    part_col = P("dp", "tp", None)
    in_specs = (act_spec, col_spec, col_spec, col_spec, P("tp", None, None), P("tp", None), P("tp", None), P(None), act_spec)
    out_specs = (act_spec, act_spec, part_col, part_col, part_col, P(("dp", "tp"), None, None), P(("dp", "tp"), None), P(("dp", "tp"), None), P("dp"))
    swap_core = [(dev, dev ^ 1) for dev in range(cp_size)]

    def local_run(x_in, w_q, w_k, w_v, w_o, q_norm_w, k_norm_w, post_norm_w, grad_y):
        rows, d_model = x_in.shape[1:]
        heads, head_dim = w_q.shape[1:]
        width = heads * head_dim
        full_width = width * tp_size
        x = x_in[0]
        gy = grad_y[0]
        cp_index = lax.axis_index("cp")
        cos_tab, sin_tab = rope_tables(cp_index * rows, rows, head_dim)
        wq, wk, wv = (w.reshape(d_model, width) for w in (w_q, w_k, w_v))

        core = cp_index % 2
        own_half = lax.dynamic_slice_in_dim(w_o, core * (heads // 2), heads // 2, axis=0)
        mine = lax.all_gather(own_half, "tp")
        other = lax.ppermute(mine, "cp", swap_core)
        wo_all = jnp.where(core == 0, jnp.concatenate([mine, other], axis=1), jnp.concatenate([other, mine], axis=1))
        wo_all = wo_all.reshape(tp_size, width, d_model)

        def by_head(t):
            return t.reshape(rows, heads, head_dim).transpose(1, 0, 2)

        q_lin = jnp.dot(x, wq, preferred_element_type=jnp.float32)
        k_lin = jnp.dot(x, wk, preferred_element_type=jnp.float32)
        v_lin = jnp.dot(x, wv, preferred_element_type=jnp.float32)
        squares = jnp.stack([jnp.sum(q_lin * q_lin, axis=1), jnp.sum(k_lin * k_lin, axis=1)])
        squares = small_sum("tp", tp_size, 0, squares)
        invs = lax.rsqrt(squares / full_width + NORM_EPS)[:, :, None]
        q_hat = by_head(q_lin * invs[0])
        k_hat = by_head(k_lin * invs[1])
        q_gain = q_norm_w[:, None, :]
        k_gain = k_norm_w[:, None, :]
        q_rot = rope(q_hat * q_gain, cos_tab, sin_tab, 1.0).astype(jnp.bfloat16)
        k_rot = rope(k_hat * k_gain, cos_tab, sin_tab, 1.0).astype(jnp.bfloat16)
        v_val = by_head(v_lin.astype(jnp.bfloat16))

        seq_shape = (cp_size * rows, head_dim)
        block_shape = (cp_size, rows, head_dim)
        q_seq, k_seq, v_seq = (t.reshape(seq_shape) for t in exchange("cp", cp_size, 1, q_rot, k_rot, v_val))
        o_seq, lse = attend(q_seq, k_seq, v_seq)
        (o_heads,) = exchange("cp", cp_size, 2, o_seq.reshape(block_shape))
        o_mine = o_heads.transpose(1, 0, 2).reshape(rows, width)
        o_all = lax.all_gather(o_mine, "tp")
        y_out, grad_proj, grad_o, grad_post = post(o_all, wo_all, w_o.reshape(width, d_model), x, gy, post_norm_w[None, :], heads, head_dim)
        (do_seq,) = exchange("cp", cp_size, 3, grad_o)
        dwo_part = lax.dot_general(o_mine, grad_proj, TN, preferred_element_type=jnp.float32)
        grad_w_o = lax.psum(dwo_part, "cp")

        dq_seq, dk_seq, dv_seq = attend_back(q_seq, k_seq, v_seq, o_seq, do_seq.reshape(seq_shape), lse)
        dq, dk, dv = exchange("cp", cp_size, 4, dq_seq.reshape(block_shape), dk_seq.reshape(block_shape), dv_seq.reshape(block_shape))

        def scaled_back(grad_rot, hat, gain):
            grad = rope(grad_rot, cos_tab, sin_tab, -1.0)
            grad_gain = jnp.sum(grad * hat, axis=1)
            grad_hat = grad * gain
            return grad_hat, grad_gain, jnp.sum(grad_hat * hat, axis=(0, 2))

        gq_hat, grad_q_norm, q_dot = scaled_back(dq, q_hat, q_gain)
        gk_hat, grad_k_norm, k_dot = scaled_back(dk, k_hat, k_gain)
        dots = small_sum("tp", tp_size, 5, jnp.stack([q_dot, k_dot])) / full_width

        def flat(t):
            return t.transpose(1, 0, 2).reshape(rows, width)

        dq16 = flat((invs[0][None] * (gq_hat - q_hat * dots[0][None, :, None])).astype(jnp.bfloat16))
        dk16 = flat((invs[1][None] * (gk_hat - k_hat * dots[1][None, :, None])).astype(jnp.bfloat16))
        dv16 = flat(dv)
        dw = tuple(lax.dot_general(x, g, TN, preferred_element_type=jnp.float32) for g in (dq16, dk16, dv16))
        dw, dq16, dk16, dv16 = lax.optimization_barrier((dw, dq16, dk16, dv16))
        dx_part = sum(lax.dot_general(g, w, NT, preferred_element_type=jnp.float32) for g, w in ((dq16, wq), (dk16, wk), (dv16, wv)))
        grad_x = chain_sum(tp_size, 6, dx_part, gy)
        grad_w_o, *dw = lax.optimization_barrier((grad_w_o,) + tuple(dw))
        sums = lax.psum((tuple(dw), grad_q_norm, grad_k_norm, grad_post[0]), "cp")
        dw, grad_q_norm, grad_k_norm, grad_post = sums
        dw = tuple(g.reshape(d_model, heads, head_dim) for g in dw)
        return (y_out[None], grad_x[None]) + dw + (grad_w_o.reshape(heads, head_dim, d_model), grad_q_norm, grad_k_norm, grad_post)

    return jax.shard_map(local_run, mesh=mesh, in_specs=in_specs, out_specs=out_specs, check_vma=False)
```

time: 1620 us -> 1160 us (0.72)
  waiting for transfers between devices: 1160 us -> 102 us
  Pallas kernels: 0 us -> 891 us
  starting transfers between devices: 152 us -> 0.62 us
  matrix products: 103 us -> 46.5 us
  local copies, waits for them, and re-layouts: 95.4 us -> 53.6 us
  blocking collectives: 35.9 us -> 10.8 us
    pallas_call x0 -> x10, Pallas kernels: none -> 891 us  [the longest x1 645 us: chain_sum(): pl.pallas_call(functools.partial(chain_kernel, size, n_chunk, min(6, n_ch...]
    psum x3 -> x2, waiting for transfers between devices: 848 us -> 32 us  [the longest x1 32 us: local_run(): grad_w_o = lax.psum(dwo_part, 'cp')]
    ppermute x20 -> x1, waiting for transfers between devices: 308 us -> 6.79 us  [local_run(): other = lax.ppermute(mine, 'cp', swap_core)]
    ppermute x20 -> x1, starting transfers between devices: 151 us -> 0.46 us  [local_run(): other = lax.ppermute(mine, 'cp', swap_core)]
    all_gather x0 -> x2, waiting for transfers between devices: none -> 63.1 us  [the longest x1 63.1 us: local_run(): o_all = lax.all_gather(o_mine, 'tp')]
    while x24 -> x0, local copies, waits for them, and re-layouts: 54 us -> none
    dot_general x16 -> x10, matrix products: 92.8 us -> 46.5 us  [the longest x3 15.5 us: local_run(): lax.dot_general(x, g, TN, preferred_element_type=jnp.float32)]
    psum x3 -> x1, blocking collectives: 35.9 us -> 10.8 us  [local_run(): sums = lax.psum((tuple(dw), grad_q_norm, grad_k_norm, grad_post[0]), 'cp')]
  transfers between devices with their start and end apart: 23 -> 5, of which waited for: 16 -> 3; matrix products, arithmetic and copies ran while one was open for 3% -> 8% of each run, Pallas kernels for 0% -> 64%
where the time goes in v1:
time: 1160 us
  Pallas kernels  891 us (77%)
  waiting for transfers between devices  102 us (9%)
  local copies, waits for them, and re-layouts  53.6 us (5%)
  matrix products  46.5 us (4%)
  other arithmetic  39.6 us (3%)
  between operations  14.4 us (1%)
    pallas_call x1, Pallas kernels, chain_sum(): pl.pallas_call(functools.partial(chain_kernel, size, n_chunk, min(6, n_ch...  645 us
    pallas_call x4, Pallas kernels, exchange(): pl.pallas_call(functools.partial(exchange_kernel, axis, size, count), out...  136 us
    all_gather x1, waiting for transfers between devices, local_run(): o_all = lax.all_gather(o_mine, 'tp')  63.1 us
    pallas_call x1, Pallas kernels, attend_back(): pl.pallas_call(functools.partial(attend_back_kernel, block, head_dim ** (...  43.2 us
    psum x1, waiting for transfers between devices, local_run(): grad_w_o = lax.psum(dwo_part, 'cp')  32 us
    pallas_call x1, Pallas kernels, attend(): pl.pallas_call(functools.partial(attend_kernel, block, head_dim ** (-0.5)...  27.6 us
    pallas_call x1, Pallas kernels, post(): pl.pallas_call(functools.partial(post_kernel, tp_size), grid=(rows // blo...  23.3 us
  transfers between devices with their start and end apart: 5, of which 3 were waited for; matrix products, arithmetic and copies ran while one was open for 8% of the time, Pallas kernels for 64%

profile of v1, /device:TPU:0, one launch (start us, length us, event | category | flops | bytes accessed | tf_op | source)
XLA Modules:
  0.0 1158.1 jit_solution(11970733061159348989)
XLA Ops:
  7.2 2.4 constant_dynamic-slice_fusion
  9.8 4.6 fusion.27
  14.3 1.8 copy.45
  16.1 5.4 multiply_reduce_fusion.1
  21.5 3.7 multiply_reduce_fusion
  25.9 9.5 small_sum_0.1
  37.7 1.9 copy.43
  39.6 3.3 broadcast_multiply_fusion
  42.9 2.9 copy.44
  45.8 1.9 broadcast_multiply_fusion.2
  47.7 1.7 bitcast_multiply_fusion.3
  51.0 2.5 pad_maximum_fusion.2
  53.5 39.9 %exchange_1.1 = (bf16[4,1024,128]{2,1,0:T(8,128)(2,1)}, bf16[4,1024,128]{2,1,0:T(8,128)(2,1)}, bf16[4,1024,128]{2,1,0:T(8,128)(2,1)}) custom-call(bf16[4,1024,128]{2,1,0:T(8,128)(2,1)} %get-tuple-element.92.refs_0_, bf16[4,1024,128]{2,1,0:T(8,128)(2,1)} %get-tuple-element.93.refs_1_, bf16[4,1024,128]{2,1,0:T(8,128)(2,1)} %bitcast.139), custom_call_target="tpu_custom_call" | custom-call | tf_op jit(solution)/shard_map/exchange_1/pallas_call | solution.py:81
  93.4 27.6 %attend.1 = (bf16[4096,128]{1,0:T(8,128)(2,1)}, f32[1,4096]{1,0:T(1,128)}) custom-call(bf16[4096,128]{1,0:T(8,128)(2,1)} %bitcast.180, bf16[4096,128]{1,0:T(8,128)(2,1)} %bitcast.182, bf16[4096,128]{1,0:T(8,128)(2,1)} %bitcast.184), custom_call_target="tpu_custom_call" | custom-call | flops 4294967296 | bytes 4194304 | tf_op jit(solution)/shard_map/attend/pallas_call | solution.py:165
  121.0 16.3 %exchange_2.1 = bf16[4,1024,128]{2,1,0:T(8,128)(2,1)} custom-call(bf16[4,1024,128]{2,1,0:T(8,128)(2,1)} %bitcast.153), custom_call_target="tpu_custom_call" | custom-call | tf_op jit(solution)/shard_map/exchange_2/pallas_call | solution.py:81
  137.3 2.4 copy.46
  139.8 2.3 copy.47
  142.6 6.8 collective-permute-done
  149.4 10.3 maximum_select_fusion
  159.7 63.1 %all-gather.4.cloned.1.call-done.o_ref = bf16[4,1024,512]{2,1,0:T(8,128)(2,1)} async-done(((bf16[1,1024,512]{2,1,0:T(8,128)(2,1)}), bf16[4,1024,512]{2,1,0:T(8,128)(2,1)}) %all-gather.4.cloned.1.call-update) | async-done | bytes 4194320 | tf_op jit(solution)/shard_map/all_gather | solution.py:433
  222.8 23.3 %post.1 = (bf16[1024,2048]{1,0:T(8,128)(2,1)}, bf16[1024,2048]{1,0:T(8,128)(2,1)}, bf16[4,1024,128]{2,1,0:T(8,128)(2,1)}, f32[1,2048]{1,0:T(1,128)}) custom-call(bf16[4,1024,512]{2,1,0:T(8,128)(2,1)} %all-gather.4.cloned.1.call-done.o_ref, bf16[4,512,2048]{2,1,0:T(8,128)(2,1)} %bitcast.132, bf16[512,2048]{1,0:T(8,128)(2,1)} %bitcast.161, ...), custom_call_target="tpu_custom_call" | custom-call | flops 10737418240 | bytes 16777216 | tf_op jit(solution)/shard_map/post/pallas_call | solution.py:271
  246.1 16.0 %exchange_3.1 = bf16[4,1024,128]{2,1,0:T(8,128)(2,1)} custom-call(bf16[4,1024,128]{2,1,0:T(8,128)(2,1)} %get-tuple-element.39.refs_0_), custom_call_target="tpu_custom_call" | custom-call | tf_op jit(solution)/shard_map/exchange_3/pallas_call | solution.py:81
  262.0 43.2 %attend_back.1 = (f32[4096,128]{1,0:T(8,128)}, f32[4096,128]{1,0:T(8,128)}, bf16[4096,128]{1,0:T(8,128)(2,1)}) custom-call(bf16[4096,128]{1,0:T(8,128)(2,1)} %bitcast.181, bf16[4096,128]{1,0:T(8,128)(2,1)} %bitcast.183, bf16[4096,128]{1,0:T(8,128)(2,1)} %bitcast.185, bf16[4096,128]{1,0:T(8,128)(2,1)} %get-tuple-element.37.o_ref, ...), custom_call_target="tpu_custom_call" | custom-call | flops 10737418240 | bytes 10485760 | tf_op jit(solution)/shard_map/attend_back/pallas_call | solution.py:228
  305.2 63.6 %exchange_4.1 = (f32[4,1024,128]{2,1,0:T(8,128)}, f32[4,1024,128]{2,1,0:T(8,128)}, bf16[4,1024,128]{2,1,0:T(8,128)(2,1)}) custom-call(f32[4,1024,128]{2,1,0:T(8,128)} %bitcast.150, f32[4,1024,128]{2,1,0:T(8,128)} %bitcast.151, bf16[4,1024,128]{2,1,0:T(8,128)(2,1)} %bitcast.152), custom_call_target="tpu_custom_call" | custom-call | tf_op jit(solution)/shard_map/exchange_4/pallas_call | solution.py:81
  368.8 2.3 copy.50
  371.1 6.9 fusion.40
  378.0 4.8 multiply_subtract_fusion.1
  387.6 6.8 small_sum_5.1
  395.2 3.7 fusion.31
  400.2 3.1 fusion.30
  404.1 6.7 convolution_bitcast_fusion.2
  410.8 4.4 convolution_bitcast_fusion.1
  415.2 4.4 convolution_bitcast_fusion
  419.6 2.4 fusion.7
  422.0 2.4 fusion.3
  424.4 5.8 add_add_fusion.part_ref
  430.2 32.0 %all-reduce.5.cloned.1.call-done = f32[512,2048]{1,0:T(8,128)} async-done(((f32[512,2048]{1,0:T(8,128)}), f32[512,2048]{1,0:T(8,128)}) %all-reduce.5.cloned.1.call-update) | async-done | bytes 4194320 | tf_op jit(solution)/shard_map/psum | solution.py:437
  462.2 5.2 copy.52
  467.4 5.2 copy.53
  472.6 5.2 copy.54
  477.9 644.5 %chain_sum.1 = bf16[1024,2048]{1,0:T(8,128)(2,1)} custom-call(f32[1024,2048]{1,0:T(8,128)} %add_add_fusion.part_ref, bf16[1024,2048]{1,0:T(8,128)(2,1)} %bitcast.175), custom_call_target="tpu_custom_call" | custom-call | flops 99999997952 | bytes 33554432 | tf_op jit(solution)/shard_map/chain_sum/pallas_call | solution.py:370
  1122.4 10.8 all-reduce
  1133.3 4.9 copy.93
  1138.2 2.1 copy.94
  1140.3 1.6 copy-done.8
  1141.9 2.1 copy.95
  1145.6 2.1 copy.96
  1149.3 2.0 copy.97
  (69 shorter events, 16.0 us)
Async XLA Ops:
  7.2 2.6 copy-start.10
  7.2 135.0 %all-gather.6.cloned.1.call-start = ((), (), s32[]{:S(2)}) async-start(), calls=%async_computation.2 | async-start | bytes 5242880 | tf_op jit(solution)/shard_map/all_gather | solution.py:405
  9.7 213.1 %all-gather.4.cloned.1.call-start = ((), (), s32[]{:S(2)}) async-start(), calls=%async_computation | async-start | bytes 5242880 | tf_op jit(solution)/shard_map/all_gather | solution.py:433
  16.1 5.4 copy-start.17
  16.1 5.4 copy-start.20
  42.9 4.8 copy-start.13
  47.7 1.8 copy-start.14
  142.1 320.1 %all-reduce.5.cloned.1.call-start = ((), (), s32[]{:S(2)}) async-start(), calls=%async_computation.1 | async-start | bytes 8388608 | tf_op jit(solution)/shard_map/psum | solution.py:437
  142.2 7.2 collective-permute-start
  377.9 755.3 %all-reduce.7.cloned.1.call-start = ((), (), s32[]{:S(2)}) async-start(), calls=%async_computation.3 | async-start | bytes 25165824 | tf_op jit(solution)/shard_map/psum | solution.py:463
  382.8 1.6 copy-start.1
  382.8 2.1 copy-start.2
  382.8 2.8 copy-start.3
  382.8 4.2 copy-start.4
  382.8 3.2 copy-start
  404.1 6.7 copy-start.12
  404.1 6.7 copy-start.18
  410.8 4.4 copy-start.5
  415.2 4.4 copy-start.19
  419.6 2.4 copy-start.21
  422.0 2.4 copy-start.11
  477.9 644.6 %copy-start.15 = (f32[4,128]{1,0:T(4,128)S(1)}, f32[4,128]{1,0:T(4,128)}, u32[]{:S(2)}) copy-start(f32[4,128]{1,0:T(4,128)} %get-tuple-element.61) | copy-start | bytes 6148
  477.9 644.6 %copy-start.16 = (f32[1,2048]{1,0:T(1,128)S(1)}, f32[1,2048]{1,0:T(1,128)}, u32[]{:S(2)}) copy-start(f32[1,2048]{1,0:T(1,128)} %get-tuple-element.58) | copy-start | bytes 24580
  1133.3 4.9 copy-start.9
  1138.2 3.7 copy-start.8
  1141.9 3.7 copy-start.7
  1145.6 3.7 copy-start.6
Sparse Core Ops, SparseCore 0:
  10.1 83.5 all-gather.5
  142.2 80.5 all-gather.3
  378.1 84.0 all-reduce.4
  478.0 220.6 all-reduce.6

commit v2 on v1

--- a/solution.py
+++ b/solution.py
@@ -76,6 +76,41 @@
         copy.wait()
 
 
+def exchange_product_kernel(axis, size, block, in_ref, a_ref, b_ref, out_ref, prod_ref, send_sem, recv_sem):
+    me = lax.axis_index(axis)
+    entry_barrier(axis, size)
+    copies = []
+    for shift in (2, 1, 3) if size == 4 else range(1, size):
+        dst = lax.rem(me + shift, size)
+        copy = pltpu.make_async_remote_copy(
+            src_ref=in_ref.at[dst], dst_ref=out_ref.at[me], send_sem=send_sem.at[shift - 1], recv_sem=recv_sem.at[shift - 1],
+            device_id={axis: dst}, device_id_type=MESH)
+        copy.start()
+        copies.append(copy)
+    out_ref[me] = in_ref[me]
+
+    def step(idx, carry):
+        cols = pl.ds(pl.multiple_of(idx * block, block), block)
+        prod_ref[:, cols] = dot_tn(a_ref[...], b_ref[:, cols])
+        return carry
+
+    lax.fori_loop(0, b_ref.shape[1] // block, step, 0)
+    for copy in copies:
+        copy.wait()
+
+
+def exchange_product(axis, size, collective_id, array, a, b):
+    return pl.pallas_call(
+        functools.partial(exchange_product_kernel, axis, size, min(512, b.shape[1])),
+        out_shape=(jax.ShapeDtypeStruct(array.shape, array.dtype), jax.ShapeDtypeStruct((a.shape[1], b.shape[1]), jnp.float32)),
+        in_specs=[VMEM_SPEC] * 3,
+        out_specs=(VMEM_SPEC, VMEM_SPEC),
+        scratch_shapes=[pltpu.SemaphoreType.DMA((size - 1,)), pltpu.SemaphoreType.DMA((size - 1,))],
+        compiler_params=pltpu.CompilerParams(collective_id=collective_id, has_side_effects=True, vmem_limit_bytes=VMEM_LIMIT),
+        name="exchange_product",
+    )(array, a, b)
+
+
 def exchange(axis, size, collective_id, *arrays):
     count = len(arrays)
     return pl.pallas_call(
@@ -315,47 +350,65 @@
             send_sem=ag_send.at[side, chunk], recv_sem=ag_recv.at[side, chunk],
             device_id={"tp": away(side)}, device_id_type=MESH)
 
-    def step(idx, carry):
+    def place(side):
+        return me if side == 0 else last - me
+
+    def push(idx, carry):
         for side in (0, 1):
-            pos = me if side == 0 else last - me
-            local, glob, sums = parts(side, idx)
-
-            @pl.when((idx < n_chunk) & (pos == last))
+            @pl.when(place(side) == last)
             def _(side=side):
                 rs_copy(side, idx, True).start()
-
-            @pl.when((idx < n_chunk) & (pos > 0) & (pos < last))
-            def _(side=side, local=local, glob=glob, sums=sums):
-                rs_copy(side, idx, False).wait_recv()
-                sums[local] = sums[local] + part_ref[glob]
-                rs_copy(side, idx, False).start()
-
-            @pl.when((idx < n_chunk) & (pos == 0))
-            def _(side=side, local=local, glob=glob, sums=sums):
-                rs_copy(side, idx, False).wait_recv()
-                out_ref[glob] = (gy_ref[glob].astype(jnp.float32) + (sums[local] + part_ref[glob])).astype(jnp.bfloat16)
-                ag_copy(side, idx).start()
-
-            @pl.when((idx >= lag) & (pos > 0))
+        return carry
+
+    lax.fori_loop(0, n_chunk, push, 0)
+
+    def pass_on(side, chunk):
+        local, glob, sums = parts(side, chunk)
+        rs_copy(side, chunk, False).wait_recv()
+        sums[local] = sums[local] + part_ref[glob]
+        rs_copy(side, chunk, False).start()
+
+    def finish(side, chunk):
+        local, glob, sums = parts(side, chunk)
+        rs_copy(side, chunk, False).wait_recv()
+        out_ref[glob] = (gy_ref[glob].astype(jnp.float32) + (sums[local] + part_ref[glob])).astype(jnp.bfloat16)
+        ag_copy(side, chunk).start()
+
+    def reduce_step(idx, carry):
+        for far in range(last - 1, 0, -1):
+            chunk = idx - (last - 1 - far) * lag
+            for side in (0, 1):
+                @pl.when((chunk >= 0) & (chunk < n_chunk) & (place(side) == far))
+                def _(side=side, chunk=chunk):
+                    pass_on(side, chunk)
+        for side in (0, 1):
+            @pl.when((idx < n_chunk) & (place(side) == 0))
             def _(side=side):
-                ag_copy(side, idx - lag).wait_recv()
-
-            @pl.when((idx >= lag) & (pos > 0) & (pos < last))
-            def _(side=side):
-                ag_copy(side, idx - lag).start()
+                finish(side, idx)
         return carry
 
-    lax.fori_loop(0, n_chunk + lag, step, 0)
+    lax.fori_loop(0, n_chunk + (last - 2) * lag, reduce_step, 0)
+
+    def return_step(idx, carry):
+        for far in range(1, last + 1):
+            chunk = idx - (far - 1) * lag
+            for side in (0, 1):
+                @pl.when((chunk >= 0) & (chunk < n_chunk) & (place(side) == far))
+                def _(side=side, chunk=chunk, far=far):
+                    ag_copy(side, chunk).wait_recv()
+                    if far < last:
+                        ag_copy(side, chunk).start()
+        return carry
+
+    lax.fori_loop(0, n_chunk + (last - 1) * lag, return_step, 0)
 
     def drain(idx, carry):
         for side in (0, 1):
-            pos = me if side == 0 else last - me
-
-            @pl.when(pos > 0)
+            @pl.when(place(side) > 0)
             def _(side=side):
                 rs_copy(side, idx, False).wait_send()
 
-            @pl.when(pos < last)
+            @pl.when(place(side) < last)
             def _(side=side):
                 ag_copy(side, idx).wait_send()
         return carry
@@ -365,10 +418,10 @@
 
 def chain_sum(size, collective_id, part, gy):
     rows, d_model = part.shape
-    n_chunk = 16 if rows >= 512 else 2
+    n_chunk = 32 if rows >= 512 else 4
     sems = [pltpu.SemaphoreType.DMA((2, n_chunk))] * 4
     return pl.pallas_call(
-        functools.partial(chain_kernel, size, n_chunk, min(6, n_chunk)),
+        functools.partial(chain_kernel, size, n_chunk, 2),
         out_shape=jax.ShapeDtypeStruct((rows, d_model), jnp.bfloat16),
         in_specs=[VMEM_SPEC, VMEM_SPEC],
         out_specs=VMEM_SPEC,
@@ -432,8 +485,7 @@
         o_mine = o_heads.transpose(1, 0, 2).reshape(rows, width)
         o_all = lax.all_gather(o_mine, "tp")
         y_out, grad_proj, grad_o, grad_post = post(o_all, wo_all, w_o.reshape(width, d_model), x, gy, post_norm_w[None, :], heads, head_dim)
-        (do_seq,) = exchange("cp", cp_size, 3, grad_o)
-        dwo_part = lax.dot_general(o_mine, grad_proj, TN, preferred_element_type=jnp.float32)
+        do_seq, dwo_part = exchange_product("cp", cp_size, 3, grad_o, o_mine, grad_proj)
         grad_w_o = lax.psum(dwo_part, "cp")
 
         dq_seq, dk_seq, dv_seq = attend_back(q_seq, k_seq, v_seq, o_seq, do_seq.reshape(seq_shape), lse)
@@ -458,11 +510,16 @@
         dw = tuple(lax.dot_general(x, g, TN, preferred_element_type=jnp.float32) for g in (dq16, dk16, dv16))
         dw, dq16, dk16, dv16 = lax.optimization_barrier((dw, dq16, dk16, dv16))
         dx_part = sum(lax.dot_general(g, w, NT, preferred_element_type=jnp.float32) for g, w in ((dq16, wq), (dk16, wk), (dv16, wv)))
+        grad_w_o, *dw = lax.optimization_barrier((grad_w_o,) + tuple(dw))
+        dw = lax.psum(tuple(dw), "cp")
+        small = jnp.concatenate([grad_q_norm.reshape(1, width), grad_k_norm.reshape(1, width), grad_post], axis=1)
+        small = small_sum("cp", cp_size, 7, small)
+        dx_part, small = lax.optimization_barrier((dx_part, small))
         grad_x = chain_sum(tp_size, 6, dx_part, gy)
-        grad_w_o, *dw = lax.optimization_barrier((grad_w_o,) + tuple(dw))
-        sums = lax.psum((tuple(dw), grad_q_norm, grad_k_norm, grad_post[0]), "cp")
-        dw, grad_q_norm, grad_k_norm, grad_post = sums
-        dw = tuple(g.reshape(d_model, heads, head_dim) for g in dw)
+        grad_q_norm = small[0, :width].reshape(heads, head_dim)
+        grad_k_norm = small[0, width:2 * width].reshape(heads, head_dim)
+        grad_post = small[0, 2 * width:]
+        dw = tuple(g.reshape(d_model, heads, head_dim) for g in lax.optimization_barrier(dw))
         return (y_out[None], grad_x[None]) + dw + (grad_w_o.reshape(heads, head_dim, d_model), grad_q_norm, grad_k_norm, grad_post)
 
     return jax.shard_map(local_run, mesh=mesh, in_specs=in_specs, out_specs=out_specs, check_vma=False)

time: 1160 us -> 721 us (0.62)
  Pallas kernels: 891 us -> 445 us
  waiting for transfers between devices: 102 us -> 130 us
    pallas_call x1 -> x2, Pallas kernels: 645 us -> 176 us  [the longest x1 157 us: chain_sum(): pl.pallas_call(functools.partial(chain_kernel, size, n_chunk, 2), out_sha...]
    psum x1, waiting for transfers between devices: 0.01 us -> 61.2 us  [local_run(): dw = lax.psum(tuple(dw), 'cp')]
    psum x1, waiting for transfers between devices: 32 us -> 0.01 us  [local_run(): grad_w_o = lax.psum(dwo_part, 'cp')]
    pallas_call x4 -> x3, Pallas kernels: 136 us -> 153 us  [exchange(): pl.pallas_call(functools.partial(exchange_kernel, axis, size, count), out...]
    reshape x3 -> x1, local copies, waits for them, and re-layouts: 15.7 us -> 1.08 us  [local_run(): o_mine = o_heads.transpose(1, 0, 2).reshape(rows, width)]
    unnamed x49 -> x53, local copies, waits for them, and re-layouts: 19.8 us -> 24.8 us
  transfers between devices with their start and end apart: 5 -> 5, of which waited for: 3 -> 3; matrix products, arithmetic and copies ran while one was open for 8% -> 14% of each run, Pallas kernels for 64% -> 56%
where the time goes in v2:
time: 721 us; the launch traced here: 718 us
  Pallas kernels  445 us (62%)
  waiting for transfers between devices  130 us (18%)
  local copies, waits for them, and re-layouts  45.2 us (6%)
  matrix products  41.7 us (6%)
  other arithmetic  41.5 us (6%)
  between operations  14.4 us (2%)
    pallas_call x1, Pallas kernels, chain_sum(): pl.pallas_call(functools.partial(chain_kernel, size, n_chunk, 2), out_sha...  157 us
    pallas_call x3, Pallas kernels, exchange(): pl.pallas_call(functools.partial(exchange_kernel, axis, size, count), out...  153 us
    all_gather x1, waiting for transfers between devices, local_run(): o_all = lax.all_gather(o_mine, 'tp')  62.9 us
    psum x1, waiting for transfers between devices, local_run(): dw = lax.psum(tuple(dw), 'cp')  61.2 us
    pallas_call x1, Pallas kernels, attend_back(): pl.pallas_call(functools.partial(attend_back_kernel, block, head_dim ** (...  43.2 us
    pallas_call x1, Pallas kernels, attend(): pl.pallas_call(functools.partial(attend_kernel, block, head_dim ** (-0.5)...  27.6 us
    unnamed x53, local copies, waits for them, and re-layouts  24.8 us
    pallas_call x1, Pallas kernels, post(): pl.pallas_call(functools.partial(post_kernel, tp_size), grid=(rows // blo...  23.3 us
  transfers between devices with their start and end apart: 5, of which 3 were waited for; matrix products, arithmetic and copies ran while one was open for 14% of the time, Pallas kernels for 56%

profile of v2, /device:TPU:0, one launch (start us, length us, event | category | flops | bytes accessed | tf_op | source)
XLA Modules:
  0.0 718.0 jit_solution(17670106688411916635)
XLA Ops:
  7.2 2.4 constant_dynamic-slice_fusion
  9.8 4.6 fusion.27
  14.3 1.8 copy.46
  16.1 5.4 multiply_reduce_fusion.1
  21.5 3.7 multiply_reduce_fusion
  25.9 9.5 %small_sum_0.1 = f32[2,1024]{1,0:T(2,128)} custom-call(f32[2,1024]{1,0:T(2,128)} %pad_maximum_fusion.5.in_ref), custom_call_target="tpu_custom_call" | custom-call | tf_op jit(solution)/shard_map/small_sum_0/pallas_call | solution.py:148
  36.1 1.7 broadcast_multiply_fusion.1
  37.8 1.9 copy.44
  39.7 3.3 broadcast_multiply_fusion
  43.0 2.9 copy.45
  45.9 3.0 broadcast_multiply_fusion.2
  48.9 1.9 bitcast_multiply_fusion.3
  51.0 1.4 subtract_convert_fusion
  52.5 2.5 pad_maximum_fusion.2
  54.9 39.8 %exchange_1.1 = (bf16[4,1024,128]{2,1,0:T(8,128)(2,1)}, bf16[4,1024,128]{2,1,0:T(8,128)(2,1)}, bf16[4,1024,128]{2,1,0:T(8,128)(2,1)}) custom-call(bf16[4,1024,128]{2,1,0:T(8,128)(2,1)} %get-tuple-element.141.refs_0_, bf16[4,1024,128]{2,1,0:T(8,128)(2,1)} %get-tuple-element.142.refs_1_, bf16[4,1024,128]{2,1,0:T(8,128)(2,1)} %bitcast.146), custom_call_target="tpu_custom_call" | custom-call | tf_op jit(solution)/shard_map/exchange_1/pallas_call | solution.py:116
  94.7 27.6 %attend.1 = (bf16[4096,128]{1,0:T(8,128)(2,1)}, f32[1,4096]{1,0:T(1,128)}) custom-call(bf16[4096,128]{1,0:T(8,128)(2,1)} %bitcast.188, bf16[4096,128]{1,0:T(8,128)(2,1)} %bitcast.190, bf16[4096,128]{1,0:T(8,128)(2,1)} %bitcast.192), custom_call_target="tpu_custom_call" | custom-call | flops 4294967296 | bytes 4194304 | tf_op jit(solution)/shard_map/attend/pallas_call | solution.py:200
  122.3 16.3 %exchange_2.1 = bf16[4,1024,128]{2,1,0:T(8,128)(2,1)} custom-call(bf16[4,1024,128]{2,1,0:T(8,128)(2,1)} %bitcast.158), custom_call_target="tpu_custom_call" | custom-call | tf_op jit(solution)/shard_map/exchange_2/pallas_call | solution.py:116
  138.6 2.3 copy.47
  140.9 2.4 copy.48
  143.8 1.1 copy_bitcast_fusion.a_ref
  144.9 5.7 collective-permute-done
  150.6 10.5 %maximum_select_fusion = bf16[4,4,128,2048]{3,2,1,0:T(8,128)(2,1)} fusion(bf16[4,2,128,2048]{3,2,1,0:T(8,128)(2,1)} %collective-permute-done, bf16[4,2,128,2048]{3,2,1,0:T(8,128)(2,1)} %bitcast.145, pred[]{:T(512)S(6)} %eq.5), kind=kLoop, calls=%fused_computation | loop fusion | flops 12582912 | bytes 16777216 | tf_op jit(solution)/shard_map/jit(_where)/select_n | solution.py:460
  161.1 62.9 %all-gather.4.cloned.1.call-done.o_ref = bf16[4,1024,512]{2,1,0:T(8,128)(2,1)} async-done(((bf16[1,1024,512]{2,1,0:T(8,128)(2,1)}), bf16[4,1024,512]{2,1,0:T(8,128)(2,1)}) %all-gather.4.cloned.1.call-update) | async-done | bytes 4194320 | tf_op jit(solution)/shard_map/all_gather | solution.py:486
  224.0 23.3 %post.1 = (bf16[1024,2048]{1,0:T(8,128)(2,1)}, bf16[1024,2048]{1,0:T(8,128)(2,1)}, bf16[4,1024,128]{2,1,0:T(8,128)(2,1)}, f32[1,2048]{1,0:T(1,128)}) custom-call(bf16[4,1024,512]{2,1,0:T(8,128)(2,1)} %all-gather.4.cloned.1.call-done.o_ref, bf16[4,512,2048]{2,1,0:T(8,128)(2,1)} %bitcast.139, bf16[512,2048]{1,0:T(8,128)(2,1)} %bitcast.165, ...), custom_call_target="tpu_custom_call" | custom-call | flops 10737418240 | bytes 16777216 | tf_op jit(solution)/shard_map/post/pallas_call | solution.py:306
  247.3 18.8 %exchange_product.1 = (bf16[4,1024,128]{2,1,0:T(8,128)(2,1)}, f32[512,2048]{1,0:T(8,128)}) custom-call(bf16[4,1024,128]{2,1,0:T(8,128)(2,1)} %get-tuple-element.46.in_ref, bf16[1024,512]{1,0:T(8,128)(2,1)} %copy_bitcast_fusion.a_ref, bf16[1024,2048]{1,0:T(8,128)(2,1)} %get-tuple-element.47.b_ref), custom_call_target="tpu_custom_call" | custom-call | tf_op jit(solution)/shard_map/exchange_product/pallas_call | solution.py:103
  266.2 43.2 %attend_back.1 = (f32[4096,128]{1,0:T(8,128)}, f32[4096,128]{1,0:T(8,128)}, bf16[4096,128]{1,0:T(8,128)(2,1)}) custom-call(bf16[4096,128]{1,0:T(8,128)(2,1)} %bitcast.189, bf16[4096,128]{1,0:T(8,128)(2,1)} %bitcast.191, bf16[4096,128]{1,0:T(8,128)(2,1)} %bitcast.193, bf16[4096,128]{1,0:T(8,128)(2,1)} %get-tuple-element.44.o_ref, ...), custom_call_target="tpu_custom_call" | custom-call | flops 10737418240 | bytes 10485760 | tf_op jit(solution)/shard_map/attend_back/pallas_call | solution.py:263
  309.4 97.3 %exchange_4.1 = (f32[4,1024,128]{2,1,0:T(8,128)}, f32[4,1024,128]{2,1,0:T(8,128)}, bf16[4,1024,128]{2,1,0:T(8,128)(2,1)}) custom-call(f32[4,1024,128]{2,1,0:T(8,128)} %bitcast.155, f32[4,1024,128]{2,1,0:T(8,128)} %bitcast.156, bf16[4,1024,128]{2,1,0:T(8,128)(2,1)} %bitcast.157), custom_call_target="tpu_custom_call" | custom-call | tf_op jit(solution)/shard_map/exchange_4/pallas_call | solution.py:116
  406.7 2.4 copy.52
  409.0 4.8 multiply_subtract_fusion.1
  417.0 1.1 fusion.15
  418.8 5.1 small_sum_7.1
  424.4 6.8 small_sum_5.1
  432.0 3.7 fusion.31
  435.7 1.3 copy.51
  437.0 3.1 fusion.30
  440.9 6.9 convolution_bitcast_fusion.2
  447.9 4.4 convolution_bitcast_fusion.1
  452.3 4.4 convolution_bitcast_fusion
  456.7 4.1 fusion.7
  460.8 2.4 fusion.3
  463.2 5.8 add_add_fusion.part_ref
  469.1 157.1 %chain_sum.1 = bf16[1024,2048]{1,0:T(8,128)(2,1)} custom-call(f32[1024,2048]{1,0:T(8,128)} %add_add_fusion.part_ref, bf16[1024,2048]{1,0:T(8,128)(2,1)} %bitcast.183), custom_call_target="tpu_custom_call" | custom-call | flops 99999997952 | bytes 33554432 | tf_op jit(solution)/shard_map/chain_sum/pallas_call | solution.py:423
  627.3 61.2 %all-reduce.6.cloned.1.call-done = (f32[2048,512]{0,1:T(8,128)}, f32[2048,512]{0,1:T(8,128)}, f32[2048,512]{0,1:T(8,128)}) async-done(((f32[2048,512]{0,1:T(8,128)}, f32[2048,512]{0,1:T(8,128)}, f32[2048,512]{0,1:T(8,128)}), (f32[2048,512]{0,1:T(8,128)}, f32[2048,512]{0,1:T(8,128)}, f32[2048,512]{0,1:T(8,128)})) %all-reduce.6.cloned.1.call-update) | async-done | bytes 12582928 | tf_op jit(solution)/shard_map/psum | solution.py:514
  688.6 5.2 copy.53
  693.8 5.2 copy.54
  699.0 5.2 copy.55
  704.2 4.9 copy.97
  709.2 2.0 copy.98
  (73 shorter events, 9.3 us)
Async XLA Ops:
  7.2 2.6 copy-start.10
  7.2 136.1 %all-gather.6.cloned.1.call-start = ((), (), s32[]{:S(2)}) async-start(), calls=%async_computation.2 | async-start | bytes 5242880 | tf_op jit(solution)/shard_map/all_gather | solution.py:458
  9.7 214.3 %all-gather.4.cloned.1.call-start = ((), (), s32[]{:S(2)}) async-start(), calls=%async_computation | async-start | bytes 5242880 | tf_op jit(solution)/shard_map/all_gather | solution.py:486
  16.1 5.4 copy-start.20
  16.1 5.4 copy-start.22
  43.0 5.9 copy-start.17
  48.9 2.1 copy-start.6
  48.9 1.9 copy-start.18
  140.9 2.9 copy-start.5
  143.3 325.8 %all-reduce.4.cloned.1.call-start = ((), (), s32[]{:S(2)}) async-start(), calls=%async_computation.1 | async-start | bytes 8388608 | tf_op jit(solution)/shard_map/psum | solution.py:489
  143.3 7.2 %collective-permute-start = (bf16[4,2,128,2048]{3,2,1,0:T(8,128)(2,1)}, bf16[4,2,128,2048]{3,2,1,0:T(8,128)(2,1)}, u32[]{:S(2)}, u32[]{:S(2)}) collective-permute-start(bf16[4,2,128,2048]{3,2,1,0:T(8,128)(2,1)} %bitcast.144), channel_id=1, source_target_pairs={{0,1},{1,0},{2,3},{3,2},{4,5},{5,4},{6,7},{7,6},{8,9},{9,8},{10,11... | collective-permute-start | bytes 12582920 | tf_op jit(solution)/shard_map/ppermute | solution.py:459
  266.1 422.4 %all-reduce.6.cloned.1.call-start = ((), (), s32[]{:S(2)}) async-start(), calls=%async_computation.3 | async-start | bytes 25165824 | tf_op jit(solution)/shard_map/psum | solution.py:514
  406.6 2.4 copy-start.7
  406.7 2.4 copy-start.12
  413.8 1.3 copy-start.1
  413.8 2.1 copy-start.2
  413.8 2.8 copy-start.3
  413.9 4.3 copy-start.4
  413.9 3.2 copy-start
  417.0 1.1 copy-start.19
  440.9 7.0 copy-start.14
  440.9 7.0 copy-start.13
  440.9 7.0 copy-start.21
  447.9 4.4 copy-start.8
  452.3 4.4 copy-start.15
  456.7 4.1 copy-start.23
  460.8 2.4 copy-start.11
  469.0 157.1 %copy-start.16 = (f32[1,3072]{1,0:T(1,128)S(1)}, f32[1,3072]{1,0:T(1,128)}, u32[]{:S(2)}) copy-start(f32[1,3072]{1,0:T(1,128)} %small_sum_7.1) | copy-start | bytes 36868
  704.2 4.9 copy-start.9
Sparse Core Ops, SparseCore 0:
  10.1 83.5 all-gather.5
  143.4 80.5 all-gather.3
  266.3 118.2 all-reduce.3
  469.2 219.3 all-reduce.5

commit v3 on v2

--- a/solution.py
+++ b/solution.py
@@ -30,19 +30,17 @@
     return jnp.dot(a, b, preferred_element_type=jnp.float32)
 
 
-def rope_tables(start_pos, seq_rows, head_dim):
+def rope_tables(positions, head_dim):
     half_dim = head_dim // 2
     inv_freq = ROPE_THETA ** (-2.0 * jnp.arange(half_dim, dtype=jnp.float32) / head_dim)
-    positions = (start_pos + jnp.arange(seq_rows)).astype(jnp.float32)
     angles = positions[:, None] * inv_freq[None, :]
     return jnp.cos(angles), jnp.sin(angles)
 
 
-def rope(values, cos_tab, sin_tab, sign):
+def rope(values, cos_tab, sin_tab):
     half_dim = values.shape[-1] // 2
     low_half = values[..., :half_dim]
     high_half = values[..., half_dim:]
-    sin_tab = sign * sin_tab
     return jnp.concatenate([low_half * cos_tab - high_half * sin_tab, high_half * cos_tab + low_half * sin_tab], axis=-1)
 
 
@@ -317,7 +315,7 @@
     )(o_all, wo_all, w_own, x, gy, gain)
 
 
-def chain_kernel(size, n_chunk, lag, part_ref, gy_ref, out_ref, sums_a, sums_b, rs_send, rs_recv, ag_send, ag_recv):
+def chain_kernel(size, n_chunk, lag, tile, dq_ref, dk_ref, dv_ref, wq_ref, wk_ref, wv_ref, gy_ref, out_ref, part_ref, sums_a, sums_b, rs_send, rs_recv, ag_send, ag_recv):
     me = lax.axis_index("tp")
     entry_barrier("tp", size)
     half = part_ref.shape[0] // 2
@@ -353,14 +351,43 @@
     def place(side):
         return me if side == 0 else last - me
 
-    def push(idx, carry):
+    heads = dq_ref.shape[0]
+    d_model = out_ref.shape[1]
+    block = min(512, d_model)
+    n_tile = 2 * half // tile
+    per_tile = tile // rows
+
+    def push(number):
         for side in (0, 1):
-            @pl.when(place(side) == last)
+            @pl.when((lax.rem(number, 2) == side) & (place(side) == last))
             def _(side=side):
-                rs_copy(side, idx, True).start()
+                def one(idx, carry):
+                    rs_copy(side, (number // 2) * per_tile + idx, True).start()
+                    return carry
+                lax.fori_loop(0, per_tile, one, 0)
+
+    def product(number, carry):
+        tile_rows = pl.ds(pl.multiple_of(lax.rem(number, 2) * half + (number // 2) * tile, tile), tile)
+
+        def columns(idx, carry):
+            cols = pl.ds(pl.multiple_of(idx * block, block), block)
+            total = None
+            for grad_ref, w_ref in ((dq_ref, wq_ref), (dk_ref, wk_ref), (dv_ref, wv_ref)):
+                grad = jnp.concatenate([grad_ref[idx_h, tile_rows, :] for idx_h in range(heads)], axis=1)
+                term = dot_nn(grad, w_ref[:, cols])
+                total = term if total is None else total + term
+            part_ref[tile_rows, cols] = total
+            return carry
+
+        lax.fori_loop(0, d_model // block, columns, 0)
+
+        @pl.when(number > 0)
+        def _():
+            push(number - 1)
         return carry
 
-    lax.fori_loop(0, n_chunk, push, 0)
+    lax.fori_loop(0, n_tile, product, 0)
+    push(jnp.int32(n_tile - 1))
 
     def pass_on(side, chunk):
         local, glob, sums = parts(side, chunk)
@@ -416,20 +443,181 @@
     lax.fori_loop(0, n_chunk, drain, 0)
 
 
-def chain_sum(size, collective_id, part, gy):
-    rows, d_model = part.shape
+def chain_sum(size, collective_id, grads, weights, gy):
+    rows, d_model = gy.shape
     n_chunk = 32 if rows >= 512 else 4
     sems = [pltpu.SemaphoreType.DMA((2, n_chunk))] * 4
     return pl.pallas_call(
-        functools.partial(chain_kernel, size, n_chunk, 2),
+        functools.partial(chain_kernel, size, n_chunk, 2, min(256, rows // 4)),
         out_shape=jax.ShapeDtypeStruct((rows, d_model), jnp.bfloat16),
-        in_specs=[VMEM_SPEC, VMEM_SPEC],
+        in_specs=[VMEM_SPEC] * 7,
         out_specs=VMEM_SPEC,
-        scratch_shapes=[pltpu.VMEM((rows // 2, d_model), jnp.float32), pltpu.VMEM((rows // 2, d_model), jnp.float32)] + sems,
+        scratch_shapes=[pltpu.VMEM((rows, d_model), jnp.float32), pltpu.VMEM((rows // 2, d_model), jnp.float32), pltpu.VMEM((rows // 2, d_model), jnp.float32)] + sems,
         compiler_params=pltpu.CompilerParams(collective_id=collective_id, has_side_effects=True, vmem_limit_bytes=VMEM_LIMIT),
         cost_estimate=pl.CostEstimate(flops=10 ** 11, bytes_accessed=16 * rows * d_model, transcendentals=0),
         name="chain_sum",
-    )(part, gy)
+    )(*grads, *weights, gy)
+
+
+def flip(index, distance):
+    if distance == 1:
+        return index + 1 - 2 * lax.rem(index, 2)
+    if distance == 2:
+        return lax.rem(index + 2, 4)
+    return 3 - index if distance == 3 else index
+
+
+def weights_back_kernel(tp_size, full_width, sub, x0, x1, x2, x3, wqk_ref, dq_ref, dk_ref, dv_ref, cos_ref, sin_ref, qg_ref, kg_ref,
+                        dwq_ref, dwk_ref, dwv_ref, exq_ref, exk_ref, exv_ref, gq_ref, gk_ref,
+                        x_buf, lin_ref, q16_ref, k16_ref, own, slots_tp, mid, slots_cp, total, x_sem, tp_send, tp_recv, cp_send, cp_recv, ex_send, ex_recv):
+    me = lax.axis_index("cp")
+    my_tp = lax.axis_index("tp")
+    rows, head_dim = dq_ref.shape[1:]
+    loads = []
+    for dist, x_ref in enumerate((x0, x1, x2, x3)):
+        load = pltpu.make_async_copy(x_ref, x_buf.at[dist], x_sem.at[dist])
+        load.start()
+        loads.append(load)
+    barrier = pltpu.get_barrier_semaphore()
+    for dist in (1, 2, 3):
+        pl.semaphore_signal(barrier, inc=1, device_id={"cp": flip(me, dist)}, device_id_type=MESH)
+    for shift in range(1, tp_size):
+        pl.semaphore_signal(barrier, inc=1, device_id={"tp": lax.rem(my_tp + shift, tp_size)}, device_id_type=MESH)
+    pl.semaphore_wait(barrier, 3 + tp_size - 1)
+
+    def ex_copy(idx, src, dst, dist):
+        peer = flip(me, dist)
+        return pltpu.make_async_remote_copy(
+            src_ref=src.at[peer], dst_ref=dst.at[me], send_sem=ex_send.at[idx, dist - 1], recv_sem=ex_recv.at[idx, dist - 1],
+            device_id={"cp": peer}, device_id_type=MESH)
+
+    copies = [ex_copy(2, dv_ref, exv_ref, dist) for dist in (2, 3, 1)]
+    for copy in copies:
+        copy.start()
+
+    def grad_of(ref, blk, part, table):
+        g = ref[blk, part, :]
+        half_dim = head_dim // 2
+        turned = jnp.concatenate([g[:, half_dim:], g[:, :half_dim]], axis=1)
+        return g * cos_ref[table, :] - turned * sin_ref[table, :]
+
+    sides = ((dq_ref, qg_ref, 0), (dk_ref, kg_ref, 1))
+    for dist in range(4):
+        blk = flip(me, dist)
+        loads[dist].wait()
+
+        def first(idx, carry, dist=dist, blk=blk):
+            part = pl.ds(pl.multiple_of(idx * sub, sub), sub)
+            table = pl.ds(pl.multiple_of(blk * rows + idx * sub, sub), sub)
+            lin = dot_nn(x_buf[dist, part, :], wqk_ref[...])
+            lin_ref[dist, part, :] = lin
+            for ref, gain_ref, number in sides:
+                mine = lin[:, number * head_dim:(number + 1) * head_dim]
+                grad = grad_of(ref, blk, part, table) * gain_ref[...]
+                own[2 * number:2 * number + 1, table] = jnp.sum((mine * mine).T, axis=0, keepdims=True)
+                own[2 * number + 1:2 * number + 2, table] = jnp.sum((grad * mine).T, axis=0, keepdims=True)
+            return carry
+
+        lax.fori_loop(0, rows // sub, first, 0)
+
+    moves = []
+    for shift in range(1, tp_size):
+        move = pltpu.make_async_remote_copy(
+            src_ref=own, dst_ref=slots_tp.at[my_tp], send_sem=tp_send.at[shift - 1], recv_sem=tp_recv.at[shift - 1],
+            device_id={"tp": lax.rem(my_tp + shift, tp_size)}, device_id_type=MESH)
+        move.start()
+        moves.append(move)
+    slots_tp[my_tp] = own[...]
+    for move in moves:
+        move.wait()
+    acc = slots_tp[0]
+    for idx in range(1, tp_size):
+        acc = acc + slots_tp[idx]
+    mid[...] = acc
+    moves = []
+    for dist in (2, 3, 1):
+        move = pltpu.make_async_remote_copy(
+            src_ref=mid, dst_ref=slots_cp.at[me], send_sem=cp_send.at[dist - 1], recv_sem=cp_recv.at[dist - 1],
+            device_id={"cp": flip(me, dist)}, device_id_type=MESH)
+        move.start()
+        moves.append(move)
+    slots_cp[me] = mid[...]
+    for move in moves:
+        move.wait()
+    total[...] = slots_cp[0] + slots_cp[1] + slots_cp[2] + slots_cp[3]
+
+    gq_ref[...] = jnp.zeros_like(gq_ref)
+    gk_ref[...] = jnp.zeros_like(gk_ref)
+    outs = ((q16_ref, exq_ref, gq_ref), (k16_ref, exk_ref, gk_ref))
+    for dist in (2, 3, 1, 0):
+        blk = flip(me, dist)
+
+        def second(idx, carry, dist=dist, blk=blk):
+            part = pl.ds(pl.multiple_of(idx * sub, sub), sub)
+            table = pl.ds(pl.multiple_of(blk * rows + idx * sub, sub), sub)
+            lin = lin_ref[dist, part, :]
+            for (ref, gain_ref, number), (d16_ref, _, gain_out) in zip(sides, outs):
+                mine = lin[:, number * head_dim:(number + 1) * head_dim]
+                inv = lax.rsqrt(total[2 * number:2 * number + 1, table] / full_width + NORM_EPS)
+                dot = inv * total[2 * number + 1:2 * number + 2, table] / full_width
+                inv = jnp.broadcast_to(inv, (head_dim, sub)).T
+                dot = jnp.broadcast_to(dot, (head_dim, sub)).T
+                raw = grad_of(ref, blk, part, table)
+                hat = mine * inv
+                d16_ref[blk, part, :] = (inv * (raw * gain_ref[...] - hat * dot)).astype(jnp.bfloat16)
+                gain_out[...] += jnp.sum(raw * hat, axis=0, keepdims=True)
+            return carry
+
+        lax.fori_loop(0, rows // sub, second, 0)
+        if dist:
+            for idx, (d16_ref, ex_ref, _) in enumerate(outs):
+                copy = ex_copy(idx, d16_ref, ex_ref, dist)
+                copy.start()
+                copies.append(copy)
+    for src, dst in ((q16_ref, exq_ref), (k16_ref, exk_ref), (dv_ref, exv_ref)):
+        dst[me] = src[me]
+
+    block = min(512, x_buf.shape[2])
+
+    def weight_step(idx, carry):
+        cols = pl.ds(pl.multiple_of(idx * block, block), block)
+        acc = None
+        for dist in range(4):
+            blk = flip(me, dist)
+            grads = jnp.concatenate([q16_ref[blk], k16_ref[blk], dv_ref[blk]], axis=1)
+            term = dot_tn(grads, x_buf[dist, :, cols])
+            acc = term if acc is None else acc + term
+        acc = acc.T
+        for number, out in enumerate((dwq_ref, dwk_ref, dwv_ref)):
+            out[cols, :] = acc[:, number * head_dim:(number + 1) * head_dim]
+        return carry
+
+    lax.fori_loop(0, x_buf.shape[2] // block, weight_step, 0)
+    for copy in copies:
+        copy.wait()
+
+
+def weights_back(tp_size, collective_id, full_width, xs, wqk, dq, dk, dv, cos_tab, sin_tab, q_gain, k_gain):
+    _, rows, head_dim = dq.shape
+    d_model = xs[0].shape[1]
+    any_spec = pl.BlockSpec(memory_space=pl.ANY)
+    dma = pltpu.SemaphoreType.DMA
+    stat = pltpu.VMEM((4, 4 * rows), jnp.float32)
+    dw = jax.ShapeDtypeStruct((d_model, head_dim), jnp.float32)
+    ex = jax.ShapeDtypeStruct(dq.shape, jnp.bfloat16)
+    gain = jax.ShapeDtypeStruct((1, head_dim), jnp.float32)
+    return pl.pallas_call(
+        functools.partial(weights_back_kernel, tp_size, full_width, min(256, rows)),
+        out_shape=(dw, dw, dw, ex, ex, ex, gain, gain),
+        in_specs=[any_spec] * 4 + [VMEM_SPEC] * 8,
+        out_specs=tuple([VMEM_SPEC] * 8),
+        scratch_shapes=[pltpu.VMEM((4, rows, d_model), jnp.bfloat16), pltpu.VMEM((4, rows, 2 * head_dim), jnp.float32),
+                        pltpu.VMEM(dq.shape, jnp.bfloat16), pltpu.VMEM(dq.shape, jnp.bfloat16),
+                        stat, pltpu.VMEM((tp_size, 4, 4 * rows), jnp.float32), stat, pltpu.VMEM((4, 4, 4 * rows), jnp.float32), stat,
+                        dma((4,)), dma((tp_size - 1,)), dma((tp_size - 1,)), dma((3,)), dma((3,)), dma((3, 3)), dma((3, 3))],
+        compiler_params=pltpu.CompilerParams(collective_id=collective_id, has_side_effects=True, vmem_limit_bytes=VMEM_LIMIT),
+        name="weights_back",
+    )(*xs, wqk, dq, dk, dv, cos_tab, sin_tab, q_gain, k_gain)
 
 
 def solution(mesh):
@@ -450,7 +638,7 @@
         x = x_in[0]
         gy = grad_y[0]
         cp_index = lax.axis_index("cp")
-        cos_tab, sin_tab = rope_tables(cp_index * rows, rows, head_dim)
+        cos_tab, sin_tab = rope_tables((cp_index * rows + jnp.arange(rows)).astype(jnp.float32), head_dim)
         wq, wk, wv = (w.reshape(d_model, width) for w in (w_q, w_k, w_v))
 
         core = cp_index % 2
@@ -473,8 +661,8 @@
         k_hat = by_head(k_lin * invs[1])
         q_gain = q_norm_w[:, None, :]
         k_gain = k_norm_w[:, None, :]
-        q_rot = rope(q_hat * q_gain, cos_tab, sin_tab, 1.0).astype(jnp.bfloat16)
-        k_rot = rope(k_hat * k_gain, cos_tab, sin_tab, 1.0).astype(jnp.bfloat16)
+        q_rot = rope(q_hat * q_gain, cos_tab, sin_tab).astype(jnp.bfloat16)
+        k_rot = rope(k_hat * k_gain, cos_tab, sin_tab).astype(jnp.bfloat16)
         v_val = by_head(v_lin.astype(jnp.bfloat16))
 
         seq_shape = (cp_size * rows, head_dim)
@@ -482,6 +670,17 @@
         q_seq, k_seq, v_seq = (t.reshape(seq_shape) for t in exchange("cp", cp_size, 1, q_rot, k_rot, v_val))
         o_seq, lse = attend(q_seq, k_seq, v_seq)
         (o_heads,) = exchange("cp", cp_size, 2, o_seq.reshape(block_shape))
+        positions = jnp.arange(cp_size * rows, dtype=jnp.float32)
+        o_heads, x_send, positions, w_q2, w_k2, w_v2 = lax.optimization_barrier((o_heads, x, positions, w_q, w_k, w_v))
+        x_far = lax.ppermute(x_send, "cp", [(dev, dev ^ 2) for dev in range(cp_size)])
+        x_near = lax.ppermute(x_send, "cp", swap_core)
+        x_cross = lax.ppermute(x_far, "cp", swap_core)
+        seq_cos, seq_sin = rope_tables(positions, head_dim)
+        seq_cos = jnp.concatenate([seq_cos, seq_cos], axis=1)
+        seq_sin = jnp.concatenate([-seq_sin, seq_sin], axis=1)
+        turned = tuple(w.reshape(d_model, width).T for w in (w_q2, w_k2, w_v2))
+        wqk_head = jnp.concatenate([lax.dynamic_slice_in_dim(w, cp_index, 1, axis=1)[:, 0, :] for w in (w_q2, w_k2)], axis=1)
+        gains_head = tuple(lax.dynamic_slice_in_dim(w, cp_index, 1, axis=0) for w in (q_norm_w, k_norm_w))
         o_mine = o_heads.transpose(1, 0, 2).reshape(rows, width)
         o_all = lax.all_gather(o_mine, "tp")
         y_out, grad_proj, grad_o, grad_post = post(o_all, wo_all, w_o.reshape(width, d_model), x, gy, post_norm_w[None, :], heads, head_dim)
@@ -489,37 +688,19 @@
         grad_w_o = lax.psum(dwo_part, "cp")
 
         dq_seq, dk_seq, dv_seq = attend_back(q_seq, k_seq, v_seq, o_seq, do_seq.reshape(seq_shape), lse)
-        dq, dk, dv = exchange("cp", cp_size, 4, dq_seq.reshape(block_shape), dk_seq.reshape(block_shape), dv_seq.reshape(block_shape))
-
-        def scaled_back(grad_rot, hat, gain):
-            grad = rope(grad_rot, cos_tab, sin_tab, -1.0)
-            grad_gain = jnp.sum(grad * hat, axis=1)
-            grad_hat = grad * gain
-            return grad_hat, grad_gain, jnp.sum(grad_hat * hat, axis=(0, 2))
-
-        gq_hat, grad_q_norm, q_dot = scaled_back(dq, q_hat, q_gain)
-        gk_hat, grad_k_norm, k_dot = scaled_back(dk, k_hat, k_gain)
-        dots = small_sum("tp", tp_size, 5, jnp.stack([q_dot, k_dot])) / full_width
-
-        def flat(t):
-            return t.transpose(1, 0, 2).reshape(rows, width)
-
-        dq16 = flat((invs[0][None] * (gq_hat - q_hat * dots[0][None, :, None])).astype(jnp.bfloat16))
-        dk16 = flat((invs[1][None] * (gk_hat - k_hat * dots[1][None, :, None])).astype(jnp.bfloat16))
-        dv16 = flat(dv)
-        dw = tuple(lax.dot_general(x, g, TN, preferred_element_type=jnp.float32) for g in (dq16, dk16, dv16))
-        dw, dq16, dk16, dv16 = lax.optimization_barrier((dw, dq16, dk16, dv16))
-        dx_part = sum(lax.dot_general(g, w, NT, preferred_element_type=jnp.float32) for g, w in ((dq16, wq), (dk16, wk), (dv16, wv)))
-        grad_w_o, *dw = lax.optimization_barrier((grad_w_o,) + tuple(dw))
-        dw = lax.psum(tuple(dw), "cp")
-        small = jnp.concatenate([grad_q_norm.reshape(1, width), grad_k_norm.reshape(1, width), grad_post], axis=1)
+        *dw, dq16, dk16, dv16, gain_q, gain_k = weights_back(
+            tp_size, 4, full_width, (x, x_near, x_far, x_cross), wqk_head,
+            dq_seq.reshape(block_shape), dk_seq.reshape(block_shape), dv_seq.reshape(block_shape), seq_cos, seq_sin, *gains_head)
+        dw = lax.all_gather(jnp.stack(dw), "cp")
+        own_head = jnp.arange(heads)[:, None] == cp_index
+        small = jnp.concatenate([jnp.where(own_head, gain, 0.0).reshape(1, width) for gain in (gain_q, gain_k)] + [grad_post], axis=1)
         small = small_sum("cp", cp_size, 7, small)
-        dx_part, small = lax.optimization_barrier((dx_part, small))
-        grad_x = chain_sum(tp_size, 6, dx_part, gy)
+        dq16, small = lax.optimization_barrier((dq16, small))
+        grad_x = chain_sum(tp_size, 6, (dq16, dk16, dv16), turned, gy)
         grad_q_norm = small[0, :width].reshape(heads, head_dim)
         grad_k_norm = small[0, width:2 * width].reshape(heads, head_dim)
         grad_post = small[0, 2 * width:]
-        dw = tuple(g.reshape(d_model, heads, head_dim) for g in lax.optimization_barrier(dw))
+        dw = tuple(dw[:, number].transpose(1, 0, 2) for number in range(3))
         return (y_out[None], grad_x[None]) + dw + (grad_w_o.reshape(heads, head_dim, d_model), grad_q_norm, grad_k_norm, grad_post)
 
     return jax.shard_map(local_run, mesh=mesh, in_specs=in_specs, out_specs=out_specs, check_vma=False)

time: 721 us -> 653 us (0.906)
  waiting for transfers between devices: 130 us -> 75 us
  local copies, waits for them, and re-layouts: 45.2 us -> 74 us
  matrix products: 41.7 us -> 15 us
  Pallas kernels: 445 us -> 430 us
    pallas_call x3 -> x2, Pallas kernels: 153 us -> 56.1 us  [exchange(): pl.pallas_call(functools.partial(exchange_kernel, axis, size, count), out...]
    pallas_call x1 -> x2, Pallas kernels: 157 us -> 246 us  [the longest x1 167 us: chain_sum(): pl.pallas_call(functools.partial(chain_kernel, size, n_chunk, 2, min(256,...]
    ppermute x0 -> x3, waiting for transfers between devices: none -> 75 us  [the longest x1 75 us: local_run(): lax.ppermute(x_send, 'cp', [(dev, dev ^ 2) for dev in range(cp_size)])]
    all_gather x1, waiting for transfers between devices: 62.9 us -> 0.01 us  [local_run(): o_all = lax.all_gather(o_mine, 'tp')]
    psum x1 -> x0, waiting for transfers between devices: 61.2 us -> none  [local_run(): dw = lax.psum(tuple(dw), 'cp')]
    dot_general x6 -> x0, matrix products: 28 us -> none  [the longest x3 15.7 us: local_run(): lax.dot_general(x, g, TN, preferred_element_type=jnp.float32)]
    optimization_barrier x0 -> x5, local copies, waits for them, and re-layouts: none -> 13.1 us  [local_run(): lax.optimization_barrier((o_heads, x, positions, w_q, w_k, w_v))]
    unnamed x53 -> x45, local copies, waits for them, and re-layouts: 24.8 us -> 37.5 us
  transfers between devices with their start and end apart: 5 -> 8, of which waited for: 3 -> 1; matrix products, arithmetic and copies ran while one was open for 14% -> 12% of each run, Pallas kernels for 56% -> 66%
where the time goes in v3:
time: 653 us; the launch traced here: 649 us
  Pallas kernels  430 us (66%)
  waiting for transfers between devices  75 us (11%)
  local copies, waits for them, and re-layouts  74 us (11%)
  other arithmetic  38.1 us (6%)
  matrix products  15 us (2%)
  between operations  14.4 us (2%)
    pallas_call x1, Pallas kernels, chain_sum(): pl.pallas_call(functools.partial(chain_kernel, size, n_chunk, 2, min(256,...  167 us
    pallas_call x1, Pallas kernels, weights_back(): pl.pallas_call(functools.partial(weights_back_kernel, tp_size, full_width...  78.4 us
    ppermute x1, waiting for transfers between devices, local_run(): lax.ppermute(x_send, 'cp', [(dev, dev ^ 2) for dev in range(cp_size)])  75 us
    pallas_call x2, Pallas kernels, exchange(): pl.pallas_call(functools.partial(exchange_kernel, axis, size, count), out...  56.1 us
    pallas_call x1, Pallas kernels, attend_back(): pl.pallas_call(functools.partial(attend_back_kernel, block, head_dim ** (...  43.3 us
    unnamed x45, local copies, waits for them, and re-layouts  37.5 us
    pallas_call x1, Pallas kernels, attend(): pl.pallas_call(functools.partial(attend_kernel, block, head_dim ** (-0.5)...  27.6 us
    pallas_call x1, Pallas kernels, post(): pl.pallas_call(functools.partial(post_kernel, tp_size), grid=(rows // blo...  23.3 us
  transfers between devices with their start and end apart: 8, of which 1 were waited for; matrix products, arithmetic and copies ran while one was open for 12% of the time, Pallas kernels for 66%

profile of v3, /device:TPU:0, one launch (start us, length us, event | category | flops | bytes accessed | tf_op | source)
XLA Modules:
  0.0 648.7 jit_solution(8994620114167188581)
XLA Ops:
  7.2 2.4 constant_dynamic-slice_fusion.2
  9.8 6.0 multiply_reduce_fusion.1
  15.8 3.7 multiply_reduce_fusion
  20.2 9.6 %small_sum_0.1 = f32[2,1024]{1,0:T(2,128)} custom-call(f32[2,1024]{1,0:T(2,128)} %pad_maximum_fusion.7.in_ref), custom_call_target="tpu_custom_call" | custom-call | tf_op jit(solution)/shard_map/small_sum_0/pallas_call | solution.py:146
  30.6 1.8 broadcast_multiply_fusion.1
  32.4 2.1 copy.51
  34.5 1.8 broadcast_multiply_fusion
  36.3 1.8 copy.52
  38.1 5.2 fusion.9
  43.4 1.3 copy.53
  44.7 1.9 multiply_cosine_fusion.1
  46.8 1.4 copy-done.8
  48.4 1.4 subtract_convert_fusion
  49.8 2.5 pad_maximum_fusion.3
  52.3 39.8 %exchange_1.1 = (bf16[4,1024,128]{2,1,0:T(8,128)(2,1)}, bf16[4,1024,128]{2,1,0:T(8,128)(2,1)}, bf16[4,1024,128]{2,1,0:T(8,128)(2,1)}) custom-call(bf16[4,1024,128]{2,1,0:T(8,128)(2,1)} %get-tuple-element.93.refs_0_, bf16[4,1024,128]{2,1,0:T(8,128)(2,1)} %get-tuple-element.94.refs_1_, bf16[4,1024,128]{2,1,0:T(8,128)(2,1)} %bitcast.112), custom_call_target="tpu_custom_call" | custom-call | tf_op jit(solution)/shard_map/exchange_1/pallas_call | solution.py:114
  92.1 27.6 %attend.1 = (bf16[4096,128]{1,0:T(8,128)(2,1)}, f32[1,4096]{1,0:T(1,128)}) custom-call(bf16[4096,128]{1,0:T(8,128)(2,1)} %bitcast.149, bf16[4096,128]{1,0:T(8,128)(2,1)} %bitcast.151, bf16[4096,128]{1,0:T(8,128)(2,1)} %bitcast.153), custom_call_target="tpu_custom_call" | custom-call | flops 4294967296 | bytes 4194304 | tf_op jit(solution)/shard_map/attend/pallas_call | solution.py:198
  119.7 16.3 %exchange_2.1 = bf16[4,1024,128]{2,1,0:T(8,128)(2,1)} custom-call(bf16[4,1024,128]{2,1,0:T(8,128)(2,1)} %bitcast.129), custom_call_target="tpu_custom_call" | custom-call | tf_op jit(solution)/shard_map/exchange_2/pallas_call | solution.py:114
  136.0 1.5 copy.54
  137.5 1.3 copy.55
  138.9 1.6 collective-permute-start.2
  141.0 3.3 copy.57
  144.6 1.2 dynamic-slice_bitcast_fusion
  146.0 1.1 copy_bitcast_fusion.3.a_ref
  147.1 9.8 %fusion.12 = (f32[4096,64]{1,0:T(8,128)S(1)}, f32[4096,64]{1,0:T(8,128)}, f32[4096,64]{1,0:T(8,128)S(1)}) fusion(f32[64]{0:T(128)S(1)} %multiply_power_fusion, f32[4096]{0:T(1024)S(1)} %iota.23), kind=kLoop, calls=%fused_computation.35 | loop fusion | flops 524288 | bytes 3162368 | tf_op jit(solution)/shard_map/neg | solution.py:680
  156.9 75.0 %collective-permute-done.2.x2 = bf16[1024,2048]{1,0:T(8,128)(2,1)} collective-permute-done((bf16[1024,2048]{1,0:T(8,128)(2,1)}, bf16[1024,2048]{1,0:T(8,128)(2,1)}, u32[]{:S(2)}, u32[]{:S(2)}) %collective-permute-start.2) | collective-permute-done | bytes 4194336 | tf_op jit(solution)/shard_map/ppermute | solution.py:675
  231.9 1.9 pad_maximum_fusion.1.cos_ref
  233.8 1.0 copy-done.9
  234.8 8.0 %maximum_select_fusion = bf16[4,4,128,2048]{3,2,1,0:T(8,128)(2,1)} fusion(bf16[4,2,128,2048]{3,2,1,0:T(8,128)(2,1)} %collective-permute-done, bf16[4,2,128,2048]{3,2,1,0:T(8,128)(2,1)S(1)} %bitcast.111, pred[]{:T(512)S(6)} %eq.16), kind=kLoop, calls=%fused_computation | loop fusion | flops 12582912 | bytes 16777216 | tf_op jit(solution)/shard_map/jit(_where)/select_n | solution.py:648
  242.8 23.3 %post.1 = (bf16[1024,2048]{1,0:T(8,128)(2,1)}, bf16[1024,2048]{1,0:T(8,128)(2,1)}, bf16[4,1024,128]{2,1,0:T(8,128)(2,1)}, f32[1,2048]{1,0:T(1,128)}) custom-call(bf16[4,1024,512]{2,1,0:T(8,128)(2,1)} %all-gather.6.cloned.1.call-done.o_ref, bf16[4,512,2048]{2,1,0:T(8,128)(2,1)} %bitcast.105, bf16[512,2048]{1,0:T(8,128)(2,1)} %bitcast.135, ...), custom_call_target="tpu_custom_call" | custom-call | flops 10737418240 | bytes 16777216 | tf_op jit(solution)/shard_map/post/pallas_call | solution.py:304
  266.1 19.0 %exchange_product.1 = (bf16[4,1024,128]{2,1,0:T(8,128)(2,1)}, f32[512,2048]{1,0:T(8,128)}) custom-call(bf16[4,1024,128]{2,1,0:T(8,128)(2,1)} %get-tuple-element.48.in_ref, bf16[1024,512]{1,0:T(8,128)(2,1)} %copy_bitcast_fusion.3.a_ref, bf16[1024,2048]{1,0:T(8,128)(2,1)} %get-tuple-element.49.b_ref), custom_call_target="tpu_custom_call" | custom-call | tf_op jit(solution)/shard_map/exchange_product/pallas_call | solution.py:101
  285.7 1.1 pad_maximum_fusion.5.wqk_ref
  286.8 1.9 pad_maximum_fusion.2.sin_ref
  288.7 43.3 %attend_back.1 = (f32[4096,128]{1,0:T(8,128)}, f32[4096,128]{1,0:T(8,128)}, bf16[4096,128]{1,0:T(8,128)(2,1)}) custom-call(bf16[4096,128]{1,0:T(8,128)(2,1)} %bitcast.150, bf16[4096,128]{1,0:T(8,128)(2,1)} %bitcast.152, bf16[4096,128]{1,0:T(8,128)(2,1)} %bitcast.154, bf16[4096,128]{1,0:T(8,128)(2,1)} %get-tuple-element.42.o_ref, ...), custom_call_target="tpu_custom_call" | custom-call | flops 10737418240 | bytes 10485760 | tf_op jit(solution)/shard_map/attend_back/pallas_call | solution.py:261
  332.0 78.4 %weights_back.1 = (f32[2048,128]{1,0:T(8,128)}, f32[2048,128]{1,0:T(8,128)}, f32[2048,128]{1,0:T(8,128)}, bf16[4,1024,128]{2,1,0:T(8,128)(2,1)}, bf16[4,1024,128...) custom-call(bf16[1024,2048]{1,0:T(8,128)(2,1)} %bitcast.122, ...), custom_call_target="tpu_custom_call" | custom-call | tf_op jit(solution)/shard_map/weights_back/pallas_call | solution.py:609
  410.5 3.7 pad_maximum_fusion
  414.2 1.6 copy-done.5
  415.8 2.5 copy.59
  418.3 4.4 copy.60
  422.8 2.6 copy.61
  426.0 5.4 small_sum_7.1
  431.4 167.1 %chain_sum.1 = bf16[1024,2048]{1,0:T(8,128)(2,1)} custom-call(bf16[4,1024,128]{2,1,0:T(8,128)(2,1)} %get-tuple-element.60.dq_ref, bf16[4,1024,128]{2,1,0:T(8,128)(2,1)} %get-tuple-element.61.dk_ref, bf16[4,1024,128]{2,1,0:T(8,128)(2,1)} %get-tuple-element.62.dv_ref, bf16[512,2048]{1,0:T(8,128)(2,1)} %bitcast.124, bf16[512,2048]{1,0:T(8,128)(2,1)} %bitcast.125, ...), custom_call_target="tpu_custom_call" | custom-call | flops 99999997952 | bytes 33554432 | tf_op jit(solution)/shard_map/chain_sum/pallas_call | solution.py:450
  599.7 8.9 %fusion.16 = (f32[4,1,2048,128]{3,2,1,0:T(8,128)}, f32[4,1,2048,128]{3,2,1,0:T(8,128)}, f32[4,1,2048,128]{3,2,1,0:T(8,128)S(1)}) fusion(f32[4,3,2048,128]{3,2,1,0:T(8,128)} %bitcast.103), kind=kLoop, calls=%fused_computation.52 | loop fusion | bytes 25165824 | tf_op jit(solution)/shard_map/slice | solution.py:703
  608.6 7.4 %copy.94 = f32[4,1,2048,128]{3,0,2,1:T(4,128)} copy(f32[4,1,2048,128]{3,2,1,0:T(8,128)} %get-tuple-element.69) | data formatting | bytes 8388608
  616.0 10.0 %copy.95 = f32[4,1,2048,128]{3,0,2,1:T(4,128)} copy(f32[4,1,2048,128]{3,2,1,0:T(8,128)S(1)} %copy-done) | data formatting | bytes 8388608
  626.0 10.2 %copy.96 = f32[4,1,2048,128]{3,0,2,1:T(4,128)} copy(f32[4,1,2048,128]{3,2,1,0:T(8,128)S(1)} %get-tuple-element.71) | data formatting | bytes 8388608
  636.2 2.1 copy.100
  638.3 1.6 copy-done.10
  639.9 2.0 copy.101
  (70 shorter events, 5.3 us)
Async XLA Ops:
  7.2 2.6 copy-start.3
  7.2 133.3 %all-gather.8.cloned.1.call-start = ((), (), s32[]{:S(2)}) async-start(), calls=%async_computation.2 | async-start | bytes 5242880 | tf_op jit(solution)/shard_map/all_gather | solution.py:646
  9.7 233.1 %all-gather.6.cloned.1.call-start = ((), (), s32[]{:S(2)}) async-start(), calls=%async_computation | async-start | bytes 5242880 | tf_op jit(solution)/shard_map/all_gather | solution.py:685
  9.8 6.1 copy-start.6
  9.8 6.0 copy-start.12
  43.4 3.2 copy-start.7
  43.4 3.2 copy-start.17
  46.6 1.6 copy-start.8
  46.6 1.6 copy-start.16
  138.9 460.9 %all-reduce.2.cloned.1.call-start = ((), (), s32[]{:S(2)}) async-start(), calls=%async_computation.1 | async-start | bytes 8388608 | tf_op jit(solution)/shard_map/psum | solution.py:688
  138.9 92.9 %collective-permute-start.2 = (bf16[1024,2048]{1,0:T(8,128)(2,1)}, bf16[1024,2048]{1,0:T(8,128)(2,1)}, u32[]{:S(2)}, u32[]{:S(2)}) collective-permute-start(bf16[1024,2048]{1,0:T(8,128)(2,1)} %bitcast.119), channel_id=1, source_target_pairs={{0,2},{1,3},{2,0},{3,1},{4,6},{5,7},{6,4},{7,5},{8,10},{9,11},{10,... | collective-permute-start | bytes 12582920 | tf_op jit(solution)/shard_map/ppermute | solution.py:675
  140.5 93.3 %collective-permute-start = (bf16[4,2,128,2048]{3,2,1,0:T(8,128)(2,1)}, bf16[4,2,128,2048]{3,2,1,0:T(8,128)(2,1)}, u32[]{:S(2)}, u32[]{:S(2)}) collective-permute-start(bf16[4,2,128,2048]{3,2,1,0:T(8,128)(2,1)} %bitcast.110), channel_id=1, source_target_pairs={{0,1},{1,0},{2,3},{3,2},{4,5},{5,4},{6,7},{7,6},{8,9},{9,8},{10,11... | collective-permute-start | bytes 12582920 | tf_op jit(solution)/shard_map/ppermute | solution.py:647
  140.6 191.4 %collective-permute-start.1 = (bf16[1024,2048]{1,0:T(8,128)(2,1)}, bf16[1024,2048]{1,0:T(8,128)(2,1)}, u32[]{:S(2)}, u32[]{:S(2)}) collective-permute-start(bf16[1024,2048]{1,0:T(8,128)(2,1)} %bitcast.120), channel_id=1, source_target_pairs={{0,1},{1,0},{2,3},{3,2},{4,5},{5,4},{6,7},{7,6},{8,9},{9,8},{10,11... | collective-permute-start | bytes 12582920 | tf_op jit(solution)/shard_map/ppermute | solution.py:676
  141.0 3.3 copy-start.4
  144.6 1.4 copy-start.1
  231.9 100.2 %collective-permute-start.3 = (bf16[1024,2048]{1,0:T(8,128)(2,1)}, bf16[1024,2048]{1,0:T(8,128)(2,1)}, u32[]{:S(2)}, u32[]{:S(2)}) collective-permute-start(bf16[1024,2048]{1,0:T(8,128)(2,1)} %collective-permute-done.2.x2), channel_id=1, source_target_pairs={{0,1},{1,0},{2,3},{3,2},{4,5},{5,4},{6,7},{7,6},{8,9},{9,8},{10,11... | collective-permute-start | bytes 12582920 | tf_op jit(solution)/shard_map/ppermute | solution.py:677
  231.9 2.9 copy-start.9
  285.1 314.6 %all-gather.10.cloned.1.call-start = ((), (), s32[]{:S(2)}) async-start(), calls=%async_computation.3 | async-start | bytes 15728640 | tf_op jit(solution)/shard_map/all_gather | solution.py:694
  285.1 1.6 copy-start.2
  414.2 1.6 copy-start.5
  418.3 4.4 copy-start.13
  422.7 2.6 copy-start.18
  422.7 2.6 copy-start.19
  422.7 2.7 copy-start.15
  431.4 167.1 %copy-start.14 = (f32[1,3072]{1,0:T(1,128)S(1)}, f32[1,3072]{1,0:T(1,128)}, u32[]{:S(2)}) copy-start(f32[1,3072]{1,0:T(1,128)} %small_sum_7.1) | copy-start | bytes 36868
  608.6 7.4 %copy-start = (f32[4,1,2048,128]{3,2,1,0:T(8,128)S(1)}, f32[4,1,2048,128]{3,2,1,0:T(8,128)}, u32[]{:S(2)}) copy-start(f32[4,1,2048,128]{3,2,1,0:T(8,128)} %get-tuple-element.70) | copy-start | bytes 12582916
  625.9 10.2 %copy-start.11 = (bf16[1024,2048]{1,0:T(8,128)(2,1)S(1)}, bf16[1024,2048]{1,0:T(8,128)(2,1)}, u32[]{:S(2)}) copy-start(bf16[1024,2048]{1,0:T(8,128)(2,1)} %chain_sum.1) | copy-start | bytes 12582916
  636.2 3.7 copy-start.10
Sparse Core Ops, SparseCore 0:
  10.1 83.5 all-gather.7
  139.0 80.8 all-gather.5
  285.2 112.9 all-reduce.1
  414.3 83.3 all-gather.9

commit v4 on v3

--- a/solution.py
+++ b/solution.py
@@ -6,6 +6,7 @@
 from jax.experimental import pallas as pl
 from jax.experimental.pallas import tpu as pltpu
 from jax.sharding import PartitionSpec as P
+
 
 ROPE_THETA = 500000.0
 NORM_EPS = 1e-6
@@ -74,39 +75,125 @@
         copy.wait()
 
 
-def exchange_product_kernel(axis, size, block, in_ref, a_ref, b_ref, out_ref, prod_ref, send_sem, recv_sem):
-    me = lax.axis_index(axis)
-    entry_barrier(axis, size)
-    copies = []
-    for shift in (2, 1, 3) if size == 4 else range(1, size):
-        dst = lax.rem(me + shift, size)
-        copy = pltpu.make_async_remote_copy(
-            src_ref=in_ref.at[dst], dst_ref=out_ref.at[me], send_sem=send_sem.at[shift - 1], recv_sem=recv_sem.at[shift - 1],
-            device_id={axis: dst}, device_id_type=MESH)
-        copy.start()
-        copies.append(copy)
-    out_ref[me] = in_ref[me]
-
-    def step(idx, carry):
-        cols = pl.ds(pl.multiple_of(idx * block, block), block)
-        prod_ref[:, cols] = dot_tn(a_ref[...], b_ref[:, cols])
-        return carry
-
-    lax.fori_loop(0, b_ref.shape[1] // block, step, 0)
-    for copy in copies:
+def peers_barrier():
+    me, my_tp = lax.axis_index("cp"), lax.axis_index("tp")
+    barrier = pltpu.get_barrier_semaphore()
+    for shift in (1, 2, 3):
+        pl.semaphore_signal(barrier, inc=1, device_id={"cp": lax.rem(me + shift, 4)}, device_id_type=MESH)
+        pl.semaphore_signal(barrier, inc=1, device_id={"tp": lax.rem(my_tp + shift, 4)}, device_id_type=MESH)
+    pl.semaphore_wait(barrier, 6)
+
+
+def flip(index, distance):
+    if distance == 1:
+        return index + 1 - 2 * lax.rem(index, 2)
+    if distance == 2:
+        return lax.rem(index + 2, 4)
+    return 3 - index if distance == 3 else index
+
+
+def heads_to_tokens_kernel(in_ref, heads_ref, tokens_ref, cp_send, cp_recv, tp_send, tp_recv):
+    me, my_tp = lax.axis_index("cp"), lax.axis_index("tp")
+    quarter = in_ref.shape[1] // 4
+    peers_barrier()
+    first = {}
+    for dist in (1, 2, 3):
+        peer = flip(me, dist)
+        first[dist] = pltpu.make_async_remote_copy(
+            src_ref=in_ref.at[peer], dst_ref=heads_ref.at[me], send_sem=cp_send.at[dist - 1], recv_sem=cp_recv.at[dist - 1],
+            device_id={"cp": peer}, device_id_type=MESH)
+        first[dist].start()
+
+    def rows_of(which):
+        return pl.ds(pl.multiple_of(which * quarter, quarter), quarter)
+
+    second = []
+
+    def forward(dist, src_ref, head):
+        for shift in (2, 1, 3):
+            peer = lax.rem(my_tp + shift, 4)
+            copy = pltpu.make_async_remote_copy(
+                src_ref=src_ref.at[head, rows_of(peer)], dst_ref=tokens_ref.at[my_tp, head],
+                send_sem=tp_send.at[dist, shift - 1], recv_sem=tp_recv.at[dist, shift - 1],
+                device_id={"tp": peer}, device_id_type=MESH)
+            copy.start()
+            second.append(copy)
+        tokens_ref[my_tp, head] = src_ref[head, rows_of(my_tp)]
+
+    forward(0, in_ref, me)
+    heads_ref[me] = in_ref[me]
+    for dist in (1, 2, 3):
+        first[dist].wait_recv()
+        forward(dist, heads_ref, flip(me, dist))
+    for dist in (1, 2, 3):
+        first[dist].wait_send()
+    for copy in second:
         copy.wait()
 
 
-def exchange_product(axis, size, collective_id, array, a, b):
-    return pl.pallas_call(
-        functools.partial(exchange_product_kernel, axis, size, min(512, b.shape[1])),
-        out_shape=(jax.ShapeDtypeStruct(array.shape, array.dtype), jax.ShapeDtypeStruct((a.shape[1], b.shape[1]), jnp.float32)),
-        in_specs=[VMEM_SPEC] * 3,
+def heads_to_tokens(collective_id, array):
+    _, rows, head_dim = array.shape
+    dma = pltpu.SemaphoreType.DMA
+    return pl.pallas_call(
+        heads_to_tokens_kernel,
+        out_shape=(jax.ShapeDtypeStruct(array.shape, array.dtype), jax.ShapeDtypeStruct((4, 4, rows // 4, head_dim), array.dtype)),
+        in_specs=[VMEM_SPEC],
         out_specs=(VMEM_SPEC, VMEM_SPEC),
-        scratch_shapes=[pltpu.SemaphoreType.DMA((size - 1,)), pltpu.SemaphoreType.DMA((size - 1,))],
+        scratch_shapes=[dma((3,)), dma((3,)), dma((4, 3)), dma((4, 3))],
         compiler_params=pltpu.CompilerParams(collective_id=collective_id, has_side_effects=True, vmem_limit_bytes=VMEM_LIMIT),
-        name="exchange_product",
-    )(array, a, b)
+        name="heads_to_tokens",
+    )(array)
+
+
+def tokens_to_heads_kernel(in_ref, seq_ref, block_ref, tp_send, tp_recv, cp_send, cp_recv):
+    me, my_tp = lax.axis_index("cp"), lax.axis_index("tp")
+    quarter = in_ref.shape[2]
+    peers_barrier()
+    first = {}
+    for shift in (2, 1, 3):
+        peer = lax.rem(my_tp + shift, 4)
+        first[shift] = pltpu.make_async_remote_copy(
+            src_ref=in_ref.at[peer], dst_ref=block_ref.at[my_tp], send_sem=tp_send.at[shift - 1], recv_sem=tp_recv.at[shift - 1],
+            device_id={"tp": peer}, device_id_type=MESH)
+        first[shift].start()
+    second = []
+
+    def forward(shift, src_ref, which):
+        rows = pl.ds(pl.multiple_of(which * quarter, quarter), quarter)
+        for dist in (2, 3, 1):
+            peer = flip(me, dist)
+            copy = pltpu.make_async_remote_copy(
+                src_ref=src_ref.at[which, peer], dst_ref=seq_ref.at[me, rows],
+                send_sem=cp_send.at[shift, dist - 1], recv_sem=cp_recv.at[shift, dist - 1],
+                device_id={"cp": peer}, device_id_type=MESH)
+            second.append(copy)
+            copy.start()
+        seq_ref[me, rows] = src_ref[which, me]
+
+    forward(0, in_ref, my_tp)
+    for shift in (1, 3, 2):
+        first[shift].wait_recv()
+        forward(shift, block_ref, lax.rem(my_tp + 4 - shift, 4))
+    for shift in (1, 2, 3):
+        first[shift].wait_send()
+    for copy in second:
+        copy.wait_send()
+    for copy in second:
+        copy.wait_recv()
+
+
+def tokens_to_heads(collective_id, array):
+    tp, heads, quarter, head_dim = array.shape
+    dma = pltpu.SemaphoreType.DMA
+    return pl.pallas_call(
+        tokens_to_heads_kernel,
+        out_shape=jax.ShapeDtypeStruct((heads, tp * quarter, head_dim), array.dtype),
+        in_specs=[VMEM_SPEC],
+        out_specs=VMEM_SPEC,
+        scratch_shapes=[pltpu.VMEM(array.shape, array.dtype), dma((3,)), dma((3,)), dma((4, 3)), dma((4, 3))],
+        compiler_params=pltpu.CompilerParams(collective_id=collective_id, has_side_effects=True, vmem_limit_bytes=VMEM_LIMIT),
+        name="tokens_to_heads",
+    )(array)
 
 
 def exchange(axis, size, collective_id, *arrays):
@@ -118,7 +205,6 @@
         out_specs=tuple([VMEM_SPEC] * count),
         scratch_shapes=[pltpu.SemaphoreType.DMA((count, size - 1)), pltpu.SemaphoreType.DMA((count, size - 1))],
         compiler_params=pltpu.CompilerParams(collective_id=collective_id, has_side_effects=True, vmem_limit_bytes=VMEM_LIMIT),
-        name="exchange_" + str(collective_id),
     )(*arrays)
 
 
@@ -150,7 +236,6 @@
         out_specs=VMEM_SPEC,
         scratch_shapes=[pltpu.VMEM((size,) + array.shape, array.dtype), pltpu.SemaphoreType.DMA((size - 1,)), pltpu.SemaphoreType.DMA((size - 1,))],
         compiler_params=pltpu.CompilerParams(collective_id=collective_id, has_side_effects=True),
-        name="small_sum_" + str(collective_id),
     )(array)
 
 
@@ -220,6 +305,7 @@
             delta_ref[:, rows] = jnp.sum(prod.T, axis=0, keepdims=True)
             dq_ref[rows, :] = jnp.zeros((block, dq_ref.shape[1]), jnp.float32)
             return carry
+
         lax.fori_loop(0, n_blk, prepare, 0)
 
     k_blk = k_ref[...]
@@ -271,10 +357,12 @@
     )(q, k, v, o, do, lse)
 
 
-def post_kernel(tp_size, o_ref, wo_ref, wown_ref, x_ref, gy_ref, pw_ref, y_ref, gp_ref, do_ref, gpost_ref):
-    proj = dot_nn(o_ref[0], wo_ref[0])
-    for idx in range(1, tp_size):
-        proj = proj + dot_nn(o_ref[idx], wo_ref[idx])
+def post_kernel(o_ref, wo_ref, x_ref, gy_ref, pw_ref, y_ref, gp_ref, do_ref, gpost_ref):
+    tp_size, heads, _, head_dim = o_ref.shape
+    proj = None
+    for idx in range(tp_size):
+        term = dot_nn(jnp.concatenate([o_ref[idx, head] for head in range(heads)], axis=1), wo_ref[idx])
+        proj = term if proj is None else proj + term
     gain = pw_ref[...]
     inv = lax.rsqrt(jnp.mean(proj * proj, axis=-1, keepdims=True) + NORM_EPS)
     hat = proj * inv
@@ -284,10 +372,10 @@
     grad_hat = grad * gain
     grad_proj = (inv * (grad_hat - hat * jnp.mean(grad_hat * hat, axis=-1, keepdims=True))).astype(jnp.bfloat16)
     gp_ref[...] = grad_proj
-    grad_o = dot_nt(grad_proj, wown_ref[...]).astype(jnp.bfloat16)
-    head_dim = do_ref.shape[2]
-    for idx in range(do_ref.shape[0]):
-        do_ref[idx] = grad_o[:, idx * head_dim:(idx + 1) * head_dim]
+    for idx in range(tp_size):
+        grad_o = dot_nt(grad_proj, wo_ref[idx]).astype(jnp.bfloat16)
+        for head in range(heads):
+            do_ref[idx, head] = grad_o[:, head * head_dim:(head + 1) * head_dim]
 
     @pl.when(pl.program_id(0) == 0)
     def _():
@@ -296,23 +384,44 @@
     gpost_ref[...] += gpost
 
 
-def post(o_all, wo_all, w_own, x, gy, gain, heads, head_dim):
-    tp_size, rows, width = o_all.shape
+def post(o_all, wo_all, x, gy, gain):
+    tp_size, heads, rows, head_dim = o_all.shape
     d_model = x.shape[1]
-    block = min(256, rows)
+    block = min(128, rows)
     act = pl.BlockSpec((block, d_model), lambda i: (i, 0))
-    return pl.pallas_call(
-        functools.partial(post_kernel, tp_size),
+    by_head = pl.BlockSpec((tp_size, heads, block, head_dim), lambda i: (0, 0, i, 0))
+    act_shape = jax.ShapeDtypeStruct((rows, d_model), jnp.bfloat16)
+    return pl.pallas_call(
+        post_kernel,
         grid=(rows // block,),
-        out_shape=(jax.ShapeDtypeStruct((rows, d_model), jnp.bfloat16), jax.ShapeDtypeStruct((rows, d_model), jnp.bfloat16),
-                   jax.ShapeDtypeStruct((heads, rows, head_dim), jnp.bfloat16), jax.ShapeDtypeStruct((1, d_model), jnp.float32)),
-        in_specs=[pl.BlockSpec((tp_size, block, width), lambda i: (0, i, 0)), pl.BlockSpec(wo_all.shape, lambda i: (0, 0, 0)),
-                  pl.BlockSpec(w_own.shape, lambda i: (0, 0)), act, act, pl.BlockSpec((1, d_model), lambda i: (0, 0))],
-        out_specs=(act, act, pl.BlockSpec((heads, block, head_dim), lambda i: (0, i, 0)), pl.BlockSpec((1, d_model), lambda i: (0, 0))),
+        out_shape=(act_shape, act_shape, jax.ShapeDtypeStruct(o_all.shape, jnp.bfloat16), jax.ShapeDtypeStruct((1, d_model), jnp.float32)),
+        in_specs=[by_head, pl.BlockSpec(wo_all.shape, lambda i: (0, 0, 0)), act, act, pl.BlockSpec((1, d_model), lambda i: (0, 0))],
+        out_specs=(act, act, by_head, pl.BlockSpec((1, d_model), lambda i: (0, 0))),
         compiler_params=pltpu.CompilerParams(vmem_limit_bytes=VMEM_LIMIT),
-        cost_estimate=pl.CostEstimate(flops=2 * rows * d_model * (d_model + width), bytes_accessed=4 * d_model * d_model, transcendentals=rows),
+        cost_estimate=pl.CostEstimate(flops=4 * rows * d_model * d_model, bytes_accessed=4 * d_model * d_model, transcendentals=rows),
         name="post",
-    )(o_all, wo_all, w_own, x, gy, gain)
+    )(o_all, wo_all, x, gy, gain)
+
+
+def spread_kernel(in_ref, *out_refs):
+    for number, out_ref in enumerate(out_refs):
+        for head in range(in_ref.shape[0]):
+            out_ref[:, head, :] = in_ref[head, number]
+
+
+def spread(gathered):
+    heads, count, d_model, head_dim = gathered.shape
+    block = min(256, d_model)
+    return pl.pallas_call(
+        spread_kernel,
+        grid=(d_model // block,),
+        out_shape=tuple([jax.ShapeDtypeStruct((d_model, heads, head_dim), gathered.dtype)] * count),
+        in_specs=[pl.BlockSpec((heads, count, block, head_dim), lambda i: (0, 0, i, 0))],
+        out_specs=tuple([pl.BlockSpec((block, heads, head_dim), lambda i: (i, 0, 0))] * count),
+        compiler_params=pltpu.CompilerParams(vmem_limit_bytes=VMEM_LIMIT),
+        cost_estimate=pl.CostEstimate(flops=d_model * heads * head_dim * count, bytes_accessed=8 * d_model * heads * head_dim * count, transcendentals=0),
+        name="spread",
+    )(gathered)
 
 
 def chain_kernel(size, n_chunk, lag, tile, dq_ref, dk_ref, dv_ref, wq_ref, wk_ref, wv_ref, gy_ref, out_ref, part_ref, sums_a, sums_b, rs_send, rs_recv, ag_send, ag_recv):
@@ -342,7 +451,7 @@
             device_id={"tp": toward(side)}, device_id_type=MESH)
 
     def ag_copy(side, chunk):
-        local, glob, sums = parts(side, chunk)
+        _, glob, _ = parts(side, chunk)
         return pltpu.make_async_remote_copy(
             src_ref=out_ref.at[glob], dst_ref=out_ref.at[glob],
             send_sem=ag_send.at[side, chunk], recv_sem=ag_recv.at[side, chunk],
@@ -364,6 +473,7 @@
                 def one(idx, carry):
                     rs_copy(side, (number // 2) * per_tile + idx, True).start()
                     return carry
+
                 lax.fori_loop(0, per_tile, one, 0)
 
     def product(number, carry):
@@ -384,6 +494,7 @@
         @pl.when(number > 0)
         def _():
             push(number - 1)
+
         return carry
 
     lax.fori_loop(0, n_tile, product, 0)
@@ -459,31 +570,32 @@
     )(*grads, *weights, gy)
 
 
-def flip(index, distance):
-    if distance == 1:
-        return index + 1 - 2 * lax.rem(index, 2)
-    if distance == 2:
-        return lax.rem(index + 2, 4)
-    return 3 - index if distance == 3 else index
-
-
-def weights_back_kernel(tp_size, full_width, sub, x0, x1, x2, x3, wqk_ref, dq_ref, dk_ref, dv_ref, cos_ref, sin_ref, qg_ref, kg_ref,
-                        dwq_ref, dwk_ref, dwv_ref, exq_ref, exk_ref, exv_ref, gq_ref, gk_ref,
-                        x_buf, lin_ref, q16_ref, k16_ref, own, slots_tp, mid, slots_cp, total, x_sem, tp_send, tp_recv, cp_send, cp_recv, ex_send, ex_recv):
+def weights_back_kernel(tp_size, full_width, sub, x_ref, far_ref, wq_ref, wk_ref, dq_ref, dk_ref, dv_ref, cos_ref, sin_ref, qg_ref, kg_ref, post_ref, o_ref, gp_ref,
+                        dw_ref, exq_ref, exk_ref, exv_ref, gains_ref, post_out, dwo_ref,
+                        x_buf, wqk_ref, gp_buf, lin_ref, q16_ref, k16_ref, own, slots_tp, mid, slots_cp, total, gq_ref, gk_ref, my_gains,
+                        x_sem, w_sem, pair_send, pair_recv, tp_send, tp_recv, cp_send, cp_recv, ex_send, ex_recv):
     me = lax.axis_index("cp")
     my_tp = lax.axis_index("tp")
     rows, head_dim = dq_ref.shape[1:]
     loads = []
-    for dist, x_ref in enumerate((x0, x1, x2, x3)):
-        load = pltpu.make_async_copy(x_ref, x_buf.at[dist], x_sem.at[dist])
+    for idx, (src, dist) in enumerate(((x_ref, 0), (far_ref, 2))):
+        load = pltpu.make_async_copy(src, x_buf.at[dist], x_sem.at[idx])
         load.start()
         loads.append(load)
-    barrier = pltpu.get_barrier_semaphore()
-    for dist in (1, 2, 3):
-        pl.semaphore_signal(barrier, inc=1, device_id={"cp": flip(me, dist)}, device_id_type=MESH)
-    for shift in range(1, tp_size):
-        pl.semaphore_signal(barrier, inc=1, device_id={"tp": lax.rem(my_tp + shift, tp_size)}, device_id_type=MESH)
-    pl.semaphore_wait(barrier, 3 + tp_size - 1)
+    own_rows = pl.ds(pl.multiple_of(me * head_dim, head_dim), head_dim)
+    w_loads = [pltpu.make_async_copy(src.at[own_rows], wqk_ref.at[pl.ds(idx * head_dim, head_dim)], w_sem.at[idx]) for idx, src in enumerate((wq_ref, wk_ref))]
+    w_loads.append(pltpu.make_async_copy(gp_ref, gp_buf, w_sem.at[2]))
+    for load in w_loads:
+        load.start()
+    peers_barrier()
+    for idx, (src, dist) in enumerate(((x_ref, 1), (far_ref, 3))):
+        load = pltpu.make_async_remote_copy(
+            src_ref=src, dst_ref=x_buf.at[dist], send_sem=pair_send.at[idx], recv_sem=pair_recv.at[idx],
+            device_id={"cp": flip(me, 1)}, device_id_type=MESH)
+        load.start()
+        loads.append(load)
+    own[4:5, :] = jnp.zeros_like(own[4:5, :])
+    own[4:5, 0:post_ref.shape[1]] = post_ref[...]
 
     def ex_copy(idx, src, dst, dist):
         peer = flip(me, dist)
@@ -501,15 +613,20 @@
         turned = jnp.concatenate([g[:, half_dim:], g[:, :half_dim]], axis=1)
         return g * cos_ref[table, :] - turned * sin_ref[table, :]
 
+    w_loads[0].wait()
+    w_loads[1].wait()
     sides = ((dq_ref, qg_ref, 0), (dk_ref, kg_ref, 1))
-    for dist in range(4):
+    for order, dist in enumerate((0, 2, 1, 3)):
         blk = flip(me, dist)
-        loads[dist].wait()
+        if order < 2:
+            loads[order].wait()
+        else:
+            loads[order].wait_recv()
 
         def first(idx, carry, dist=dist, blk=blk):
             part = pl.ds(pl.multiple_of(idx * sub, sub), sub)
             table = pl.ds(pl.multiple_of(blk * rows + idx * sub, sub), sub)
-            lin = dot_nn(x_buf[dist, part, :], wqk_ref[...])
+            lin = dot_nt(x_buf[dist, part, :], wqk_ref[...])
             lin_ref[dist, part, :] = lin
             for ref, gain_ref, number in sides:
                 mine = lin[:, number * head_dim:(number + 1) * head_dim]
@@ -546,6 +663,7 @@
         move.wait()
     total[...] = slots_cp[0] + slots_cp[1] + slots_cp[2] + slots_cp[3]
 
+    post_out[...] = total[4:5, 0:post_ref.shape[1]]
     gq_ref[...] = jnp.zeros_like(gq_ref)
     gk_ref[...] = jnp.zeros_like(gk_ref)
     outs = ((q16_ref, exq_ref, gq_ref), (k16_ref, exk_ref, gk_ref))
@@ -574,8 +692,17 @@
                 copy = ex_copy(idx, d16_ref, ex_ref, dist)
                 copy.start()
                 copies.append(copy)
+    my_gains[0:1, :] = gq_ref[...]
+    my_gains[1:2, :] = gk_ref[...]
     for src, dst in ((q16_ref, exq_ref), (k16_ref, exk_ref), (dv_ref, exv_ref)):
         dst[me] = src[me]
+    gains_ref[me] = my_gains[...]
+    for dist in (1, 2, 3):
+        copy = pltpu.make_async_remote_copy(
+            src_ref=my_gains, dst_ref=gains_ref.at[me], send_sem=ex_send.at[3, dist - 1], recv_sem=ex_recv.at[3, dist - 1],
+            device_id={"cp": flip(me, dist)}, device_id_type=MESH)
+        copy.start()
+        copies.append(copy)
 
     block = min(512, x_buf.shape[2])
 
@@ -588,36 +715,52 @@
             term = dot_tn(grads, x_buf[dist, :, cols])
             acc = term if acc is None else acc + term
         acc = acc.T
-        for number, out in enumerate((dwq_ref, dwk_ref, dwv_ref)):
-            out[cols, :] = acc[:, number * head_dim:(number + 1) * head_dim]
+        for number in range(3):
+            dw_ref[number, cols, :] = acc[:, number * head_dim:(number + 1) * head_dim]
         return carry
 
     lax.fori_loop(0, x_buf.shape[2] // block, weight_step, 0)
+    w_loads[2].wait()
+
+    def output_step(idx, carry):
+        cols = pl.ds(pl.multiple_of(idx * block, block), block)
+        grads = jnp.concatenate([o_ref[head] for head in range(o_ref.shape[0])], axis=1)
+        acc = dot_tn(grads, gp_buf[:, cols])
+        for head in range(o_ref.shape[0]):
+            dwo_ref[head, :, cols] = acc[head * head_dim:(head + 1) * head_dim, :]
+        return carry
+
+    lax.fori_loop(0, x_buf.shape[2] // block, output_step, 0)
     for copy in copies:
         copy.wait()
-
-
-def weights_back(tp_size, collective_id, full_width, xs, wqk, dq, dk, dv, cos_tab, sin_tab, q_gain, k_gain):
+    loads[2].wait_send()
+    loads[3].wait_send()
+
+
+def weights_back(tp_size, collective_id, full_width, x, x_far, wq, wk, dq, dk, dv, cos_tab, sin_tab, q_gain, k_gain, grad_post, o_heads, grad_proj):
     _, rows, head_dim = dq.shape
-    d_model = xs[0].shape[1]
+    d_model = x.shape[1]
     any_spec = pl.BlockSpec(memory_space=pl.ANY)
     dma = pltpu.SemaphoreType.DMA
-    stat = pltpu.VMEM((4, 4 * rows), jnp.float32)
-    dw = jax.ShapeDtypeStruct((d_model, head_dim), jnp.float32)
+    span = max(4 * rows, d_model)
+    stat = pltpu.VMEM((5, span), jnp.float32)
+    slots = pltpu.VMEM((4, 5, span), jnp.float32)
     ex = jax.ShapeDtypeStruct(dq.shape, jnp.bfloat16)
-    gain = jax.ShapeDtypeStruct((1, head_dim), jnp.float32)
-    return pl.pallas_call(
-        functools.partial(weights_back_kernel, tp_size, full_width, min(256, rows)),
-        out_shape=(dw, dw, dw, ex, ex, ex, gain, gain),
-        in_specs=[any_spec] * 4 + [VMEM_SPEC] * 8,
-        out_specs=tuple([VMEM_SPEC] * 8),
-        scratch_shapes=[pltpu.VMEM((4, rows, d_model), jnp.bfloat16), pltpu.VMEM((4, rows, 2 * head_dim), jnp.float32),
+    return pl.pallas_call(
+        functools.partial(weights_back_kernel, tp_size, full_width, min(512, rows)),
+        out_shape=(jax.ShapeDtypeStruct((3, d_model, head_dim), jnp.float32), ex, ex, ex,
+                   jax.ShapeDtypeStruct((4, 2, head_dim), jnp.float32), jax.ShapeDtypeStruct((1, d_model), jnp.float32),
+                   jax.ShapeDtypeStruct((o_heads.shape[0], head_dim, d_model), jnp.float32)),
+        in_specs=[any_spec] * 4 + [VMEM_SPEC] * 9 + [any_spec],
+        out_specs=tuple([VMEM_SPEC] * 7),
+        scratch_shapes=[pltpu.VMEM((4, rows, d_model), jnp.bfloat16), pltpu.VMEM((2 * head_dim, d_model), jnp.bfloat16), pltpu.VMEM((rows, d_model), jnp.bfloat16), pltpu.VMEM((4, rows, 2 * head_dim), jnp.float32),
                         pltpu.VMEM(dq.shape, jnp.bfloat16), pltpu.VMEM(dq.shape, jnp.bfloat16),
-                        stat, pltpu.VMEM((tp_size, 4, 4 * rows), jnp.float32), stat, pltpu.VMEM((4, 4, 4 * rows), jnp.float32), stat,
-                        dma((4,)), dma((tp_size - 1,)), dma((tp_size - 1,)), dma((3,)), dma((3,)), dma((3, 3)), dma((3, 3))],
+                        stat, slots, stat, slots, stat,
+                        pltpu.VMEM((1, head_dim), jnp.float32), pltpu.VMEM((1, head_dim), jnp.float32), pltpu.VMEM((2, head_dim), jnp.float32),
+                        dma((2,)), dma((3,)), dma((2,)), dma((2,)), dma((tp_size - 1,)), dma((tp_size - 1,)), dma((3,)), dma((3,)), dma((4, 3)), dma((4, 3))],
         compiler_params=pltpu.CompilerParams(collective_id=collective_id, has_side_effects=True, vmem_limit_bytes=VMEM_LIMIT),
         name="weights_back",
-    )(*xs, wqk, dq, dk, dv, cos_tab, sin_tab, q_gain, k_gain)
+    )(x, x_far, wq, wk, dq, dk, dv, cos_tab, sin_tab, q_gain, k_gain, grad_post, o_heads, grad_proj)
 
 
 def solution(mesh):
@@ -667,40 +810,36 @@
 
         seq_shape = (cp_size * rows, head_dim)
         block_shape = (cp_size, rows, head_dim)
-        q_seq, k_seq, v_seq = (t.reshape(seq_shape) for t in exchange("cp", cp_size, 1, q_rot, k_rot, v_val))
+        q_seq, k_seq, v_seq = exchange("cp", cp_size, 1, q_rot, k_rot, v_val)
+        q_seq, x_send = lax.optimization_barrier((q_seq, x))
+        x_far = lax.ppermute(x_send, "cp", [(dev, dev ^ 2) for dev in range(cp_size)])
+        q_seq, k_seq, v_seq = (t.reshape(seq_shape) for t in (q_seq, k_seq, v_seq))
         o_seq, lse = attend(q_seq, k_seq, v_seq)
-        (o_heads,) = exchange("cp", cp_size, 2, o_seq.reshape(block_shape))
-        positions = jnp.arange(cp_size * rows, dtype=jnp.float32)
-        o_heads, x_send, positions, w_q2, w_k2, w_v2 = lax.optimization_barrier((o_heads, x, positions, w_q, w_k, w_v))
-        x_far = lax.ppermute(x_send, "cp", [(dev, dev ^ 2) for dev in range(cp_size)])
-        x_near = lax.ppermute(x_send, "cp", swap_core)
-        x_cross = lax.ppermute(x_far, "cp", swap_core)
-        seq_cos, seq_sin = rope_tables(positions, head_dim)
+        o_heads, o_tokens = heads_to_tokens(2, o_seq.reshape(block_shape))
+        quarter = rows // tp_size
+        first_row = lax.axis_index("tp") * quarter
+        x_mine, gy_mine = (lax.dynamic_slice_in_dim(t, first_row, quarter, axis=0) for t in (x, gy))
+        y_mine, gp_mine, do_tokens, grad_post = post(o_tokens, wo_all, x_mine, gy_mine, post_norm_w[None, :])
+        do_seq = tokens_to_heads(3, do_tokens)
+        grad_proj = lax.all_gather(gp_mine, "tp", tiled=True)
+        y_mine, do_seq = lax.optimization_barrier((y_mine, do_seq))
+        y_out = lax.all_gather(y_mine, "tp", tiled=True)
+
+        coarse_cos, coarse_sin = (t[:, None, :] for t in rope_tables(jnp.arange(0, cp_size * rows, 64, dtype=jnp.float32), head_dim))
+        fine_cos, fine_sin = (t[None, :, :] for t in rope_tables(jnp.arange(64, dtype=jnp.float32), head_dim))
+        seq_cos = (coarse_cos * fine_cos - coarse_sin * fine_sin).reshape(cp_size * rows, head_dim // 2)
+        seq_sin = (coarse_sin * fine_cos + coarse_cos * fine_sin).reshape(cp_size * rows, head_dim // 2)
         seq_cos = jnp.concatenate([seq_cos, seq_cos], axis=1)
         seq_sin = jnp.concatenate([-seq_sin, seq_sin], axis=1)
-        turned = tuple(w.reshape(d_model, width).T for w in (w_q2, w_k2, w_v2))
-        wqk_head = jnp.concatenate([lax.dynamic_slice_in_dim(w, cp_index, 1, axis=1)[:, 0, :] for w in (w_q2, w_k2)], axis=1)
+        turned = tuple(w.reshape(d_model, width).T for w in (w_q, w_k, w_v))
         gains_head = tuple(lax.dynamic_slice_in_dim(w, cp_index, 1, axis=0) for w in (q_norm_w, k_norm_w))
-        o_mine = o_heads.transpose(1, 0, 2).reshape(rows, width)
-        o_all = lax.all_gather(o_mine, "tp")
-        y_out, grad_proj, grad_o, grad_post = post(o_all, wo_all, w_o.reshape(width, d_model), x, gy, post_norm_w[None, :], heads, head_dim)
-        do_seq, dwo_part = exchange_product("cp", cp_size, 3, grad_o, o_mine, grad_proj)
-        grad_w_o = lax.psum(dwo_part, "cp")
-
         dq_seq, dk_seq, dv_seq = attend_back(q_seq, k_seq, v_seq, o_seq, do_seq.reshape(seq_shape), lse)
-        *dw, dq16, dk16, dv16, gain_q, gain_k = weights_back(
-            tp_size, 4, full_width, (x, x_near, x_far, x_cross), wqk_head,
-            dq_seq.reshape(block_shape), dk_seq.reshape(block_shape), dv_seq.reshape(block_shape), seq_cos, seq_sin, *gains_head)
-        dw = lax.all_gather(jnp.stack(dw), "cp")
-        own_head = jnp.arange(heads)[:, None] == cp_index
-        small = jnp.concatenate([jnp.where(own_head, gain, 0.0).reshape(1, width) for gain in (gain_q, gain_k)] + [grad_post], axis=1)
-        small = small_sum("cp", cp_size, 7, small)
-        dq16, small = lax.optimization_barrier((dq16, small))
+        dw, dq16, dk16, dv16, gains, grad_post, grad_w_o = weights_back(
+            tp_size, 4, full_width, x, x_far, turned[0], turned[1],
+            dq_seq.reshape(block_shape), dk_seq.reshape(block_shape), dv_seq.reshape(block_shape), seq_cos, seq_sin, *gains_head, grad_post, o_heads, grad_proj)
+        grad_w_o = lax.psum(grad_w_o, "cp")
+        dw = spread(lax.all_gather(dw, "cp"))
         grad_x = chain_sum(tp_size, 6, (dq16, dk16, dv16), turned, gy)
-        grad_q_norm = small[0, :width].reshape(heads, head_dim)
-        grad_k_norm = small[0, width:2 * width].reshape(heads, head_dim)
-        grad_post = small[0, 2 * width:]
-        dw = tuple(dw[:, number].transpose(1, 0, 2) for number in range(3))
-        return (y_out[None], grad_x[None]) + dw + (grad_w_o.reshape(heads, head_dim, d_model), grad_q_norm, grad_k_norm, grad_post)
+        return (y_out[None], grad_x[None]) + tuple(dw) + (grad_w_o, gains[:, 0], gains[:, 1], grad_post[0])
 
     return jax.shard_map(local_run, mesh=mesh, in_specs=in_specs, out_specs=out_specs, check_vma=False)

time: 653 us -> 675 us (1.034)
  Pallas kernels: 430 us -> 479 us
  local copies, waits for them, and re-layouts: 74 us -> 37 us
  waiting for transfers between devices: 75 us -> 104 us
  other arithmetic: 38.1 us -> 23.3 us
    all_gather x1, waiting for transfers between devices: 0.01 us -> 56 us  [local_run(): mine = lax.all_gather(own_half, 'tp')]
    pallas_call x2 -> x4, Pallas kernels: 42.3 us -> 97.5 us  [the longest x1 41 us: tokens_to_heads(): pl.pallas_call(tokens_to_heads_kernel, out_shape=jax.ShapeDtypeStruct((he...]
    ppermute x1, waiting for transfers between devices: 75 us -> 45.4 us  [local_run(): lax.ppermute(x_send, 'cp', [(dev, dev ^ 2) for dev in range(cp_size)])]
    pallas_call x2 -> x1, Pallas kernels: 56.1 us -> 39.9 us  [exchange(): pl.pallas_call(functools.partial(exchange_kernel, axis, size, count), out...]
    pallas_call x1, Pallas kernels: 78.4 us -> 93.3 us  [weights_back(): pl.pallas_call(functools.partial(weights_back_kernel, tp_size, full_width...]
    optimization_barrier x5 -> x0, local copies, waits for them, and re-layouts: 13.1 us -> none  [local_run(): lax.optimization_barrier((o_heads, x, positions, w_q, w_k, w_v))]
    unnamed x45 -> x37, local copies, waits for them, and re-layouts: 37.5 us -> 26.6 us
    neg x1, other arithmetic: 9.77 us -> 0.14 us  [local_run(): seq_sin = jnp.concatenate([-seq_sin, seq_sin], axis=1)]
  transfers between devices with their start and end apart: 8 -> 7, of which waited for: 1 -> 3; matrix products, arithmetic and copies ran while one was open for 12% -> 7% of each run, Pallas kernels for 66% -> 67%
where the time goes in v4:
time: 675 us; the launch traced here: 674 us
  Pallas kernels  479 us (71%)
  waiting for transfers between devices  104 us (15%)
  local copies, waits for them, and re-layouts  37 us (5%)
  other arithmetic  23.3 us (3%)
  matrix products  14.5 us (2%)
  between operations  14.1 us (2%)
    pallas_call x1, Pallas kernels, chain_sum(): pl.pallas_call(functools.partial(chain_kernel, size, n_chunk, 2, min(256,...  168 us
    pallas_call x1, Pallas kernels, weights_back(): pl.pallas_call(functools.partial(weights_back_kernel, tp_size, full_width...  93.3 us
    all_gather x1, waiting for transfers between devices, local_run(): mine = lax.all_gather(own_half, 'tp')  56 us
    ppermute x1, waiting for transfers between devices, local_run(): lax.ppermute(x_send, 'cp', [(dev, dev ^ 2) for dev in range(cp_size)])  45.4 us
    pallas_call x1, Pallas kernels, attend_back(): pl.pallas_call(functools.partial(attend_back_kernel, block, head_dim ** (...  43.2 us
    pallas_call x1, Pallas kernels, tokens_to_heads(): pl.pallas_call(tokens_to_heads_kernel, out_shape=jax.ShapeDtypeStruct((he...  41 us
    pallas_call x1, Pallas kernels, exchange(): pl.pallas_call(functools.partial(exchange_kernel, axis, size, count), out...  39.9 us
    pallas_call x1, Pallas kernels, heads_to_tokens(): pl.pallas_call(heads_to_tokens_kernel, out_shape=(jax.ShapeDtypeStruct(ar...  28.3 us
  transfers between devices with their start and end apart: 7, of which 3 were waited for; matrix products, arithmetic and copies ran while one was open for 7% of the time, Pallas kernels for 67%

profile of v4, /device:TPU:0, one launch (start us, length us, event | category | flops | bytes accessed | tf_op | source)
XLA Modules:
  0.0 673.7 jit_solution(8369330216457060629)
XLA Ops:
  7.3 1.5 copy-done
  8.8 1.1 constant_dynamic-slice_fusion.2
  9.9 3.0 copy.27
  12.9 4.7 copy.28
  17.6 6.2 multiply_reduce_fusion.1
  23.8 3.7 multiply_reduce_fusion
  27.6 0.6 pad_maximum_fusion.4.in_ref
  28.2 10.1 %shard_map.160 = f32[2,1024]{1,0:T(2,128)} custom-call(f32[2,1024]{1,0:T(2,128)} %pad_maximum_fusion.4.in_ref), custom_call_target="tpu_custom_call" | custom-call | tf_op jit(solution)/shard_map/pallas_call | solution.py:232
  38.3 56.0 %all-gather.11.cloned.1.call-done = bf16[8,128,2048]{2,1,0:T(8,128)(2,1)} async-done(((bf16[2,128,2048]{2,1,0:T(8,128)(2,1)}), bf16[8,128,2048]{2,1,0:T(8,128)(2,1)}) %all-gather.11.cloned.1.call-update) | async-done | bytes 4194320 | tf_op jit(solution)/shard_map/all_gather | solution.py:789
  94.3 0.7 add_rsqrt_fusion
  95.0 1.9 broadcast_multiply_fusion.1
  97.0 1.8 copy.29
  98.8 1.9 broadcast_multiply_fusion
  100.7 1.8 copy.30
  102.5 3.0 copy.31
  105.5 1.3 copy-done.10
  106.8 4.5 convolution_convert_fusion
  111.4 1.3 copy.32
  112.7 1.9 multiply_cosine_fusion
  114.8 1.4 copy-done.5
  116.4 1.4 subtract_convert_fusion
  117.8 2.5 pad_maximum_fusion.2
  120.3 39.9 %shard_map.161 = (bf16[4,1024,128]{2,1,0:T(8,128)(2,1)}, bf16[4,1024,128]{2,1,0:T(8,128)(2,1)}, bf16[4,1024,128]{2,1,0:T(8,128)(2,1)}) custom-call(bf16[4,1024,128]{2,1,0:T(8,128)(2,1)} %get-tuple-element.87.refs_0_, bf16[4,1024,128]{2,1,0:T(8,128)(2,1)} %get-tuple-element.88.refs_1_, bf16[4,1024,128]{2,1,0:T(8,128)(2,1)} %bitcast.76), custom_call_target="tpu_custom_call" | custom-call | tf_op jit(solution)/shard_map/pallas_call | solution.py:201
  160.2 27.6 %attend.1 = (bf16[4096,128]{1,0:T(8,128)(2,1)}, f32[1,4096]{1,0:T(1,128)}) custom-call(bf16[4096,128]{1,0:T(8,128)(2,1)} %bitcast.95, bf16[4096,128]{1,0:T(8,128)(2,1)} %bitcast.97, bf16[4096,128]{1,0:T(8,128)(2,1)} %bitcast.99), custom_call_target="tpu_custom_call" | custom-call | flops 4294967296 | bytes 4194304 | tf_op jit(solution)/shard_map/attend/pallas_call | solution.py:283
  187.8 28.3 %heads_to_tokens.1 = (bf16[4,1024,128]{2,1,0:T(8,128)(2,1)}, bf16[4,4,256,128]{3,2,1,0:T(8,128)(2,1)}) custom-call(bf16[4,1024,128]{2,1,0:T(8,128)(2,1)} %bitcast.84), custom_call_target="tpu_custom_call" | custom-call | tf_op jit(solution)/shard_map/heads_to_tokens/pallas_call | solution.py:137
  216.2 3.3 dynamic-slice_bitcast_fusion
  219.4 8.0 %maximum_select_fusion = bf16[4,4,128,2048]{3,2,1,0:T(8,128)(2,1)} fusion(bf16[4,2,128,2048]{3,2,1,0:T(8,128)(2,1)} %collective-permute-done, bf16[4,2,128,2048]{3,2,1,0:T(8,128)(2,1)S(1)} %bitcast.75, pred[]{:T(512)S(6)} %eq.5), kind=kLoop, calls=%fused_computation | loop fusion | flops 12582912 | bytes 16777216 | tf_op jit(solution)/shard_map/jit(_where)/select_n | solution.py:791
  227.4 14.5 %post.1 = (bf16[256,2048]{1,0:T(8,128)(2,1)}, bf16[256,2048]{1,0:T(8,128)(2,1)}, bf16[4,4,256,128]{3,2,1,0:T(8,128)(2,1)}, f32[1,2048]{1,0:T(1,128)}) custom-call(bf16[4,4,256,128]{3,2,1,0:T(8,128)(2,1)} %get-tuple-element.42.o_ref, bf16[4,512,2048]{2,1,0:T(8,128)(2,1)} %bitcast.62, bf16[256,2048]{1,0:T(8,128)(2,1)} %get-tuple-element.90.x_ref, ...), custom_call_target="tpu_custom_call" | custom-call | flops 4294967296 | bytes 16777216 | tf_op jit(solution)/shard_map/post/pallas_call | solution.py:394
  242.0 41.0 %tokens_to_heads.1 = bf16[4,1024,128]{2,1,0:T(8,128)(2,1)} custom-call(bf16[4,4,256,128]{3,2,1,0:T(8,128)(2,1)} %get-tuple-element.44.in_ref), custom_call_target="tpu_custom_call" | custom-call | tf_op jit(solution)/shard_map/tokens_to_heads/pallas_call | solution.py:188
  283.3 0.6 collective-permute-start.1
  283.9 0.5 constant_dynamic-slice_fusion
  284.7 0.4 multiply_add_fusion
  285.3 3.2 pad_maximum_fusion
  288.5 43.2 %attend_back.1 = (f32[4096,128]{1,0:T(8,128)}, f32[4096,128]{1,0:T(8,128)}, bf16[4096,128]{1,0:T(8,128)(2,1)}) custom-call(bf16[4096,128]{1,0:T(8,128)(2,1)} %bitcast.96, bf16[4096,128]{1,0:T(8,128)(2,1)} %bitcast.98, bf16[4096,128]{1,0:T(8,128)(2,1)} %bitcast.100, bf16[4096,128]{1,0:T(8,128)(2,1)} %get-tuple-element.41.o_ref, bf16[4096,128]{1,0:T(8,128)(2,1)} %bitcast.85, ...), custom_call_target="tpu_custom_call" | custom-call | flops 10737418240 | bytes 10485760 | tf_op jit(solution)/shard_map/attend_back/pallas_call | solution.py:347
  331.7 45.4 %collective-permute-done.1.far_ref = bf16[1024,2048]{1,0:T(8,128)(2,1)} collective-permute-done((bf16[1024,2048]{1,0:T(8,128)(2,1)}, bf16[1024,2048]{1,0:T(8,128)(2,1)}, u32[]{:S(2)}, u32[]{:S(2)}) %collective-permute-start.1) | collective-permute-done | bytes 4194336 | tf_op jit(solution)/shard_map/ppermute | solution.py:815
  377.1 93.3 %weights_back.1 = (f32[3,2048,128]{2,1,0:T(8,128)}, bf16[4,1024,128]{2,1,0:T(8,128)(2,1)}, bf16[4,1024,128]{2,1,0:T(8,128)(2,1)}, bf16[4,1024,128]{2,1,0:T(8,128...) custom-call(bf16[1024,2048]{1,0:T(8,128)(2,1)} %bitcast.73, ...), custom_call_target="tpu_custom_call" | custom-call | tf_op jit(solution)/shard_map/weights_back/pallas_call | solution.py:749
  470.4 0.3 all-gather.13.cloned.1.call-start
  470.8 0.3 all-gather.13.cloned.1.call-update
  471.0 167.8 %chain_sum.1 = bf16[1024,2048]{1,0:T(8,128)(2,1)} custom-call(bf16[4,1024,128]{2,1,0:T(8,128)(2,1)} %get-tuple-element.55.dq_ref, bf16[4,1024,128]{2,1,0:T(8,128)(2,1)} %get-tuple-element.56.dk_ref, bf16[4,1024,128]{2,1,0:T(8,128)(2,1)} %get-tuple-element.57.dv_ref, bf16[512,2048]{1,0:T(8,128)(2,1)} %bitcast.65, bf16[512,2048]{1,0:T(8,128)(2,1)} %bitcast.67, ...), custom_call_target="tpu_custom_call" | custom-call | flops 99999997952 | bytes 33554432 | tf_op jit(solution)/shard_map/chain_sum/pallas_call | solution.py:561
  638.9 0.6 fusion.8
  639.5 2.3 all-gather.13.cloned.1.call-done
  641.7 13.6 %spread.1 = (f32[2048,4,128]{2,1,0:T(4,128)}, f32[2048,4,128]{2,1,0:T(4,128)}, f32[2048,4,128]{2,1,0:T(4,128)}) custom-call(f32[4,3,2048,128]{3,2,1,0:T(8,128)} %bitcast.61), custom_call_target="tpu_custom_call" | custom-call | flops 3145728 | bytes 25165824 | tf_op jit(solution)/shard_map/spread/pallas_call | solution.py:415
  655.4 4.9 copy.38
  660.3 2.1 copy.39
  662.4 1.6 copy-done.8
  664.0 2.1 copy.40
  666.2 0.6 copy.41
  666.8 0.4 copy-done.1
  (46 shorter events, 1.3 us)
Async XLA Ops:
  7.2 1.6 copy-start
  7.2 87.1 %all-gather.11.cloned.1.call-start = ((), (), s32[]{:S(2)}) async-start(), calls=%async_computation.3 | async-start | bytes 5242880 | tf_op jit(solution)/shard_map/all_gather | solution.py:789
  9.9 367.2 %all-gather.9.cloned.1.call-start = ((), (), s32[]{:S(2)}) async-start(), calls=%async_computation.1 | async-start | bytes 5242880 | tf_op jit(solution)/shard_map/all_gather | solution.py:824
  12.9 4.7 copy-start.2
  17.6 6.3 copy-start.3
  17.6 6.3 copy-start.6
  94.3 125.1 %collective-permute-start = (bf16[4,2,128,2048]{3,2,1,0:T(8,128)(2,1)}, bf16[4,2,128,2048]{3,2,1,0:T(8,128)(2,1)}, u32[]{:S(2)}, u32[]{:S(2)}) collective-permute-start(bf16[4,2,128,2048]{3,2,1,0:T(8,128)(2,1)} %bitcast.74), channel_id=1, source_target_pairs={{0,1},{1,0},{2,3},{3,2},{4,5},{5,4},{6,7},{7,6},{8,9},{9,8},{10,11... | collective-permute-start | bytes 12582920 | tf_op jit(solution)/shard_map/ppermute | solution.py:790
  105.5 1.3 copy-start.10
  111.4 3.2 copy-start.4
  111.4 3.2 copy-start.14
  114.6 1.6 copy-start.5
  114.7 1.6 copy-start.13
  216.1 3.3 copy-start.7
  241.9 396.9 %all-gather.7.cloned.1.call-start = ((), (), s32[]{:S(2)}) async-start(), calls=%async_computation | async-start | bytes 5242880 | tf_op jit(solution)/shard_map/all_gather | solution.py:826
  283.0 356.4 %all-reduce.2.cloned.1.call-start = ((), (), s32[]{:S(2)}) async-start(), calls=%async_computation.2 | async-start | bytes 8388608 | tf_op jit(solution)/shard_map/psum | solution.py:840
  283.3 93.8 %collective-permute-start.1 = (bf16[1024,2048]{1,0:T(8,128)(2,1)}, bf16[1024,2048]{1,0:T(8,128)(2,1)}, u32[]{:S(2)}, u32[]{:S(2)}) collective-permute-start(bf16[1024,2048]{1,0:T(8,128)(2,1)} %bitcast.72), channel_id=1, source_target_pairs={{0,2},{1,3},{2,0},{3,1},{4,6},{5,7},{6,4},{7,5},{8,10},{9,11},{10,... | collective-permute-start | bytes 12582920 | tf_op jit(solution)/shard_map/ppermute | solution.py:815
  470.4 171.3 %all-gather.13.cloned.1.call-start = ((), (), s32[]{:S(2)}) async-start(), calls=%async_computation.4 | async-start | bytes 15728640 | tf_op jit(solution)/shard_map/all_gather | solution.py:841
  471.0 167.8 %copy-start.12 = (f32[4,2,128]{2,1,0:T(2,128)S(1)}, f32[4,2,128]{2,1,0:T(2,128)}, u32[]{:S(2)}) copy-start(f32[4,2,128]{2,1,0:T(2,128)} %get-tuple-element.63) | copy-start | bytes 12292
  655.4 4.9 copy-start.9
  660.3 3.7 copy-start.8
  664.0 2.1 copy-start.11
  664.0 3.1 copy-start.1
Sparse Core Ops, SparseCore 0:
  10.1 84.1 all-gather.10
  242.1 95.3 all-gather.8
  339.0 79.7 all-gather.6
  470.6 87.4 all-reduce.1
  559.5 82.2 all-gather.12

commit v5 on v4

--- a/solution.py
+++ b/solution.py
@@ -38,41 +38,12 @@
     return jnp.cos(angles), jnp.sin(angles)
 
 
-def rope(values, cos_tab, sin_tab):
-    half_dim = values.shape[-1] // 2
-    low_half = values[..., :half_dim]
-    high_half = values[..., half_dim:]
-    return jnp.concatenate([low_half * cos_tab - high_half * sin_tab, high_half * cos_tab + low_half * sin_tab], axis=-1)
-
-
 def entry_barrier(axis, size):
     me = lax.axis_index(axis)
     barrier = pltpu.get_barrier_semaphore()
     for shift in range(1, size):
         pl.semaphore_signal(barrier, inc=1, device_id={axis: lax.rem(me + shift, size)}, device_id_type=MESH)
     pl.semaphore_wait(barrier, size - 1)
-
-
-def exchange_kernel(axis, size, count, *refs):
-    ins = refs[:count]
-    outs = refs[count:2 * count]
-    send_sem, recv_sem = refs[2 * count:]
-    me = lax.axis_index(axis)
-    entry_barrier(axis, size)
-    copies = []
-    for idx in range(count):
-        for shift in (2, 1, 3) if size == 4 else range(1, size):
-            dst = lax.rem(me + shift, size)
-            copy = pltpu.make_async_remote_copy(
-                src_ref=ins[idx].at[dst], dst_ref=outs[idx].at[me],
-                send_sem=send_sem.at[idx, shift - 1], recv_sem=recv_sem.at[idx, shift - 1],
-                device_id={axis: dst}, device_id_type=MESH)
-            copy.start()
-            copies.append(copy)
-    for idx in range(count):
-        outs[idx][me] = ins[idx][me]
-    for copy in copies:
-        copy.wait()
 
 
 def peers_barrier():
@@ -196,47 +167,96 @@
     )(array)
 
 
-def exchange(axis, size, collective_id, *arrays):
-    count = len(arrays)
-    return pl.pallas_call(
-        functools.partial(exchange_kernel, axis, size, count),
-        out_shape=tuple(jax.ShapeDtypeStruct(a.shape, a.dtype) for a in arrays),
-        in_specs=[VMEM_SPEC] * count,
-        out_specs=tuple([VMEM_SPEC] * count),
-        scratch_shapes=[pltpu.SemaphoreType.DMA((count, size - 1)), pltpu.SemaphoreType.DMA((count, size - 1))],
-        compiler_params=pltpu.CompilerParams(collective_id=collective_id, has_side_effects=True, vmem_limit_bytes=VMEM_LIMIT),
-    )(*arrays)
-
-
-def sum_kernel(axis, size, in_ref, out_ref, slots, send_sem, recv_sem):
-    me = lax.axis_index(axis)
-    entry_barrier(axis, size)
+def turn(values):
+    half_dim = values.shape[1] // 2
+    return jnp.concatenate([values[:, half_dim:], values[:, :half_dim]], axis=1)
+
+
+def front_kernel(full_width, sub, x_ref, wq_ref, wk_ref, wv_ref, cos_ref, sin_ref, qg_ref, kg_ref, q_out, k_out, v_out,
+                 q_buf, k_buf, v_buf, lin_ref, own, slots, total, tp_send, tp_recv, ex_send, ex_recv):
+    me, my_tp = lax.axis_index("cp"), lax.axis_index("tp")
+    rows = x_ref.shape[0]
+    heads, head_dim = qg_ref.shape
+    peers_barrier()
     copies = []
-    for shift in range(1, size):
-        copy = pltpu.make_async_remote_copy(
-            src_ref=in_ref, dst_ref=slots.at[me],
-            send_sem=send_sem.at[shift - 1], recv_sem=recv_sem.at[shift - 1],
-            device_id={axis: lax.rem(me + shift, size)}, device_id_type=MESH)
-        copy.start()
-        copies.append(copy)
-    slots[me] = in_ref[...]
+
+    def send(idx, src, dst):
+        for dist in (2, 3, 1):
+            peer = flip(me, dist)
+            copy = pltpu.make_async_remote_copy(
+                src_ref=src.at[peer], dst_ref=dst.at[me], send_sem=ex_send.at[idx, dist - 1], recv_sem=ex_recv.at[idx, dist - 1],
+                device_id={"cp": peer}, device_id_type=MESH)
+            copy.start()
+            copies.append(copy)
+        dst[me] = src[me]
+
+    def part_of(idx):
+        return pl.ds(pl.multiple_of(idx * sub, sub), sub)
+
+    def values(idx, carry):
+        part = part_of(idx)
+        out = dot_nt(x_ref[part, :], wv_ref[...]).astype(jnp.bfloat16)
+        for head in range(heads):
+            v_buf[head, part, :] = out[:, head * head_dim:(head + 1) * head_dim]
+        return carry
+
+    lax.fori_loop(0, rows // sub, values, 0)
+    send(2, v_buf, v_out)
+
+    def linear(idx, carry):
+        part = part_of(idx)
+        for number, w_ref in enumerate((wq_ref, wk_ref)):
+            out = dot_nt(x_ref[part, :], w_ref[...])
+            lin_ref[number, part, :] = out
+            square = out * out
+            square = sum(square[:, head * head_dim:(head + 1) * head_dim] for head in range(heads))
+            own[number:number + 1, part] = jnp.sum(square.T, axis=0, keepdims=True)
+        return carry
+
+    lax.fori_loop(0, rows // sub, linear, 0)
+    moves = []
+    for shift in (1, 2, 3):
+        move = pltpu.make_async_remote_copy(
+            src_ref=own, dst_ref=slots.at[my_tp], send_sem=tp_send.at[shift - 1], recv_sem=tp_recv.at[shift - 1],
+            device_id={"tp": lax.rem(my_tp + shift, 4)}, device_id_type=MESH)
+        move.start()
+        moves.append(move)
+    slots[my_tp] = own[...]
+    for move in moves:
+        move.wait()
+    total[...] = lax.rsqrt((slots[0] + slots[1] + slots[2] + slots[3]) / full_width + NORM_EPS)
+
+    for number, (gain_ref, buf, out_ref) in enumerate(((qg_ref, q_buf, q_out), (kg_ref, k_buf, k_out))):
+        def rotate(idx, carry, number=number, gain_ref=gain_ref, buf=buf):
+            part = part_of(idx)
+            inv = jnp.broadcast_to(total[number:number + 1, part], (head_dim, sub)).T
+            for head in range(heads):
+                scaled = lin_ref[number, part, head * head_dim:(head + 1) * head_dim] * inv * gain_ref[head:head + 1, :]
+                buf[head, part, :] = (scaled * cos_ref[part, :] + turn(scaled) * sin_ref[part, :]).astype(jnp.bfloat16)
+            return carry
+
+        lax.fori_loop(0, rows // sub, rotate, 0)
+        send(number, buf, out_ref)
     for copy in copies:
         copy.wait()
-    total = slots[0]
-    for idx in range(1, size):
-        total = total + slots[idx]
-    out_ref[...] = total
-
-
-def small_sum(axis, size, collective_id, array):
+
+
+def front(collective_id, full_width, x, weights, cos_tab, sin_tab, q_gain, k_gain):
+    rows, _ = x.shape
+    heads, head_dim = q_gain.shape
+    dma = pltpu.SemaphoreType.DMA
+    block = (heads, rows, head_dim)
+    stat = pltpu.VMEM((2, rows), jnp.float32)
     return pl.pallas_call(
-        functools.partial(sum_kernel, axis, size),
-        out_shape=jax.ShapeDtypeStruct(array.shape, array.dtype),
-        in_specs=[VMEM_SPEC],
-        out_specs=VMEM_SPEC,
-        scratch_shapes=[pltpu.VMEM((size,) + array.shape, array.dtype), pltpu.SemaphoreType.DMA((size - 1,)), pltpu.SemaphoreType.DMA((size - 1,))],
-        compiler_params=pltpu.CompilerParams(collective_id=collective_id, has_side_effects=True),
-    )(array)
+        functools.partial(front_kernel, full_width, min(256, rows)),
+        out_shape=tuple([jax.ShapeDtypeStruct(block, jnp.bfloat16)] * 3),
+        in_specs=[VMEM_SPEC] * 8,
+        out_specs=tuple([VMEM_SPEC] * 3),
+        scratch_shapes=[pltpu.VMEM(block, jnp.bfloat16)] * 3 + [pltpu.VMEM((2, rows, heads * head_dim), jnp.float32),
+                        stat, pltpu.VMEM((4, 2, rows), jnp.float32), stat, dma((3,)), dma((3,)), dma((3, 3)), dma((3, 3))],
+        compiler_params=pltpu.CompilerParams(collective_id=collective_id, has_side_effects=True, vmem_limit_bytes=VMEM_LIMIT),
+        name="front",
+    )(x, *weights, cos_tab, sin_tab, q_gain, k_gain)
 
 
 def causal_mask(scores):
@@ -357,12 +377,15 @@
     )(q, k, v, o, do, lse)
 
 
-def post_kernel(o_ref, wo_ref, x_ref, gy_ref, pw_ref, y_ref, gp_ref, do_ref, gpost_ref):
+def post_kernel(o_ref, mine_ref, other_ref, x_ref, gy_ref, pw_ref, y_ref, gp_ref, do_ref, gpost_ref):
     tp_size, heads, _, head_dim = o_ref.shape
+    core = lax.rem(lax.axis_index("cp"), 2)
+    halves = ((mine_ref, core * (heads // 2)), (other_ref, (1 - core) * (heads // 2)))
     proj = None
     for idx in range(tp_size):
-        term = dot_nn(jnp.concatenate([o_ref[idx, head] for head in range(heads)], axis=1), wo_ref[idx])
-        proj = term if proj is None else proj + term
+        for w_ref, start in halves:
+            term = dot_nn(jnp.concatenate([o_ref[idx, start + head] for head in range(heads // 2)], axis=1), w_ref[idx])
+            proj = term if proj is None else proj + term
     gain = pw_ref[...]
     inv = lax.rsqrt(jnp.mean(proj * proj, axis=-1, keepdims=True) + NORM_EPS)
     hat = proj * inv
@@ -373,9 +396,10 @@
     grad_proj = (inv * (grad_hat - hat * jnp.mean(grad_hat * hat, axis=-1, keepdims=True))).astype(jnp.bfloat16)
     gp_ref[...] = grad_proj
     for idx in range(tp_size):
-        grad_o = dot_nt(grad_proj, wo_ref[idx]).astype(jnp.bfloat16)
-        for head in range(heads):
-            do_ref[idx, head] = grad_o[:, head * head_dim:(head + 1) * head_dim]
+        for w_ref, start in halves:
+            grad_o = dot_nt(grad_proj, w_ref[idx]).astype(jnp.bfloat16)
+            for head in range(heads // 2):
+                do_ref[idx, start + head] = grad_o[:, head * head_dim:(head + 1) * head_dim]
 
     @pl.when(pl.program_id(0) == 0)
     def _():
@@ -384,7 +408,7 @@
     gpost_ref[...] += gpost
 
 
-def post(o_all, wo_all, x, gy, gain):
+def post(o_all, wo_mine, wo_other, x, gy, gain):
     tp_size, heads, rows, head_dim = o_all.shape
     d_model = x.shape[1]
     block = min(128, rows)
@@ -395,12 +419,12 @@
         post_kernel,
         grid=(rows // block,),
         out_shape=(act_shape, act_shape, jax.ShapeDtypeStruct(o_all.shape, jnp.bfloat16), jax.ShapeDtypeStruct((1, d_model), jnp.float32)),
-        in_specs=[by_head, pl.BlockSpec(wo_all.shape, lambda i: (0, 0, 0)), act, act, pl.BlockSpec((1, d_model), lambda i: (0, 0))],
+        in_specs=[by_head] + [pl.BlockSpec(wo_mine.shape, lambda i: (0, 0, 0))] * 2 + [act, act, pl.BlockSpec((1, d_model), lambda i: (0, 0))],
         out_specs=(act, act, by_head, pl.BlockSpec((1, d_model), lambda i: (0, 0))),
         compiler_params=pltpu.CompilerParams(vmem_limit_bytes=VMEM_LIMIT),
         cost_estimate=pl.CostEstimate(flops=4 * rows * d_model * d_model, bytes_accessed=4 * d_model * d_model, transcendentals=rows),
         name="post",
-    )(o_all, wo_all, x, gy, gain)
+    )(o_all, wo_mine, wo_other, x, gy, gain)
 
 
 def spread_kernel(in_ref, *out_refs):
@@ -570,7 +594,7 @@
     )(*grads, *weights, gy)
 
 
-def weights_back_kernel(tp_size, full_width, sub, x_ref, far_ref, wq_ref, wk_ref, dq_ref, dk_ref, dv_ref, cos_ref, sin_ref, qg_ref, kg_ref, post_ref, o_ref, gp_ref,
+def weights_back_kernel(tp_size, full_width, sub, x_ref, far0_ref, far1_ref, far2_ref, wq_ref, wk_ref, dq_ref, dk_ref, dv_ref, cos_ref, sin_ref, qg_ref, kg_ref, post_ref, o_ref, gp_ref,
                         dw_ref, exq_ref, exk_ref, exv_ref, gains_ref, post_out, dwo_ref,
                         x_buf, wqk_ref, gp_buf, lin_ref, q16_ref, k16_ref, own, slots_tp, mid, slots_cp, total, gq_ref, gk_ref, my_gains,
                         x_sem, w_sem, pair_send, pair_recv, tp_send, tp_recv, cp_send, cp_recv, ex_send, ex_recv):
@@ -578,8 +602,11 @@
     my_tp = lax.axis_index("tp")
     rows, head_dim = dq_ref.shape[1:]
     loads = []
-    for idx, (src, dist) in enumerate(((x_ref, 0), (far_ref, 2))):
-        load = pltpu.make_async_copy(src, x_buf.at[dist], x_sem.at[idx])
+    step = far0_ref.shape[0]
+    fars = ((far0_ref, pl.ds(0, step)), (far1_ref, pl.ds(step, step)), (far2_ref, pl.ds(2 * step, rows - 2 * step)))
+    pieces = ((x_ref, 0, pl.ds(0, rows)),) + tuple((ref, 2, part) for ref, part in fars)
+    for idx, (src, dist, part) in enumerate(pieces):
+        load = pltpu.make_async_copy(src, x_buf.at[dist, part], x_sem.at[idx])
         load.start()
         loads.append(load)
     own_rows = pl.ds(pl.multiple_of(me * head_dim, head_dim), head_dim)
@@ -588,9 +615,9 @@
     for load in w_loads:
         load.start()
     peers_barrier()
-    for idx, (src, dist) in enumerate(((x_ref, 1), (far_ref, 3))):
+    for idx, (src, dist, part) in enumerate(pieces):
         load = pltpu.make_async_remote_copy(
-            src_ref=src, dst_ref=x_buf.at[dist], send_sem=pair_send.at[idx], recv_sem=pair_recv.at[idx],
+            src_ref=src, dst_ref=x_buf.at[dist + 1, part], send_sem=pair_send.at[idx], recv_sem=pair_recv.at[idx],
             device_id={"cp": flip(me, 1)}, device_id_type=MESH)
         load.start()
         loads.append(load)
@@ -609,19 +636,18 @@
 
     def grad_of(ref, blk, part, table):
         g = ref[blk, part, :]
-        half_dim = head_dim // 2
-        turned = jnp.concatenate([g[:, half_dim:], g[:, :half_dim]], axis=1)
-        return g * cos_ref[table, :] - turned * sin_ref[table, :]
+        return g * cos_ref[table, :] - turn(g) * sin_ref[table, :]
 
     w_loads[0].wait()
     w_loads[1].wait()
     sides = ((dq_ref, qg_ref, 0), (dk_ref, kg_ref, 1))
     for order, dist in enumerate((0, 2, 1, 3)):
         blk = flip(me, dist)
-        if order < 2:
-            loads[order].wait()
-        else:
-            loads[order].wait_recv()
+        for load in (loads[0:1], loads[1:4], loads[4:5], loads[5:8])[order]:
+            if order < 2:
+                load.wait()
+            else:
+                load.wait_recv()
 
         def first(idx, carry, dist=dist, blk=blk):
             part = pl.ds(pl.multiple_of(idx * sub, sub), sub)
@@ -733,8 +759,8 @@
     lax.fori_loop(0, x_buf.shape[2] // block, output_step, 0)
     for copy in copies:
         copy.wait()
-    loads[2].wait_send()
-    loads[3].wait_send()
+    for load in loads[4:]:
+        load.wait_send()
 
 
 def weights_back(tp_size, collective_id, full_width, x, x_far, wq, wk, dq, dk, dv, cos_tab, sin_tab, q_gain, k_gain, grad_post, o_heads, grad_proj):
@@ -751,16 +777,16 @@
         out_shape=(jax.ShapeDtypeStruct((3, d_model, head_dim), jnp.float32), ex, ex, ex,
                    jax.ShapeDtypeStruct((4, 2, head_dim), jnp.float32), jax.ShapeDtypeStruct((1, d_model), jnp.float32),
                    jax.ShapeDtypeStruct((o_heads.shape[0], head_dim, d_model), jnp.float32)),
-        in_specs=[any_spec] * 4 + [VMEM_SPEC] * 9 + [any_spec],
+        in_specs=[any_spec] * 6 + [VMEM_SPEC] * 9 + [any_spec],
         out_specs=tuple([VMEM_SPEC] * 7),
         scratch_shapes=[pltpu.VMEM((4, rows, d_model), jnp.bfloat16), pltpu.VMEM((2 * head_dim, d_model), jnp.bfloat16), pltpu.VMEM((rows, d_model), jnp.bfloat16), pltpu.VMEM((4, rows, 2 * head_dim), jnp.float32),
                         pltpu.VMEM(dq.shape, jnp.bfloat16), pltpu.VMEM(dq.shape, jnp.bfloat16),
                         stat, slots, stat, slots, stat,
                         pltpu.VMEM((1, head_dim), jnp.float32), pltpu.VMEM((1, head_dim), jnp.float32), pltpu.VMEM((2, head_dim), jnp.float32),
-                        dma((2,)), dma((3,)), dma((2,)), dma((2,)), dma((tp_size - 1,)), dma((tp_size - 1,)), dma((3,)), dma((3,)), dma((4, 3)), dma((4, 3))],
+                        dma((4,)), dma((3,)), dma((4,)), dma((4,)), dma((tp_size - 1,)), dma((tp_size - 1,)), dma((3,)), dma((3,)), dma((4, 3)), dma((4, 3))],
         compiler_params=pltpu.CompilerParams(collective_id=collective_id, has_side_effects=True, vmem_limit_bytes=VMEM_LIMIT),
         name="weights_back",
-    )(x, x_far, wq, wk, dq, dk, dv, cos_tab, sin_tab, q_gain, k_gain, grad_post, o_heads, grad_proj)
+    )(x, *x_far, wq, wk, dq, dk, dv, cos_tab, sin_tab, q_gain, k_gain, grad_post, o_heads, grad_proj)
 
 
 def solution(mesh):
@@ -781,61 +807,52 @@
         x = x_in[0]
         gy = grad_y[0]
         cp_index = lax.axis_index("cp")
-        cos_tab, sin_tab = rope_tables((cp_index * rows + jnp.arange(rows)).astype(jnp.float32), head_dim)
-        wq, wk, wv = (w.reshape(d_model, width) for w in (w_q, w_k, w_v))
+
+        def wide_tables(cos_tab, sin_tab):
+            return jnp.concatenate([cos_tab, cos_tab], axis=1), jnp.concatenate([-sin_tab, sin_tab], axis=1)
+
+        cos_tab, sin_tab = wide_tables(*rope_tables((cp_index * rows + jnp.arange(rows)).astype(jnp.float32), head_dim))
+        turned = tuple(w.reshape(d_model, width).T for w in (w_q, w_k, w_v))
 
         core = cp_index % 2
         own_half = lax.dynamic_slice_in_dim(w_o, core * (heads // 2), heads // 2, axis=0)
-        mine = lax.all_gather(own_half, "tp")
-        other = lax.ppermute(mine, "cp", swap_core)
-        wo_all = jnp.where(core == 0, jnp.concatenate([mine, other], axis=1), jnp.concatenate([other, mine], axis=1))
-        wo_all = wo_all.reshape(tp_size, width, d_model)
-
-        def by_head(t):
-            return t.reshape(rows, heads, head_dim).transpose(1, 0, 2)
-
-        q_lin = jnp.dot(x, wq, preferred_element_type=jnp.float32)
-        k_lin = jnp.dot(x, wk, preferred_element_type=jnp.float32)
-        v_lin = jnp.dot(x, wv, preferred_element_type=jnp.float32)
-        squares = jnp.stack([jnp.sum(q_lin * q_lin, axis=1), jnp.sum(k_lin * k_lin, axis=1)])
-        squares = small_sum("tp", tp_size, 0, squares)
-        invs = lax.rsqrt(squares / full_width + NORM_EPS)[:, :, None]
-        q_hat = by_head(q_lin * invs[0])
-        k_hat = by_head(k_lin * invs[1])
-        q_gain = q_norm_w[:, None, :]
-        k_gain = k_norm_w[:, None, :]
-        q_rot = rope(q_hat * q_gain, cos_tab, sin_tab).astype(jnp.bfloat16)
-        k_rot = rope(k_hat * k_gain, cos_tab, sin_tab).astype(jnp.bfloat16)
-        v_val = by_head(v_lin.astype(jnp.bfloat16))
-
+        wo_mine = lax.all_gather(own_half, "tp").reshape(tp_size, width // 2, d_model)
+        q_seq, k_seq, v_seq = front(1, full_width, x, turned, cos_tab, sin_tab, q_norm_w, k_norm_w)
         seq_shape = (cp_size * rows, head_dim)
         block_shape = (cp_size, rows, head_dim)
-        q_seq, k_seq, v_seq = exchange("cp", cp_size, 1, q_rot, k_rot, v_val)
-        q_seq, x_send = lax.optimization_barrier((q_seq, x))
-        x_far = lax.ppermute(x_send, "cp", [(dev, dev ^ 2) for dev in range(cp_size)])
+        piece = rows // 4
+
+        def fetch(start, size):
+            return lax.ppermute(x_free[start:start + size], "cp", [(dev, dev ^ 2) for dev in range(cp_size)])
+
+        q_seq, x_free = lax.optimization_barrier((q_seq, x))
+        far0 = fetch(0, piece)
         q_seq, k_seq, v_seq = (t.reshape(seq_shape) for t in (q_seq, k_seq, v_seq))
         o_seq, lse = attend(q_seq, k_seq, v_seq)
+        o_seq, wo_mine = lax.optimization_barrier((o_seq, wo_mine))
+        wo_other = lax.ppermute(wo_mine, "cp", swap_core)
         o_heads, o_tokens = heads_to_tokens(2, o_seq.reshape(block_shape))
+        o_tokens, x_free = lax.optimization_barrier((o_tokens, x))
+        far1 = fetch(piece, piece)
         quarter = rows // tp_size
         first_row = lax.axis_index("tp") * quarter
         x_mine, gy_mine = (lax.dynamic_slice_in_dim(t, first_row, quarter, axis=0) for t in (x, gy))
-        y_mine, gp_mine, do_tokens, grad_post = post(o_tokens, wo_all, x_mine, gy_mine, post_norm_w[None, :])
+        y_mine, gp_mine, do_tokens, grad_post = post(o_tokens, wo_mine, wo_other, x_mine, gy_mine, post_norm_w[None, :])
         do_seq = tokens_to_heads(3, do_tokens)
         grad_proj = lax.all_gather(gp_mine, "tp", tiled=True)
-        y_mine, do_seq = lax.optimization_barrier((y_mine, do_seq))
+        y_mine, do_seq, x_free = lax.optimization_barrier((y_mine, do_seq, x))
+        far2 = fetch(2 * piece, rows - 2 * piece)
         y_out = lax.all_gather(y_mine, "tp", tiled=True)
 
         coarse_cos, coarse_sin = (t[:, None, :] for t in rope_tables(jnp.arange(0, cp_size * rows, 64, dtype=jnp.float32), head_dim))
         fine_cos, fine_sin = (t[None, :, :] for t in rope_tables(jnp.arange(64, dtype=jnp.float32), head_dim))
         seq_cos = (coarse_cos * fine_cos - coarse_sin * fine_sin).reshape(cp_size * rows, head_dim // 2)
         seq_sin = (coarse_sin * fine_cos + coarse_cos * fine_sin).reshape(cp_size * rows, head_dim // 2)
-        seq_cos = jnp.concatenate([seq_cos, seq_cos], axis=1)
-        seq_sin = jnp.concatenate([-seq_sin, seq_sin], axis=1)
-        turned = tuple(w.reshape(d_model, width).T for w in (w_q, w_k, w_v))
+        seq_cos, seq_sin = wide_tables(seq_cos, seq_sin)
         gains_head = tuple(lax.dynamic_slice_in_dim(w, cp_index, 1, axis=0) for w in (q_norm_w, k_norm_w))
         dq_seq, dk_seq, dv_seq = attend_back(q_seq, k_seq, v_seq, o_seq, do_seq.reshape(seq_shape), lse)
         dw, dq16, dk16, dv16, gains, grad_post, grad_w_o = weights_back(
-            tp_size, 4, full_width, x, x_far, turned[0], turned[1],
+            tp_size, 4, full_width, x, (far0, far1, far2), turned[0], turned[1],
             dq_seq.reshape(block_shape), dk_seq.reshape(block_shape), dv_seq.reshape(block_shape), seq_cos, seq_sin, *gains_head, grad_post, o_heads, grad_proj)
         grad_w_o = lax.psum(grad_w_o, "cp")
         dw = spread(lax.all_gather(dw, "cp"))

time: 675 us -> 582 us (0.86)
  waiting for transfers between devices: 104 us -> 33.6 us
  matrix products: 14.5 us -> 0 us
  other arithmetic: 23.3 us -> 13 us
    all_gather x1, waiting for transfers between devices: 56 us -> 0.01 us  [local_run(): lax.all_gather(own_half, 'tp').reshape(tp_size, width // 2, d_model)]
    dot_general x3 -> x0, matrix products: 14.5 us -> none  [the longest x1 6.25 us: local_run(): q_lin = jnp.dot(x, wq, preferred_element_type=jnp.float32)]
    ppermute x2 -> x4, waiting for transfers between devices: 45.4 us -> 31.8 us  [the longest x3 31.8 us: fetch(): lax.ppermute(x_free[start:start + size], 'cp', [(dev, dev ^ 2) for dev in...]
    select_n x1 -> x0, other arithmetic: 7.99 us -> none  [local_run(): jnp.where(core == 0, jnp.concatenate([mine, other], axis=1), jnp.concaten...]
    pallas_call x2 -> x1, Pallas kernels: 50 us -> 49.5 us  [front(): pl.pallas_call(functools.partial(front_kernel, full_width, min(256, rows)...]
    unnamed x37 -> x27, local copies, waits for them, and re-layouts: 26.6 us -> 26.6 us
  transfers between devices with their start and end apart: 7 -> 9, of which waited for: 3 -> 2; matrix products, arithmetic and copies ran while one was open for 7% -> 6% of each run, Pallas kernels for 67% -> 77%
where the time goes in v5:
time: 582 us; the launch traced here: 581 us
  Pallas kernels  478 us (82%)
  local copies, waits for them, and re-layouts  37.7 us (6%)
  waiting for transfers between devices  33.6 us (6%)
  between operations  14 us (2%)
  other arithmetic  13 us (2%)
    pallas_call x1, Pallas kernels, chain_sum(): pl.pallas_call(functools.partial(chain_kernel, size, n_chunk, 2, min(256,...  169 us
    pallas_call x1, Pallas kernels, weights_back(): pl.pallas_call(functools.partial(weights_back_kernel, tp_size, full_width...  92.5 us
    pallas_call x1, Pallas kernels, front(): pl.pallas_call(functools.partial(front_kernel, full_width, min(256, rows)...  49.5 us
    pallas_call x1, Pallas kernels, attend_back(): pl.pallas_call(functools.partial(attend_back_kernel, block, head_dim ** (...  43.2 us
    pallas_call x1, Pallas kernels, tokens_to_heads(): pl.pallas_call(tokens_to_heads_kernel, out_shape=jax.ShapeDtypeStruct((he...  39.7 us
    ppermute x3, waiting for transfers between devices, fetch(): lax.ppermute(x_free[start:start + size], 'cp', [(dev, dev ^ 2) for dev in...  31.8 us
    pallas_call x1, Pallas kernels, heads_to_tokens(): pl.pallas_call(heads_to_tokens_kernel, out_shape=(jax.ShapeDtypeStruct(ar...  28.1 us
    pallas_call x1, Pallas kernels, attend(): pl.pallas_call(functools.partial(attend_kernel, block, head_dim ** (-0.5)...  27.6 us
  transfers between devices with their start and end apart: 9, of which 2 were waited for; matrix products, arithmetic and copies ran while one was open for 6% of the time, Pallas kernels for 77%

profile of v5, /device:TPU:0, one launch (start us, length us, event | category | flops | bytes accessed | tf_op | source)
XLA Modules:
  0.0 580.9 jit_solution(13460669028560515075)
XLA Ops:
  7.2 0.0 all-gather.11.cloned.1.call-start
  7.3 1.5 copy-done
  8.8 1.1 constant_dynamic-slice_fusion.2
  9.9 0.0 all-gather.9.cloned.1.call-start
  9.9 4.4 copy.21
  14.3 2.6 copy.22
  16.9 4.3 copy.23
  21.2 1.9 fusion
  23.1 1.3 pad_maximum_fusion.2
  24.4 49.5 %front.1 = (bf16[4,1024,128]{2,1,0:T(8,128)(2,1)}, bf16[4,1024,128]{2,1,0:T(8,128)(2,1)}, bf16[4,1024,128]{2,1,0:T(8,128)(2,1)}) custom-call(bf16[1024,2048]{1,0:T(8,128)(2,1)} %bitcast.34, bf16[512,2048]{1,0:T(8,128)(2,1)} %bitcast.40, bf16[512,2048]{1,0:T(8,128)(2,1)} %bitcast.43, bf16[512,2048]{1,0:T(8,128)(2,1)} %bitcast.48, ...), custom_call_target="tpu_custom_call" | custom-call | tf_op jit(solution)/shard_map/front/pallas_call | solution.py:250
  74.0 27.6 %attend.1 = (bf16[4096,128]{1,0:T(8,128)(2,1)}, f32[1,4096]{1,0:T(1,128)}) custom-call(bf16[4096,128]{1,0:T(8,128)(2,1)} %bitcast.63, bf16[4096,128]{1,0:T(8,128)(2,1)} %bitcast.65, bf16[4096,128]{1,0:T(8,128)(2,1)} %bitcast.67), custom_call_target="tpu_custom_call" | custom-call | flops 4294967296 | bytes 4194304 | tf_op jit(solution)/shard_map/attend/pallas_call | solution.py:303
  101.6 0.7 collective-permute-start
  102.3 3.1 dynamic-slice_bitcast_fusion
  105.4 28.1 %heads_to_tokens.1 = (bf16[4,1024,128]{2,1,0:T(8,128)(2,1)}, bf16[4,4,256,128]{3,2,1,0:T(8,128)(2,1)}) custom-call(bf16[4,1024,128]{2,1,0:T(8,128)(2,1)} %bitcast.55), custom_call_target="tpu_custom_call" | custom-call | tf_op jit(solution)/shard_map/heads_to_tokens/pallas_call | solution.py:108
  133.5 14.6 %post.1 = (bf16[256,2048]{1,0:T(8,128)(2,1)}, bf16[256,2048]{1,0:T(8,128)(2,1)}, bf16[4,4,256,128]{3,2,1,0:T(8,128)(2,1)}, f32[1,2048]{1,0:T(1,128)}) custom-call(bf16[4,4,256,128]{3,2,1,0:T(8,128)(2,1)} %get-tuple-element.49.o_ref, bf16[4,256,2048]{2,1,0:T(8,128)(2,1)} %bitcast.62, bf16[4,256,2048]{2,1,0:T(8,128)(2,1)} %collective-permute-done.other_ref, ...), custom_call_target="tpu_custom_call" | custom-call | flops 4294967296 | bytes 16777216 | tf_op jit(solution)/shard_map/post/pallas_call | solution.py:418
  148.1 0.0 all-gather.7.cloned.1.call-start
  148.1 39.7 %tokens_to_heads.1 = bf16[4,1024,128]{2,1,0:T(8,128)(2,1)} custom-call(bf16[4,4,256,128]{3,2,1,0:T(8,128)(2,1)} %get-tuple-element.52.in_ref), custom_call_target="tpu_custom_call" | custom-call | tf_op jit(solution)/shard_map/tokens_to_heads/pallas_call | solution.py:159
  187.9 0.0 all-gather.7.cloned.1.call-update
  187.9 0.2 all-reduce.2.cloned.1.call-start
  188.1 2.3 slice.15
  190.4 1.7 collective-permute-start.1
  192.2 0.3 multiply_cosine_fusion.1
  192.5 1.9 multiply_add_fusion
  194.4 1.1 copy-done.2
  195.4 1.5 slice.17
  196.9 0.3 collective-permute-start.3
  197.2 1.5 bitcast_negate_fusion
  198.6 6.1 %pad_maximum_fusion = (f32[4096,128]{1,0:T(8,128)}, f32[4096,128]{1,0:T(8,128)}) fusion(f32[4096,64]{1,0:T(8,128)} %bitcast.47, f32[4096,64]{1,0:T(8,128)S(1)} %bitcast.39, f32[4096,64]{1,0:T(8,128)} %bitcast_negate_fusion), kind=kLoop, calls=%fused_computation | loop fusion | flops 1048576 | bytes 7340032 | tf_op jit(solution)/shard_map/concatenate | solution.py:812
  204.7 1.3 slice.16
  206.1 1.8 collective-permute-start.2
  207.9 1.2 constant_dynamic-slice_fusion
  209.1 43.2 %attend_back.1 = (f32[4096,128]{1,0:T(8,128)}, f32[4096,128]{1,0:T(8,128)}, bf16[4096,128]{1,0:T(8,128)(2,1)}) custom-call(bf16[4096,128]{1,0:T(8,128)(2,1)} %bitcast.64, bf16[4096,128]{1,0:T(8,128)(2,1)} %bitcast.66, bf16[4096,128]{1,0:T(8,128)(2,1)} %bitcast.68, bf16[4096,128]{1,0:T(8,128)(2,1)} %get-tuple-element.47.o_ref, bf16[4096,128]{1,0:T(8,128)(2,1)} %bitcast.56, ...), custom_call_target="tpu_custom_call" | custom-call | flops 10737418240 | bytes 10485760 | tf_op jit(solution)/shard_map/attend_back/pallas_call | solution.py:367
  252.3 31.7 %collective-permute-done.2.far1_ref = bf16[256,2048]{1,0:T(8,128)(2,1)S(1)} collective-permute-done((bf16[256,2048]{1,0:T(8,128)(2,1)S(1)}, bf16[256,2048]{1,0:T(8,128)(2,1)S(1)}, u32[]{:S(2)}, u32[]{:S(2)}) %collective-permute-start.2) | collective-permute-done | bytes 1048608 | tf_op jit(solution)/shard_map/ppermute | solution.py:826
  284.0 1.0 copy-done.7
  285.0 92.5 %weights_back.1 = (f32[3,2048,128]{2,1,0:T(8,128)}, bf16[4,1024,128]{2,1,0:T(8,128)(2,1)}, bf16[4,1024,128]{2,1,0:T(8,128)(2,1)}, bf16[4,1024,128]{2,1,0:T(8,128...) custom-call(bf16[1024,2048]{1,0:T(8,128)(2,1)} %bitcast.37, ...), custom_call_target="tpu_custom_call" | custom-call | tf_op jit(solution)/shard_map/weights_back/pallas_call | solution.py:775
  377.6 0.0 all-gather.13.cloned.1.call-start
  377.6 0.5 all-gather.13.cloned.1.call-update
  378.2 168.9 %chain_sum.1 = bf16[1024,2048]{1,0:T(8,128)(2,1)} custom-call(bf16[4,1024,128]{2,1,0:T(8,128)(2,1)} %get-tuple-element.65.dq_ref, bf16[4,1024,128]{2,1,0:T(8,128)(2,1)} %get-tuple-element.66.dk_ref, bf16[4,1024,128]{2,1,0:T(8,128)(2,1)} %get-tuple-element.67.dv_ref, bf16[512,2048]{1,0:T(8,128)(2,1)} %bitcast.42, bf16[512,2048]{1,0:T(8,128)(2,1)} %bitcast.45, ...), custom_call_target="tpu_custom_call" | custom-call | flops 99999997952 | bytes 33554432 | tf_op jit(solution)/shard_map/chain_sum/pallas_call | solution.py:585
  547.1 0.0 all-gather.7.cloned.1.call-done
  547.2 0.6 fusion.3
  547.7 1.2 all-gather.13.cloned.1.call-done
  548.9 13.6 %spread.1 = (f32[2048,4,128]{2,1,0:T(4,128)}, f32[2048,4,128]{2,1,0:T(4,128)}, f32[2048,4,128]{2,1,0:T(4,128)}) custom-call(f32[4,3,2048,128]{3,2,1,0:T(8,128)} %bitcast.46), custom_call_target="tpu_custom_call" | custom-call | flops 3145728 | bytes 25165824 | tf_op jit(solution)/shard_map/spread/pallas_call | solution.py:439
  562.6 4.9 copy.29
  567.5 2.1 copy.30
  569.7 1.6 copy-done.3
  571.2 2.1 copy.31
  573.4 0.6 copy.32
  574.0 0.4 copy-done.1
  (27 shorter events, 0.1 us)
Async XLA Ops:
  7.2 1.6 copy-start
  7.2 94.4 %all-gather.11.cloned.1.call-start = ((), (), s32[]{:S(2)}) async-start(), calls=%async_computation.3 | async-start | bytes 5242880 | tf_op jit(solution)/shard_map/all_gather | solution.py:819
  9.9 274.1 %all-gather.9.cloned.1.call-start = ((), (), s32[]{:S(2)}) async-start(), calls=%async_computation.1 | async-start | bytes 5242880 | tf_op jit(solution)/shard_map/all_gather | solution.py:842
  9.9 4.4 copy-start.5
  101.6 31.9 %collective-permute-start = (bf16[4,256,2048]{2,1,0:T(8,128)(2,1)}, bf16[4,256,2048]{2,1,0:T(8,128)(2,1)}, u32[]{:S(2)}, u32[]{:S(2)}) collective-permute-start(bf16[4,256,2048]{2,1,0:T(8,128)(2,1)} %bitcast.61), channel_id=1, source_target_pairs={{0,1},{1,0},{2,3},{3,2},{4,5},{5,4},{6,7},{7,6},{8,9},{9,8},{10,11... | collective-permute-start | bytes 12582920 | tf_op jit(solution)/shard_map/ppermute | solution.py:833
  148.1 399.0 %all-gather.7.cloned.1.call-start = ((), (), s32[]{:S(2)}) async-start(), calls=%async_computation | async-start | bytes 5242880 | tf_op jit(solution)/shard_map/all_gather | solution.py:845
  187.9 359.9 %all-reduce.2.cloned.1.call-start = ((), (), s32[]{:S(2)}) async-start(), calls=%async_computation.2 | async-start | bytes 8388608 | tf_op jit(solution)/shard_map/psum | solution.py:857
  190.4 61.8 %collective-permute-start.1 = (bf16[256,2048]{1,0:T(8,128)(2,1)}, bf16[256,2048]{1,0:T(8,128)(2,1)S(1)}, u32[]{:S(2)}, u32[]{:S(2)}) collective-permute-start(bf16[256,2048]{1,0:T(8,128)(2,1)} %slice.15), channel_id=1, source_target_pairs={{0,2},{1,3},{2,0},{3,1},{4,6},{5,7},{6,4},{7,5},{8,10},{9,11},{10,... | collective-permute-start | bytes 3145736 | tf_op jit(solution)/shard_map/ppermute | solution.py:826
  192.4 3.0 copy-start.2
  196.9 87.1 %collective-permute-start.3 = (bf16[512,2048]{1,0:T(8,128)(2,1)}, bf16[512,2048]{1,0:T(8,128)(2,1)}, u32[]{:S(2)}, u32[]{:S(2)}) collective-permute-start(bf16[512,2048]{1,0:T(8,128)(2,1)} %slice.17), channel_id=1, source_target_pairs={{0,2},{1,3},{2,0},{3,1},{4,6},{5,7},{6,4},{7,5},{8,10},{9,11},{10,... | collective-permute-start | bytes 6291464 | tf_op jit(solution)/shard_map/ppermute | solution.py:826
  206.1 77.9 %collective-permute-start.2 = (bf16[256,2048]{1,0:T(8,128)(2,1)S(1)}, bf16[256,2048]{1,0:T(8,128)(2,1)S(1)}, u32[]{:S(2)}, u32[]{:S(2)}) collective-permute-start(bf16[256,2048]{1,0:T(8,128)(2,1)S(1)} %slice.16), channel_id=1, source_target_pairs={{0,2},{1,3},{2,0},{3,1},{4,6},{5,7},{6,4},{7,5},{8,10},{9,11},{10,... | collective-permute-start | bytes 3145736 | tf_op jit(solution)/shard_map/ppermute | solution.py:826
  252.3 31.8 %copy-start.6 = (bf16[256,2048]{1,0:T(8,128)(2,1)}, bf16[256,2048]{1,0:T(8,128)(2,1)S(1)}, u32[]{:S(2)}) copy-start(bf16[256,2048]{1,0:T(8,128)(2,1)S(1)} %collective-permute-done.1.far0_ref) | copy-start | bytes 3145732
  284.0 1.0 copy-start.7
  377.6 171.4 %all-gather.13.cloned.1.call-start = ((), (), s32[]{:S(2)}) async-start(), calls=%async_computation.4 | async-start | bytes 15728640 | tf_op jit(solution)/shard_map/all_gather | solution.py:858
  378.2 169.0 %copy-start.9 = (f32[4,2,128]{2,1,0:T(2,128)S(1)}, f32[4,2,128]{2,1,0:T(2,128)}, u32[]{:S(2)}) copy-start(f32[4,2,128]{2,1,0:T(2,128)} %get-tuple-element.73) | copy-start | bytes 12292
  562.6 4.9 copy-start.4
  567.5 3.7 copy-start.3
  571.2 2.1 copy-start.8
  571.2 3.1 copy-start.1
Sparse Core Ops, SparseCore 0:
  10.1 84.1 all-gather.10
  148.2 94.9 all-gather.8
  244.8 79.9 all-gather.6
  377.7 87.5 all-reduce.1
  466.7 82.2 all-gather.12

commit v6 on v5

--- a/solution.py
+++ b/solution.py
@@ -377,8 +377,15 @@
     )(q, k, v, o, do, lse)
 
 
-def post_kernel(o_ref, mine_ref, other_ref, x_ref, gy_ref, pw_ref, y_ref, gp_ref, do_ref, gpost_ref):
+def post_kernel(o_ref, mine_ref, other_ref, x_any, gy_any, pw_ref, y_ref, gp_ref, do_ref, gpost_ref, x_ref, gy_ref, sems):
     tp_size, heads, _, head_dim = o_ref.shape
+    block = x_ref.shape[0]
+    first_row = (lax.axis_index("tp") * pl.num_programs(0) + pl.program_id(0)) * block
+    loads = []
+    for idx, (src, dst) in enumerate(((x_any, x_ref), (gy_any, gy_ref))):
+        load = pltpu.make_async_copy(src.at[pl.ds(pl.multiple_of(first_row, block), block)], dst, sems.at[idx])
+        load.start()
+        loads.append(load)
     core = lax.rem(lax.axis_index("cp"), 2)
     halves = ((mine_ref, core * (heads // 2)), (other_ref, (1 - core) * (heads // 2)))
     proj = None
@@ -386,6 +393,8 @@
         for w_ref, start in halves:
             term = dot_nn(jnp.concatenate([o_ref[idx, start + head] for head in range(heads // 2)], axis=1), w_ref[idx])
             proj = term if proj is None else proj + term
+    for load in loads:
+        load.wait()
     gain = pw_ref[...]
     inv = lax.rsqrt(jnp.mean(proj * proj, axis=-1, keepdims=True) + NORM_EPS)
     hat = proj * inv
@@ -412,6 +421,8 @@
     tp_size, heads, rows, head_dim = o_all.shape
     d_model = x.shape[1]
     block = min(128, rows)
+    any_spec = pl.BlockSpec(memory_space=pl.ANY)
+    piece = pltpu.VMEM((block, d_model), jnp.bfloat16)
     act = pl.BlockSpec((block, d_model), lambda i: (i, 0))
     by_head = pl.BlockSpec((tp_size, heads, block, head_dim), lambda i: (0, 0, i, 0))
     act_shape = jax.ShapeDtypeStruct((rows, d_model), jnp.bfloat16)
@@ -419,12 +430,36 @@
         post_kernel,
         grid=(rows // block,),
         out_shape=(act_shape, act_shape, jax.ShapeDtypeStruct(o_all.shape, jnp.bfloat16), jax.ShapeDtypeStruct((1, d_model), jnp.float32)),
-        in_specs=[by_head] + [pl.BlockSpec(wo_mine.shape, lambda i: (0, 0, 0))] * 2 + [act, act, pl.BlockSpec((1, d_model), lambda i: (0, 0))],
+        in_specs=[by_head] + [pl.BlockSpec(wo_mine.shape, lambda i: (0, 0, 0))] * 2 + [any_spec, any_spec, pl.BlockSpec((1, d_model), lambda i: (0, 0))],
         out_specs=(act, act, by_head, pl.BlockSpec((1, d_model), lambda i: (0, 0))),
+        scratch_shapes=[piece, piece, pltpu.SemaphoreType.DMA((2,))],
         compiler_params=pltpu.CompilerParams(vmem_limit_bytes=VMEM_LIMIT),
         cost_estimate=pl.CostEstimate(flops=4 * rows * d_model * d_model, bytes_accessed=4 * d_model * d_model, transcendentals=rows),
         name="post",
     )(o_all, wo_mine, wo_other, x, gy, gain)
+
+
+def output_weights_kernel(o_ref, gp_ref, out_ref):
+    heads, _, head_dim = o_ref.shape
+    acc = dot_tn(jnp.concatenate([o_ref[head] for head in range(heads)], axis=1), gp_ref[...])
+    for head in range(heads):
+        out_ref[head] = acc[head * head_dim:(head + 1) * head_dim, :]
+
+
+def output_weights(o_heads, grad_proj):
+    heads, rows, head_dim = o_heads.shape
+    d_model = grad_proj.shape[1]
+    block = min(512, d_model)
+    return pl.pallas_call(
+        output_weights_kernel,
+        grid=(d_model // block,),
+        out_shape=jax.ShapeDtypeStruct((heads, head_dim, d_model), jnp.float32),
+        in_specs=[pl.BlockSpec(o_heads.shape, lambda i: (0, 0, 0)), pl.BlockSpec((rows, block), lambda i: (0, i))],
+        out_specs=pl.BlockSpec((heads, head_dim, block), lambda i: (0, 0, i)),
+        compiler_params=pltpu.CompilerParams(vmem_limit_bytes=VMEM_LIMIT),
+        cost_estimate=pl.CostEstimate(flops=2 * rows * d_model * heads * head_dim, bytes_accessed=12 * rows * d_model, transcendentals=0),
+        name="output_weights",
+    )(o_heads, grad_proj)
 
 
 def spread_kernel(in_ref, *out_refs):
@@ -594,10 +629,10 @@
     )(*grads, *weights, gy)
 
 
-def weights_back_kernel(tp_size, full_width, sub, x_ref, far0_ref, far1_ref, far2_ref, wq_ref, wk_ref, dq_ref, dk_ref, dv_ref, cos_ref, sin_ref, qg_ref, kg_ref, post_ref, o_ref, gp_ref,
-                        dw_ref, exq_ref, exk_ref, exv_ref, gains_ref, post_out, dwo_ref,
-                        x_buf, wqk_ref, gp_buf, lin_ref, q16_ref, k16_ref, own, slots_tp, mid, slots_cp, total, gq_ref, gk_ref, my_gains,
-                        x_sem, w_sem, pair_send, pair_recv, tp_send, tp_recv, cp_send, cp_recv, ex_send, ex_recv):
+def weights_back_kernel(full_width, sub, x_ref, far0_ref, far1_ref, far2_ref, wq_ref, wk_ref, dq_ref, dk_ref, dv_ref, cos_ref, sin_ref, qg_ref, kg_ref, post_ref,
+                        dw_ref, exq_ref, exk_ref, exv_ref, gains_ref, post_out,
+                        x_buf, wqk_ref, lin_ref, q16_ref, k16_ref, own, slots_tp, mid, slots_cp, done, total, gq_ref, gk_ref, my_gains,
+                        x_sem, w_sem, pair_send, pair_recv, tp_send, tp_recv, cp_send, cp_recv, back_send, back_recv, ex_send, ex_recv):
     me = lax.axis_index("cp")
     my_tp = lax.axis_index("tp")
     rows, head_dim = dq_ref.shape[1:]
@@ -611,7 +646,6 @@
         loads.append(load)
     own_rows = pl.ds(pl.multiple_of(me * head_dim, head_dim), head_dim)
     w_loads = [pltpu.make_async_copy(src.at[own_rows], wqk_ref.at[pl.ds(idx * head_dim, head_dim)], w_sem.at[idx]) for idx, src in enumerate((wq_ref, wk_ref))]
-    w_loads.append(pltpu.make_async_copy(gp_ref, gp_buf, w_sem.at[2]))
     for load in w_loads:
         load.start()
     peers_barrier()
@@ -663,20 +697,23 @@
 
         lax.fori_loop(0, rows // sub, first, 0)
 
+    quarter = own.shape[1] // 4
+
+    def quarter_of(which):
+        return pl.ds(pl.multiple_of(which * quarter, quarter), quarter)
+
     moves = []
-    for shift in range(1, tp_size):
+    for shift in (2, 1, 3):
+        peer = lax.rem(my_tp + shift, 4)
         move = pltpu.make_async_remote_copy(
-            src_ref=own, dst_ref=slots_tp.at[my_tp], send_sem=tp_send.at[shift - 1], recv_sem=tp_recv.at[shift - 1],
-            device_id={"tp": lax.rem(my_tp + shift, tp_size)}, device_id_type=MESH)
+            src_ref=own.at[:, quarter_of(peer)], dst_ref=slots_tp.at[my_tp], send_sem=tp_send.at[shift - 1], recv_sem=tp_recv.at[shift - 1],
+            device_id={"tp": peer}, device_id_type=MESH)
         move.start()
         moves.append(move)
-    slots_tp[my_tp] = own[...]
+    slots_tp[my_tp] = own[:, quarter_of(my_tp)]
     for move in moves:
         move.wait()
-    acc = slots_tp[0]
-    for idx in range(1, tp_size):
-        acc = acc + slots_tp[idx]
-    mid[...] = acc
+    mid[...] = slots_tp[0] + slots_tp[1] + slots_tp[2] + slots_tp[3]
     moves = []
     for dist in (2, 3, 1):
         move = pltpu.make_async_remote_copy(
@@ -687,7 +724,17 @@
     slots_cp[me] = mid[...]
     for move in moves:
         move.wait()
-    total[...] = slots_cp[0] + slots_cp[1] + slots_cp[2] + slots_cp[3]
+    done[...] = slots_cp[0] + slots_cp[1] + slots_cp[2] + slots_cp[3]
+    moves = []
+    for shift in (2, 1, 3):
+        move = pltpu.make_async_remote_copy(
+            src_ref=done, dst_ref=total.at[:, quarter_of(my_tp)], send_sem=back_send.at[shift - 1], recv_sem=back_recv.at[shift - 1],
+            device_id={"tp": lax.rem(my_tp + shift, 4)}, device_id_type=MESH)
+        move.start()
+        moves.append(move)
+    total[:, quarter_of(my_tp)] = done[...]
+    for move in moves:
+        move.wait()
 
     post_out[...] = total[4:5, 0:post_ref.shape[1]]
     gq_ref[...] = jnp.zeros_like(gq_ref)
@@ -746,47 +793,36 @@
         return carry
 
     lax.fori_loop(0, x_buf.shape[2] // block, weight_step, 0)
-    w_loads[2].wait()
-
-    def output_step(idx, carry):
-        cols = pl.ds(pl.multiple_of(idx * block, block), block)
-        grads = jnp.concatenate([o_ref[head] for head in range(o_ref.shape[0])], axis=1)
-        acc = dot_tn(grads, gp_buf[:, cols])
-        for head in range(o_ref.shape[0]):
-            dwo_ref[head, :, cols] = acc[head * head_dim:(head + 1) * head_dim, :]
-        return carry
-
-    lax.fori_loop(0, x_buf.shape[2] // block, output_step, 0)
     for copy in copies:
         copy.wait()
     for load in loads[4:]:
         load.wait_send()
 
 
-def weights_back(tp_size, collective_id, full_width, x, x_far, wq, wk, dq, dk, dv, cos_tab, sin_tab, q_gain, k_gain, grad_post, o_heads, grad_proj):
+def weights_back(collective_id, full_width, x, x_far, wq, wk, dq, dk, dv, cos_tab, sin_tab, q_gain, k_gain, grad_post):
     _, rows, head_dim = dq.shape
     d_model = x.shape[1]
     any_spec = pl.BlockSpec(memory_space=pl.ANY)
     dma = pltpu.SemaphoreType.DMA
     span = max(4 * rows, d_model)
     stat = pltpu.VMEM((5, span), jnp.float32)
-    slots = pltpu.VMEM((4, 5, span), jnp.float32)
+    slots = pltpu.VMEM((4, 5, span // 4), jnp.float32)
+    small = pltpu.VMEM((5, span // 4), jnp.float32)
     ex = jax.ShapeDtypeStruct(dq.shape, jnp.bfloat16)
     return pl.pallas_call(
-        functools.partial(weights_back_kernel, tp_size, full_width, min(512, rows)),
+        functools.partial(weights_back_kernel, full_width, min(512, rows)),
         out_shape=(jax.ShapeDtypeStruct((3, d_model, head_dim), jnp.float32), ex, ex, ex,
-                   jax.ShapeDtypeStruct((4, 2, head_dim), jnp.float32), jax.ShapeDtypeStruct((1, d_model), jnp.float32),
-                   jax.ShapeDtypeStruct((o_heads.shape[0], head_dim, d_model), jnp.float32)),
-        in_specs=[any_spec] * 6 + [VMEM_SPEC] * 9 + [any_spec],
-        out_specs=tuple([VMEM_SPEC] * 7),
-        scratch_shapes=[pltpu.VMEM((4, rows, d_model), jnp.bfloat16), pltpu.VMEM((2 * head_dim, d_model), jnp.bfloat16), pltpu.VMEM((rows, d_model), jnp.bfloat16), pltpu.VMEM((4, rows, 2 * head_dim), jnp.float32),
+                   jax.ShapeDtypeStruct((4, 2, head_dim), jnp.float32), jax.ShapeDtypeStruct((1, d_model), jnp.float32)),
+        in_specs=[any_spec] * 6 + [VMEM_SPEC] * 8,
+        out_specs=tuple([VMEM_SPEC] * 6),
+        scratch_shapes=[pltpu.VMEM((4, rows, d_model), jnp.bfloat16), pltpu.VMEM((2 * head_dim, d_model), jnp.bfloat16), pltpu.VMEM((4, rows, 2 * head_dim), jnp.float32),
                         pltpu.VMEM(dq.shape, jnp.bfloat16), pltpu.VMEM(dq.shape, jnp.bfloat16),
-                        stat, slots, stat, slots, stat,
+                        stat, slots, small, slots, small, stat,
                         pltpu.VMEM((1, head_dim), jnp.float32), pltpu.VMEM((1, head_dim), jnp.float32), pltpu.VMEM((2, head_dim), jnp.float32),
-                        dma((4,)), dma((3,)), dma((4,)), dma((4,)), dma((tp_size - 1,)), dma((tp_size - 1,)), dma((3,)), dma((3,)), dma((4, 3)), dma((4, 3))],
+                        dma((4,)), dma((2,)), dma((4,)), dma((4,)), dma((3,)), dma((3,)), dma((3,)), dma((3,)), dma((3,)), dma((3,)), dma((4, 3)), dma((4, 3))],
         compiler_params=pltpu.CompilerParams(collective_id=collective_id, has_side_effects=True, vmem_limit_bytes=VMEM_LIMIT),
         name="weights_back",
-    )(x, *x_far, wq, wk, dq, dk, dv, cos_tab, sin_tab, q_gain, k_gain, grad_post, o_heads, grad_proj)
+    )(x, *x_far, wq, wk, dq, dk, dv, cos_tab, sin_tab, q_gain, k_gain, grad_post)
 
 
 def solution(mesh):
@@ -834,27 +870,28 @@
         o_heads, o_tokens = heads_to_tokens(2, o_seq.reshape(block_shape))
         o_tokens, x_free = lax.optimization_barrier((o_tokens, x))
         far1 = fetch(piece, piece)
-        quarter = rows // tp_size
-        first_row = lax.axis_index("tp") * quarter
-        x_mine, gy_mine = (lax.dynamic_slice_in_dim(t, first_row, quarter, axis=0) for t in (x, gy))
-        y_mine, gp_mine, do_tokens, grad_post = post(o_tokens, wo_mine, wo_other, x_mine, gy_mine, post_norm_w[None, :])
+        y_mine, gp_mine, do_tokens, grad_post = post(o_tokens, wo_mine, wo_other, x, gy, post_norm_w[None, :])
         do_seq = tokens_to_heads(3, do_tokens)
+        y_mine, gp_mine, do_seq, x_free = lax.optimization_barrier((y_mine, gp_mine, do_seq, x))
         grad_proj = lax.all_gather(gp_mine, "tp", tiled=True)
-        y_mine, do_seq, x_free = lax.optimization_barrier((y_mine, do_seq, x))
         far2 = fetch(2 * piece, rows - 2 * piece)
-        y_out = lax.all_gather(y_mine, "tp", tiled=True)
-
-        coarse_cos, coarse_sin = (t[:, None, :] for t in rope_tables(jnp.arange(0, cp_size * rows, 64, dtype=jnp.float32), head_dim))
-        fine_cos, fine_sin = (t[None, :, :] for t in rope_tables(jnp.arange(64, dtype=jnp.float32), head_dim))
-        seq_cos = (coarse_cos * fine_cos - coarse_sin * fine_sin).reshape(cp_size * rows, head_dim // 2)
-        seq_sin = (coarse_sin * fine_cos + coarse_cos * fine_sin).reshape(cp_size * rows, head_dim // 2)
-        seq_cos, seq_sin = wide_tables(seq_cos, seq_sin)
+
+        coarse_cos, coarse_sin = rope_tables(jnp.arange(0, cp_size * rows, 64, dtype=jnp.float32), head_dim)
+        fine_cos, fine_sin = (jnp.concatenate([t, t], axis=1)[None] for t in rope_tables(jnp.arange(64, dtype=jnp.float32), head_dim))
+        wide_cos, wide_sin, sign_cos, sign_sin = lax.optimization_barrier(tuple(
+            jnp.concatenate([sign * t, t], axis=1)[:, None, :] for sign in (1.0, -1.0) for t in (coarse_cos, coarse_sin)))
+        fine_cos, fine_sin = lax.optimization_barrier((fine_cos, fine_sin))
+        seq_cos = (wide_cos * fine_cos - wide_sin * fine_sin).reshape(cp_size * rows, head_dim)
+        seq_sin = (sign_sin * fine_cos + sign_cos * fine_sin).reshape(cp_size * rows, head_dim)
         gains_head = tuple(lax.dynamic_slice_in_dim(w, cp_index, 1, axis=0) for w in (q_norm_w, k_norm_w))
         dq_seq, dk_seq, dv_seq = attend_back(q_seq, k_seq, v_seq, o_seq, do_seq.reshape(seq_shape), lse)
-        dw, dq16, dk16, dv16, gains, grad_post, grad_w_o = weights_back(
-            tp_size, 4, full_width, x, (far0, far1, far2), turned[0], turned[1],
-            dq_seq.reshape(block_shape), dk_seq.reshape(block_shape), dv_seq.reshape(block_shape), seq_cos, seq_sin, *gains_head, grad_post, o_heads, grad_proj)
-        grad_w_o = lax.psum(grad_w_o, "cp")
+        y_mine, dq_seq = lax.optimization_barrier((y_mine, dq_seq))
+        y_out = lax.all_gather(y_mine, "tp", tiled=True)
+        dw, dq16, dk16, dv16, gains, grad_post = weights_back(
+            4, full_width, x, (far0, far1, far2), turned[0], turned[1],
+            dq_seq.reshape(block_shape), dk_seq.reshape(block_shape), dv_seq.reshape(block_shape), seq_cos, seq_sin, *gains_head, grad_post)
+        o_heads, dw = lax.optimization_barrier((o_heads, dw))
+        grad_w_o = lax.psum(output_weights(o_heads, grad_proj), "cp")
         dw = spread(lax.all_gather(dw, "cp"))
         grad_x = chain_sum(tp_size, 6, (dq16, dk16, dv16), turned, gy)
         return (y_out[None], grad_x[None]) + tuple(dw) + (grad_w_o, gains[:, 0], gains[:, 1], grad_post[0])

time: 582 us -> 593 us (1.019)
  waiting for transfers between devices: 33.6 us -> 84.7 us
  Pallas kernels: 478 us -> 450 us
  other arithmetic: 13 us -> 6.31 us
    ppermute x3, waiting for transfers between devices: 31.8 us -> 84.6 us  [fetch(): lax.ppermute(x_free[start:start + size], 'cp', [(dev, dev ^ 2) for dev in...]
    pallas_call x1 -> x2, Pallas kernels: 92.5 us -> 76.3 us  [the longest x1 69.8 us: weights_back(): pl.pallas_call(functools.partial(weights_back_kernel, full_width, min(512...]
    pallas_call x1, Pallas kernels: 39.7 us -> 28 us  [tokens_to_heads(): pl.pallas_call(tokens_to_heads_kernel, out_shape=jax.ShapeDtypeStruct((he...]
    concatenate x2 -> x1, other arithmetic: 7.4 us -> 1.31 us  [wide_tables(): jnp.concatenate([cos_tab, cos_tab], axis=1)]
  transfers between devices with their start and end apart: 9 -> 9, of which waited for: 2 -> 2; matrix products, arithmetic and copies ran while one was open for 6% -> 4% of each run, Pallas kernels for 77% -> 68%
where the time goes in v6:
time: 593 us
  Pallas kernels  450 us (76%)
  waiting for transfers between devices  84.7 us (14%)
  local copies, waits for them, and re-layouts  34.2 us (6%)
  between operations  14 us (2%)
  other arithmetic  6.31 us (1%)
    pallas_call x1, Pallas kernels, chain_sum(): pl.pallas_call(functools.partial(chain_kernel, size, n_chunk, 2, min(256,...  167 us
    ppermute x3, waiting for transfers between devices, fetch(): lax.ppermute(x_free[start:start + size], 'cp', [(dev, dev ^ 2) for dev in...  84.6 us
    pallas_call x1, Pallas kernels, weights_back(): pl.pallas_call(functools.partial(weights_back_kernel, full_width, min(512...  69.8 us
    pallas_call x1, Pallas kernels, front(): pl.pallas_call(functools.partial(front_kernel, full_width, min(256, rows)...  49.5 us
    pallas_call x1, Pallas kernels, attend_back(): pl.pallas_call(functools.partial(attend_back_kernel, block, head_dim ** (...  43.2 us
    pallas_call x1, Pallas kernels, heads_to_tokens(): pl.pallas_call(heads_to_tokens_kernel, out_shape=(jax.ShapeDtypeStruct(ar...  28.2 us
    pallas_call x1, Pallas kernels, tokens_to_heads(): pl.pallas_call(tokens_to_heads_kernel, out_shape=jax.ShapeDtypeStruct((he...  28 us
    pallas_call x1, Pallas kernels, attend(): pl.pallas_call(functools.partial(attend_kernel, block, head_dim ** (-0.5)...  27.6 us
  transfers between devices with their start and end apart: 9, of which 2 were waited for; matrix products, arithmetic and copies ran while one was open for 4% of the time, Pallas kernels for 68%

profile of v6, /device:TPU:0, one launch (start us, length us, event | category | flops | bytes accessed | tf_op | source)
XLA Modules:
  0.0 592.6 jit_solution(9122404034597598079)
XLA Ops:
  7.2 0.0 all-gather.11.cloned.1.call-start
  7.3 1.5 copy-done
  8.8 1.1 constant_dynamic-slice_fusion.2
  9.9 0.0 all-gather.11.cloned.1.call-update
  9.9 0.0 all-gather.9.cloned.1.call-start
  9.9 4.4 copy.21
  14.3 2.6 copy.22
  16.9 4.3 copy.23
  21.2 1.9 fusion
  23.1 1.3 pad_maximum_fusion
  24.4 49.5 %front.1 = (bf16[4,1024,128]{2,1,0:T(8,128)(2,1)}, bf16[4,1024,128]{2,1,0:T(8,128)(2,1)}, bf16[4,1024,128]{2,1,0:T(8,128)(2,1)}) custom-call(bf16[1024,2048]{1,0:T(8,128)(2,1)} %bitcast.47, bf16[512,2048]{1,0:T(8,128)(2,1)} %bitcast.53, bf16[512,2048]{1,0:T(8,128)(2,1)} %bitcast.56, bf16[512,2048]{1,0:T(8,128)(2,1)} %bitcast.62, ...), custom_call_target="tpu_custom_call" | custom-call | tf_op jit(solution)/shard_map/front/pallas_call | solution.py:250
  73.9 27.6 %attend.1 = (bf16[4096,128]{1,0:T(8,128)(2,1)}, f32[1,4096]{1,0:T(1,128)}) custom-call(bf16[4096,128]{1,0:T(8,128)(2,1)} %bitcast.85, bf16[4096,128]{1,0:T(8,128)(2,1)} %bitcast.87, bf16[4096,128]{1,0:T(8,128)(2,1)} %bitcast.89), custom_call_target="tpu_custom_call" | custom-call | flops 4294967296 | bytes 4194304 | tf_op jit(solution)/shard_map/attend/pallas_call | solution.py:303
  101.5 0.7 collective-permute-start
  102.2 28.2 %heads_to_tokens.1 = (bf16[4,1024,128]{2,1,0:T(8,128)(2,1)}, bf16[4,4,256,128]{3,2,1,0:T(8,128)(2,1)}) custom-call(bf16[4,1024,128]{2,1,0:T(8,128)(2,1)} %bitcast.73), custom_call_target="tpu_custom_call" | custom-call | tf_op jit(solution)/shard_map/heads_to_tokens/pallas_call | solution.py:108
  130.5 16.3 %post.1 = (bf16[256,2048]{1,0:T(8,128)(2,1)}, bf16[256,2048]{1,0:T(8,128)(2,1)}, bf16[4,4,256,128]{3,2,1,0:T(8,128)(2,1)}, f32[1,2048]{1,0:T(1,128)}) custom-call(bf16[4,4,256,128]{3,2,1,0:T(8,128)(2,1)} %get-tuple-element.59.o_ref, bf16[4,256,2048]{2,1,0:T(8,128)(2,1)} %bitcast.69, bf16[4,256,2048]{2,1,0:T(8,128)(2,1)} %collective-permute-done.other_ref, ...), custom_call_target="tpu_custom_call" | custom-call | flops 4294967296 | bytes 16777216 | tf_op jit(solution)/shard_map/post/pallas_call | solution.py:429
  146.8 28.0 %tokens_to_heads.1 = bf16[4,1024,128]{2,1,0:T(8,128)(2,1)} custom-call(bf16[4,4,256,128]{3,2,1,0:T(8,128)(2,1)} %get-tuple-element.63.in_ref), custom_call_target="tpu_custom_call" | custom-call | tf_op jit(solution)/shard_map/tokens_to_heads/pallas_call | solution.py:159
  174.8 0.0 all-gather.9.cloned.1.call-update
  174.8 0.2 all-gather.7.cloned.1.call-start
  175.0 43.2 %attend_back.1 = (f32[4096,128]{1,0:T(8,128)}, f32[4096,128]{1,0:T(8,128)}, bf16[4096,128]{1,0:T(8,128)(2,1)}) custom-call(bf16[4096,128]{1,0:T(8,128)(2,1)} %bitcast.86, bf16[4096,128]{1,0:T(8,128)(2,1)} %bitcast.88, bf16[4096,128]{1,0:T(8,128)(2,1)} %bitcast.90, bf16[4096,128]{1,0:T(8,128)(2,1)} %get-tuple-element.57.o_ref, bf16[4096,128]{1,0:T(8,128)(2,1)} %bitcast.74, ...), custom_call_target="tpu_custom_call" | custom-call | flops 10737418240 | bytes 10485760 | tf_op jit(solution)/shard_map/attend_back/pallas_call | solution.py:367
  218.2 0.0 all-gather.13.cloned.1.call-start
  218.3 3.3 slice.17
  221.6 0.2 collective-permute-start.3
  221.8 1.1 slice.15
  222.9 1.8 collective-permute-start.1
  224.7 1.0 slice.16
  225.7 0.2 collective-permute-start.2
  225.9 0.3 broadcast_multiply_fusion
  226.2 0.1 maximum_bitcast_fusion.2
  226.3 0.1 maximum_bitcast_fusion.4
  226.4 1.2 constant_dynamic-slice_fusion
  227.6 2.6 multiply_add_fusion
  230.3 62.5 %collective-permute-done.1.far0_ref = bf16[256,2048]{1,0:T(8,128)(2,1)S(1)} collective-permute-done((bf16[256,2048]{1,0:T(8,128)(2,1)}, bf16[256,2048]{1,0:T(8,128)(2,1)S(1)}, u32[]{:S(2)}, u32[]{:S(2)}) %collective-permute-start.1) | collective-permute-done | bytes 1048608 | tf_op jit(solution)/shard_map/ppermute | solution.py:862
  292.8 22.1 %collective-permute-done.2.far1_ref = bf16[256,2048]{1,0:T(8,128)(2,1)} collective-permute-done((bf16[256,2048]{1,0:T(8,128)(2,1)}, bf16[256,2048]{1,0:T(8,128)(2,1)}, u32[]{:S(2)}, u32[]{:S(2)}) %collective-permute-start.2) | collective-permute-done | bytes 1048608 | tf_op jit(solution)/shard_map/ppermute | solution.py:862
  314.9 1.3 copy-done.5
  316.2 69.8 %weights_back.1 = (f32[3,2048,128]{2,1,0:T(8,128)}, bf16[4,1024,128]{2,1,0:T(8,128)(2,1)}, bf16[4,1024,128]{2,1,0:T(8,128)(2,1)}, bf16[4,1024,128]{2,1,0:T(8,128...) custom-call(bf16[1024,2048]{1,0:T(8,128)(2,1)} %bitcast.50, bf16[256,2048]{1,0:T(8,128)(2,1)} %copy-done.7, ...), custom_call_target="tpu_custom_call" | custom-call | tf_op jit(solution)/shard_map/weights_back/pallas_call | solution.py:812
  386.1 0.0 all-gather.13.cloned.1.call-update
  386.1 0.0 all-reduce.2.cloned.1.call-start
  386.1 0.0 all-gather.9.cloned.1.call-done.gp_ref
  386.2 6.4 %output_weights.1 = f32[4,128,2048]{2,1,0:T(8,128)} custom-call(bf16[4,1024,128]{2,1,0:T(8,128)(2,1)} %get-tuple-element.91.o_ref, bf16[1024,2048]{1,0:T(8,128)(2,1)} %all-gather.9.cloned.1.call-done.gp_ref), custom_call_target="tpu_custom_call" | custom-call | flops 2147483648 | bytes 25165824 | tf_op jit(solution)/shard_map/output_weights/pallas_call | solution.py:453
  392.6 167.5 %chain_sum.1 = bf16[1024,2048]{1,0:T(8,128)(2,1)} custom-call(bf16[4,1024,128]{2,1,0:T(8,128)(2,1)} %get-tuple-element.82.dq_ref, bf16[4,1024,128]{2,1,0:T(8,128)(2,1)} %get-tuple-element.83.dk_ref, bf16[4,1024,128]{2,1,0:T(8,128)(2,1)} %get-tuple-element.84.dv_ref, bf16[512,2048]{1,0:T(8,128)(2,1)} %bitcast.55, bf16[512,2048]{1,0:T(8,128)(2,1)} %bitcast.58, ...), custom_call_target="tpu_custom_call" | custom-call | flops 99999997952 | bytes 33554432 | tf_op jit(solution)/shard_map/chain_sum/pallas_call | solution.py:620
  560.1 0.6 fusion.3
  560.7 13.6 %spread.1 = (f32[2048,4,128]{2,1,0:T(4,128)}, f32[2048,4,128]{2,1,0:T(4,128)}, f32[2048,4,128]{2,1,0:T(4,128)}) custom-call(f32[4,3,2048,128]{3,2,1,0:T(8,128)} %bitcast.59), custom_call_target="tpu_custom_call" | custom-call | flops 3145728 | bytes 25165824 | tf_op jit(solution)/shard_map/spread/pallas_call | solution.py:474
  574.3 4.9 copy.28
  579.3 2.1 copy.29
  581.4 1.6 copy-done.3
  583.0 2.1 copy.30
  585.1 0.6 copy.31
  585.7 0.4 copy-done.1
  (27 shorter events, 0.1 us)
Async XLA Ops:
  7.2 1.6 copy-start
  7.2 94.4 %all-gather.11.cloned.1.call-start = ((), (), s32[]{:S(2)}) async-start(), calls=%async_computation.3 | async-start | bytes 5242880 | tf_op jit(solution)/shard_map/all_gather | solution.py:855
  9.9 4.5 copy-start.6
  9.9 376.3 %all-gather.9.cloned.1.call-start = ((), (), s32[]{:S(2)}) async-start(), calls=%async_computation.1 | async-start | bytes 5242880 | tf_op jit(solution)/shard_map/all_gather | solution.py:876
  101.5 28.9 %collective-permute-start = (bf16[4,256,2048]{2,1,0:T(8,128)(2,1)}, bf16[4,256,2048]{2,1,0:T(8,128)(2,1)}, u32[]{:S(2)}, u32[]{:S(2)}) collective-permute-start(bf16[4,256,2048]{2,1,0:T(8,128)(2,1)} %bitcast.68), channel_id=1, source_target_pairs={{0,1},{1,0},{2,3},{3,2},{4,5},{5,4},{6,7},{7,6},{8,9},{9,8},{10,11... | collective-permute-start | bytes 12582920 | tf_op jit(solution)/shard_map/ppermute | solution.py:869
  174.8 385.9 %all-gather.7.cloned.1.call-start = ((), (), s32[]{:S(2)}) async-start(), calls=%async_computation | async-start | bytes 5242880 | tf_op jit(solution)/shard_map/all_gather | solution.py:889
  218.2 342.5 %all-gather.13.cloned.1.call-start = ((), (), s32[]{:S(2)}) async-start(), calls=%async_computation.4 | async-start | bytes 15728640 | tf_op jit(solution)/shard_map/all_gather | solution.py:895
  218.3 3.6 copy-start.2
  221.6 93.3 %collective-permute-start.3 = (bf16[512,2048]{1,0:T(8,128)(2,1)}, bf16[512,2048]{1,0:T(8,128)(2,1)S(1)}, u32[]{:S(2)}, u32[]{:S(2)}) collective-permute-start(bf16[512,2048]{1,0:T(8,128)(2,1)} %slice.17), channel_id=1, source_target_pairs={{0,2},{1,3},{2,0},{3,1},{4,6},{5,7},{6,4},{7,5},{8,10},{9,11},{10,... | collective-permute-start | bytes 6291464 | tf_op jit(solution)/shard_map/ppermute | solution.py:862
  222.9 69.9 %collective-permute-start.1 = (bf16[256,2048]{1,0:T(8,128)(2,1)}, bf16[256,2048]{1,0:T(8,128)(2,1)S(1)}, u32[]{:S(2)}, u32[]{:S(2)}) collective-permute-start(bf16[256,2048]{1,0:T(8,128)(2,1)} %slice.15), channel_id=1, source_target_pairs={{0,2},{1,3},{2,0},{3,1},{4,6},{5,7},{6,4},{7,5},{8,10},{9,11},{10,... | collective-permute-start | bytes 3145736 | tf_op jit(solution)/shard_map/ppermute | solution.py:862
  225.7 89.2 %collective-permute-start.2 = (bf16[256,2048]{1,0:T(8,128)(2,1)}, bf16[256,2048]{1,0:T(8,128)(2,1)}, u32[]{:S(2)}, u32[]{:S(2)}) collective-permute-start(bf16[256,2048]{1,0:T(8,128)(2,1)} %slice.16), channel_id=1, source_target_pairs={{0,2},{1,3},{2,0},{3,1},{4,6},{5,7},{6,4},{7,5},{8,10},{9,11},{10,... | collective-permute-start | bytes 3145736 | tf_op jit(solution)/shard_map/ppermute | solution.py:862
  292.8 22.1 %copy-start.7 = (bf16[256,2048]{1,0:T(8,128)(2,1)}, bf16[256,2048]{1,0:T(8,128)(2,1)S(1)}, u32[]{:S(2)}) copy-start(bf16[256,2048]{1,0:T(8,128)(2,1)S(1)} %collective-permute-done.1.far0_ref) | copy-start | bytes 3145732
  314.9 1.3 copy-start.5
  386.1 188.3 %all-reduce.2.cloned.1.call-start = ((), (), s32[]{:S(2)}) async-start(), calls=%async_computation.2 | async-start | bytes 8388608 | tf_op jit(solution)/shard_map/psum | solution.py:894
  392.6 167.5 %copy-start.9 = (f32[4,2,128]{2,1,0:T(2,128)S(1)}, f32[4,2,128]{2,1,0:T(2,128)}, u32[]{:S(2)}) copy-start(f32[4,2,128]{2,1,0:T(2,128)} %get-tuple-element.93) | copy-start | bytes 12292
  574.3 4.9 copy-start.4
  579.3 3.7 copy-start.3
  583.0 2.1 copy-start.8
  583.0 3.1 copy-start.1
Sparse Core Ops, SparseCore 0:
  10.1 84.1 all-gather.10
  174.9 88.7 all-gather.8
  265.3 79.2 all-gather.6
  386.2 81.0 all-gather.12
  470.1 85.4 all-reduce.1

commit v7 on v6

--- a/solution.py
+++ b/solution.py
@@ -377,7 +377,7 @@
     )(q, k, v, o, do, lse)
 
 
-def post_kernel(o_ref, mine_ref, other_ref, x_any, gy_any, pw_ref, y_ref, gp_ref, do_ref, gpost_ref, x_ref, gy_ref, sems):
+def post_kernel(o_ref, mine_ref, other_ref, x_any, gy_any, pw_ref, both_ref, do_ref, gpost_ref, x_ref, gy_ref, sems):
     tp_size, heads, _, head_dim = o_ref.shape
     block = x_ref.shape[0]
     first_row = (lax.axis_index("tp") * pl.num_programs(0) + pl.program_id(0)) * block
@@ -398,12 +398,13 @@
     gain = pw_ref[...]
     inv = lax.rsqrt(jnp.mean(proj * proj, axis=-1, keepdims=True) + NORM_EPS)
     hat = proj * inv
-    y_ref[...] = (x_ref[...].astype(jnp.float32) + hat * gain).astype(jnp.bfloat16)
+    d_model = x_ref.shape[1]
+    both_ref[:, d_model:] = (x_ref[...].astype(jnp.float32) + hat * gain).astype(jnp.bfloat16)
     grad = gy_ref[...].astype(jnp.float32)
     gpost = jnp.sum(grad * hat, axis=0, keepdims=True)
     grad_hat = grad * gain
     grad_proj = (inv * (grad_hat - hat * jnp.mean(grad_hat * hat, axis=-1, keepdims=True))).astype(jnp.bfloat16)
-    gp_ref[...] = grad_proj
+    both_ref[:, :d_model] = grad_proj
     for idx in range(tp_size):
         for w_ref, start in halves:
             grad_o = dot_nt(grad_proj, w_ref[idx]).astype(jnp.bfloat16)
@@ -423,15 +424,14 @@
     block = min(128, rows)
     any_spec = pl.BlockSpec(memory_space=pl.ANY)
     piece = pltpu.VMEM((block, d_model), jnp.bfloat16)
-    act = pl.BlockSpec((block, d_model), lambda i: (i, 0))
+    both = pl.BlockSpec((block, 2 * d_model), lambda i: (i, 0))
     by_head = pl.BlockSpec((tp_size, heads, block, head_dim), lambda i: (0, 0, i, 0))
-    act_shape = jax.ShapeDtypeStruct((rows, d_model), jnp.bfloat16)
     return pl.pallas_call(
         post_kernel,
         grid=(rows // block,),
-        out_shape=(act_shape, act_shape, jax.ShapeDtypeStruct(o_all.shape, jnp.bfloat16), jax.ShapeDtypeStruct((1, d_model), jnp.float32)),
+        out_shape=(jax.ShapeDtypeStruct((rows, 2 * d_model), jnp.bfloat16), jax.ShapeDtypeStruct(o_all.shape, jnp.bfloat16), jax.ShapeDtypeStruct((1, d_model), jnp.float32)),
         in_specs=[by_head] + [pl.BlockSpec(wo_mine.shape, lambda i: (0, 0, 0))] * 2 + [any_spec, any_spec, pl.BlockSpec((1, d_model), lambda i: (0, 0))],
-        out_specs=(act, act, by_head, pl.BlockSpec((1, d_model), lambda i: (0, 0))),
+        out_specs=(both, by_head, pl.BlockSpec((1, d_model), lambda i: (0, 0))),
         scratch_shapes=[piece, piece, pltpu.SemaphoreType.DMA((2,))],
         compiler_params=pltpu.CompilerParams(vmem_limit_bytes=VMEM_LIMIT),
         cost_estimate=pl.CostEstimate(flops=4 * rows * d_model * d_model, bytes_accessed=4 * d_model * d_model, transcendentals=rows),
@@ -446,9 +446,9 @@
         out_ref[head] = acc[head * head_dim:(head + 1) * head_dim, :]
 
 
-def output_weights(o_heads, grad_proj):
+def output_weights(o_heads, both):
     heads, rows, head_dim = o_heads.shape
-    d_model = grad_proj.shape[1]
+    d_model = both.shape[1] // 2
     block = min(512, d_model)
     return pl.pallas_call(
         output_weights_kernel,
@@ -459,7 +459,7 @@
         compiler_params=pltpu.CompilerParams(vmem_limit_bytes=VMEM_LIMIT),
         cost_estimate=pl.CostEstimate(flops=2 * rows * d_model * heads * head_dim, bytes_accessed=12 * rows * d_model, transcendentals=0),
         name="output_weights",
-    )(o_heads, grad_proj)
+    )(o_heads, both)
 
 
 def spread_kernel(in_ref, *out_refs):
@@ -870,10 +870,10 @@
         o_heads, o_tokens = heads_to_tokens(2, o_seq.reshape(block_shape))
         o_tokens, x_free = lax.optimization_barrier((o_tokens, x))
         far1 = fetch(piece, piece)
-        y_mine, gp_mine, do_tokens, grad_post = post(o_tokens, wo_mine, wo_other, x, gy, post_norm_w[None, :])
+        both, do_tokens, grad_post = post(o_tokens, wo_mine, wo_other, x, gy, post_norm_w[None, :])
         do_seq = tokens_to_heads(3, do_tokens)
-        y_mine, gp_mine, do_seq, x_free = lax.optimization_barrier((y_mine, gp_mine, do_seq, x))
-        grad_proj = lax.all_gather(gp_mine, "tp", tiled=True)
+        both, do_seq, x_free = lax.optimization_barrier((both, do_seq, x))
+        both = lax.all_gather(both, "tp", tiled=True)
         far2 = fetch(2 * piece, rows - 2 * piece)
 
         coarse_cos, coarse_sin = rope_tables(jnp.arange(0, cp_size * rows, 64, dtype=jnp.float32), head_dim)
@@ -885,13 +885,12 @@
         seq_sin = (sign_sin * fine_cos + sign_cos * fine_sin).reshape(cp_size * rows, head_dim)
         gains_head = tuple(lax.dynamic_slice_in_dim(w, cp_index, 1, axis=0) for w in (q_norm_w, k_norm_w))
         dq_seq, dk_seq, dv_seq = attend_back(q_seq, k_seq, v_seq, o_seq, do_seq.reshape(seq_shape), lse)
-        y_mine, dq_seq = lax.optimization_barrier((y_mine, dq_seq))
-        y_out = lax.all_gather(y_mine, "tp", tiled=True)
         dw, dq16, dk16, dv16, gains, grad_post = weights_back(
             4, full_width, x, (far0, far1, far2), turned[0], turned[1],
             dq_seq.reshape(block_shape), dk_seq.reshape(block_shape), dv_seq.reshape(block_shape), seq_cos, seq_sin, *gains_head, grad_post)
         o_heads, dw = lax.optimization_barrier((o_heads, dw))
-        grad_w_o = lax.psum(output_weights(o_heads, grad_proj), "cp")
+        grad_w_o = lax.psum(output_weights(o_heads, both), "cp")
+        y_out = both[:, d_model:]
         dw = spread(lax.all_gather(dw, "cp"))
         grad_x = chain_sum(tp_size, 6, (dq16, dk16, dv16), turned, gy)
         return (y_out[None], grad_x[None]) + tuple(dw) + (grad_w_o, gains[:, 0], gains[:, 1], grad_post[0])

time: 593 us -> 559 us (0.943)
  waiting for transfers between devices: 84.7 us -> 38.5 us
  Pallas kernels: 450 us -> 458 us
    ppermute x3, waiting for transfers between devices: 84.6 us -> 38.5 us  [fetch(): lax.ppermute(x_free[start:start + size], 'cp', [(dev, dev ^ 2) for dev in...]
    pallas_call x1, Pallas kernels: 69.8 us -> 76.9 us  [weights_back(): pl.pallas_call(functools.partial(weights_back_kernel, full_width, min(512...]
    unnamed x27 -> x22, local copies, waits for them, and re-layouts: 25.9 us -> 22.2 us
  transfers between devices with their start and end apart: 9 -> 8, of which waited for: 2 -> 2; matrix products, arithmetic and copies ran while one was open for 4% -> 6% of each run, Pallas kernels for 68% -> 74%
where the time goes in v7:
time: 559 us; the launch traced here: 558 us
  Pallas kernels  458 us (82%)
  waiting for transfers between devices  38.5 us (7%)
  local copies, waits for them, and re-layouts  37.6 us (7%)
  between operations  13.9 us (2%)
  other arithmetic  6.3 us (1%)
    pallas_call x1, Pallas kernels, chain_sum(): pl.pallas_call(functools.partial(chain_kernel, size, n_chunk, 2, min(256,...  168 us
    pallas_call x1, Pallas kernels, weights_back(): pl.pallas_call(functools.partial(weights_back_kernel, full_width, min(512...  76.9 us
    pallas_call x1, Pallas kernels, front(): pl.pallas_call(functools.partial(front_kernel, full_width, min(256, rows)...  49.5 us
    pallas_call x1, Pallas kernels, attend_back(): pl.pallas_call(functools.partial(attend_back_kernel, block, head_dim ** (...  43.6 us
    ppermute x3, waiting for transfers between devices, fetch(): lax.ppermute(x_free[start:start + size], 'cp', [(dev, dev ^ 2) for dev in...  38.5 us
    pallas_call x1, Pallas kernels, heads_to_tokens(): pl.pallas_call(heads_to_tokens_kernel, out_shape=(jax.ShapeDtypeStruct(ar...  28.1 us
    pallas_call x1, Pallas kernels, tokens_to_heads(): pl.pallas_call(tokens_to_heads_kernel, out_shape=jax.ShapeDtypeStruct((he...  27.9 us
    pallas_call x1, Pallas kernels, attend(): pl.pallas_call(functools.partial(attend_kernel, block, head_dim ** (-0.5)...  27.6 us
  transfers between devices with their start and end apart: 8, of which 2 were waited for; matrix products, arithmetic and copies ran while one was open for 6% of the time, Pallas kernels for 74%

profile of v7, /device:TPU:0, one launch (start us, length us, event | category | flops | bytes accessed | tf_op | source)
XLA Modules:
  0.0 558.1 jit_solution(1412633884904632768)
XLA Ops:
  7.2 0.0 copy-start
  7.2 0.0 all-gather.8.cloned.1.call-start
  7.3 1.5 copy-done
  8.8 1.1 constant_dynamic-slice_fusion.2
  9.9 0.0 all-gather.8.cloned.1.call-update
  9.9 0.0 all-gather.6.cloned.1.call-start
  9.9 4.4 copy.21
  14.3 2.6 copy.22
  16.9 4.3 copy.23
  21.2 1.9 fusion
  23.1 1.3 pad_maximum_fusion
  24.4 49.5 %front.1 = (bf16[4,1024,128]{2,1,0:T(8,128)(2,1)}, bf16[4,1024,128]{2,1,0:T(8,128)(2,1)}, bf16[4,1024,128]{2,1,0:T(8,128)(2,1)}) custom-call(bf16[1024,2048]{1,0:T(8,128)(2,1)} %bitcast.48, bf16[512,2048]{1,0:T(8,128)(2,1)} %bitcast.54, bf16[512,2048]{1,0:T(8,128)(2,1)} %bitcast.57, bf16[512,2048]{1,0:T(8,128)(2,1)} %bitcast.63, ...), custom_call_target="tpu_custom_call" | custom-call | tf_op jit(solution)/shard_map/front/pallas_call | solution.py:250
  74.0 27.6 %attend.1 = (bf16[4096,128]{1,0:T(8,128)(2,1)}, f32[1,4096]{1,0:T(1,128)}) custom-call(bf16[4096,128]{1,0:T(8,128)(2,1)} %bitcast.85, bf16[4096,128]{1,0:T(8,128)(2,1)} %bitcast.87, bf16[4096,128]{1,0:T(8,128)(2,1)} %bitcast.89), custom_call_target="tpu_custom_call" | custom-call | flops 4294967296 | bytes 4194304 | tf_op jit(solution)/shard_map/attend/pallas_call | solution.py:303
  101.6 0.7 collective-permute-start
  102.3 28.1 %heads_to_tokens.1 = (bf16[4,1024,128]{2,1,0:T(8,128)(2,1)}, bf16[4,4,256,128]{3,2,1,0:T(8,128)(2,1)}) custom-call(bf16[4,1024,128]{2,1,0:T(8,128)(2,1)} %bitcast.73), custom_call_target="tpu_custom_call" | custom-call | tf_op jit(solution)/shard_map/heads_to_tokens/pallas_call | solution.py:108
  130.4 16.3 %post.1 = (bf16[256,4096]{1,0:T(8,128)(2,1)}, bf16[4,4,256,128]{3,2,1,0:T(8,128)(2,1)}, f32[1,2048]{1,0:T(1,128)}) custom-call(bf16[4,4,256,128]{3,2,1,0:T(8,128)(2,1)} %get-tuple-element.55.o_ref, bf16[4,256,2048]{2,1,0:T(8,128)(2,1)} %bitcast.69, bf16[4,256,2048]{2,1,0:T(8,128)(2,1)} %collective-permute-done.other_ref, bf16[1024,2048]{1,0:T(8,128)(2,1)} %bitcast.49, ...), custom_call_target="tpu_custom_call" | custom-call | flops 4294967296 | bytes 16777216 | tf_op jit(solution)/shard_map/post/pallas_call | solution.py:429
  146.7 27.9 %tokens_to_heads.1 = bf16[4,1024,128]{2,1,0:T(8,128)(2,1)} custom-call(bf16[4,4,256,128]{3,2,1,0:T(8,128)(2,1)} %get-tuple-element.58.in_ref), custom_call_target="tpu_custom_call" | custom-call | tf_op jit(solution)/shard_map/tokens_to_heads/pallas_call | solution.py:159
  174.6 0.0 all-gather.6.cloned.1.call-update
  174.6 0.2 all-gather.10.cloned.1.call-start
  174.8 3.2 slice.21
  178.0 0.3 collective-permute-start.3
  178.3 2.3 slice.19
  180.6 1.8 collective-permute-start.1
  182.3 0.3 broadcast_multiply_fusion
  182.6 0.1 maximum_bitcast_fusion.2
  182.7 0.1 maximum_bitcast_fusion.4
  182.8 2.6 multiply_add_fusion
  185.4 2.3 slice.20
  187.7 0.3 collective-permute-start.2
  188.0 1.2 constant_dynamic-slice_fusion
  189.2 43.6 %attend_back.1 = (f32[4096,128]{1,0:T(8,128)}, f32[4096,128]{1,0:T(8,128)}, bf16[4096,128]{1,0:T(8,128)(2,1)}) custom-call(bf16[4096,128]{1,0:T(8,128)(2,1)} %bitcast.86, bf16[4096,128]{1,0:T(8,128)(2,1)} %bitcast.88, bf16[4096,128]{1,0:T(8,128)(2,1)} %bitcast.90, bf16[4096,128]{1,0:T(8,128)(2,1)} %get-tuple-element.53.o_ref, bf16[4096,128]{1,0:T(8,128)(2,1)} %bitcast.74, ...), custom_call_target="tpu_custom_call" | custom-call | flops 10737418240 | bytes 10485760 | tf_op jit(solution)/shard_map/attend_back/pallas_call | solution.py:367
  232.8 16.3 %collective-permute-done.1.far0_ref = bf16[256,2048]{1,0:T(8,128)(2,1)S(1)} collective-permute-done((bf16[256,2048]{1,0:T(8,128)(2,1)}, bf16[256,2048]{1,0:T(8,128)(2,1)S(1)}, u32[]{:S(2)}, u32[]{:S(2)}) %collective-permute-start.1) | collective-permute-done | bytes 1048608 | tf_op jit(solution)/shard_map/ppermute | solution.py:862
  249.2 22.1 %collective-permute-done.2.far1_ref = bf16[256,2048]{1,0:T(8,128)(2,1)} collective-permute-done((bf16[256,2048]{1,0:T(8,128)(2,1)}, bf16[256,2048]{1,0:T(8,128)(2,1)}, u32[]{:S(2)}, u32[]{:S(2)}) %collective-permute-start.2) | collective-permute-done | bytes 1048608 | tf_op jit(solution)/shard_map/ppermute | solution.py:862
  271.3 1.3 copy-done.3
  272.6 76.9 %weights_back.1 = (f32[3,2048,128]{2,1,0:T(8,128)}, bf16[4,1024,128]{2,1,0:T(8,128)(2,1)}, bf16[4,1024,128]{2,1,0:T(8,128)(2,1)}, bf16[4,1024,128]{2,1,0:T(8,128...) custom-call(bf16[1024,2048]{1,0:T(8,128)(2,1)} %bitcast.53, bf16[256,2048]{1,0:T(8,128)(2,1)} %copy-done.5, ...), custom_call_target="tpu_custom_call" | custom-call | tf_op jit(solution)/shard_map/weights_back/pallas_call | solution.py:812
  349.5 0.0 all-gather.10.cloned.1.call-update
  349.6 0.0 all-reduce.2.cloned.1.call-start
  349.6 0.0 all-gather.6.cloned.1.call-done.gp_ref
  349.6 6.5 %output_weights.1 = f32[4,128,2048]{2,1,0:T(8,128)} custom-call(bf16[4,1024,128]{2,1,0:T(8,128)(2,1)} %get-tuple-element.84.o_ref, bf16[1024,4096]{1,0:T(8,128)(2,1)} %all-gather.6.cloned.1.call-done.gp_ref), custom_call_target="tpu_custom_call" | custom-call | flops 2147483648 | bytes 25165824 | tf_op jit(solution)/shard_map/output_weights/pallas_call | solution.py:453
  356.2 0.0 all-reduce.2.cloned.1.call-update
  356.2 168.2 %chain_sum.1 = bf16[1024,2048]{1,0:T(8,128)(2,1)} custom-call(bf16[4,1024,128]{2,1,0:T(8,128)(2,1)} %get-tuple-element.75.dq_ref, bf16[4,1024,128]{2,1,0:T(8,128)(2,1)} %get-tuple-element.76.dk_ref, bf16[4,1024,128]{2,1,0:T(8,128)(2,1)} %get-tuple-element.77.dv_ref, bf16[512,2048]{1,0:T(8,128)(2,1)} %bitcast.56, bf16[512,2048]{1,0:T(8,128)(2,1)} %bitcast.59, ...), custom_call_target="tpu_custom_call" | custom-call | flops 99999997952 | bytes 33554432 | tf_op jit(solution)/shard_map/chain_sum/pallas_call | solution.py:620
  524.4 0.6 fusion.3
  525.0 4.8 slice_bitcast_fusion
  529.8 13.6 %spread.1 = (f32[2048,4,128]{2,1,0:T(4,128)}, f32[2048,4,128]{2,1,0:T(4,128)}, f32[2048,4,128]{2,1,0:T(4,128)}) custom-call(f32[4,3,2048,128]{3,2,1,0:T(8,128)} %bitcast.60), custom_call_target="tpu_custom_call" | custom-call | flops 3145728 | bytes 25165824 | tf_op jit(solution)/shard_map/spread/pallas_call | solution.py:474
  543.5 4.9 copy.27
  548.4 2.1 copy.28
  550.5 0.6 copy.29
  551.1 0.4 copy-done.1
  (20 shorter events, 0.1 us)
Async XLA Ops:
  7.2 1.6 copy-start
  7.2 94.4 %all-gather.8.cloned.1.call-start = ((), (), s32[]{:S(2)}) async-start(), calls=%async_computation.2 | async-start | bytes 5242880 | tf_op jit(solution)/shard_map/all_gather | solution.py:855
  9.9 339.8 %all-gather.6.cloned.1.call-start = ((), (), s32[]{:S(2)}) async-start(), calls=%async_computation | async-start | bytes 10485760 | tf_op jit(solution)/shard_map/all_gather | solution.py:876
  9.9 4.4 copy-start.4
  101.6 28.8 %collective-permute-start = (bf16[4,256,2048]{2,1,0:T(8,128)(2,1)}, bf16[4,256,2048]{2,1,0:T(8,128)(2,1)}, u32[]{:S(2)}, u32[]{:S(2)}) collective-permute-start(bf16[4,256,2048]{2,1,0:T(8,128)(2,1)} %bitcast.68), channel_id=1, source_target_pairs={{0,1},{1,0},{2,3},{3,2},{4,5},{5,4},{6,7},{7,6},{8,9},{9,8},{10,11... | collective-permute-start | bytes 12582920 | tf_op jit(solution)/shard_map/ppermute | solution.py:869
  174.6 355.2 %all-gather.10.cloned.1.call-start = ((), (), s32[]{:S(2)}) async-start(), calls=%async_computation.3 | async-start | bytes 15728640 | tf_op jit(solution)/shard_map/all_gather | solution.py:894
  178.0 93.3 %collective-permute-start.3 = (bf16[512,2048]{1,0:T(8,128)(2,1)}, bf16[512,2048]{1,0:T(8,128)(2,1)S(1)}, u32[]{:S(2)}, u32[]{:S(2)}) collective-permute-start(bf16[512,2048]{1,0:T(8,128)(2,1)} %slice.21), channel_id=1, source_target_pairs={{0,2},{1,3},{2,0},{3,1},{4,6},{5,7},{6,4},{7,5},{8,10},{9,11},{10,... | collective-permute-start | bytes 6291464 | tf_op jit(solution)/shard_map/ppermute | solution.py:862
  180.6 68.6 %collective-permute-start.1 = (bf16[256,2048]{1,0:T(8,128)(2,1)}, bf16[256,2048]{1,0:T(8,128)(2,1)S(1)}, u32[]{:S(2)}, u32[]{:S(2)}) collective-permute-start(bf16[256,2048]{1,0:T(8,128)(2,1)} %slice.19), channel_id=1, source_target_pairs={{0,2},{1,3},{2,0},{3,1},{4,6},{5,7},{6,4},{7,5},{8,10},{9,11},{10,... | collective-permute-start | bytes 3145736 | tf_op jit(solution)/shard_map/ppermute | solution.py:862
  187.7 83.6 %collective-permute-start.2 = (bf16[256,2048]{1,0:T(8,128)(2,1)}, bf16[256,2048]{1,0:T(8,128)(2,1)}, u32[]{:S(2)}, u32[]{:S(2)}) collective-permute-start(bf16[256,2048]{1,0:T(8,128)(2,1)} %slice.20), channel_id=1, source_target_pairs={{0,2},{1,3},{2,0},{3,1},{4,6},{5,7},{6,4},{7,5},{8,10},{9,11},{10,... | collective-permute-start | bytes 3145736 | tf_op jit(solution)/shard_map/ppermute | solution.py:862
  249.2 22.1 %copy-start.5 = (bf16[256,2048]{1,0:T(8,128)(2,1)}, bf16[256,2048]{1,0:T(8,128)(2,1)S(1)}, u32[]{:S(2)}) copy-start(bf16[256,2048]{1,0:T(8,128)(2,1)S(1)} %collective-permute-done.1.far0_ref) | copy-start | bytes 3145732
  271.3 1.3 copy-start.3
  349.6 193.9 %all-reduce.2.cloned.1.call-start = ((), (), s32[]{:S(2)}) async-start(), calls=%async_computation.1 | async-start | bytes 8388608 | tf_op jit(solution)/shard_map/psum | solution.py:892
  356.2 168.2 %copy-start.7 = (f32[4,2,128]{2,1,0:T(2,128)S(1)}, f32[4,2,128]{2,1,0:T(2,128)}, u32[]{:S(2)}) copy-start(f32[4,2,128]{2,1,0:T(2,128)} %get-tuple-element.85) | copy-start | bytes 12292
  543.4 4.9 copy-start.2
  548.4 2.1 copy-start.6
  548.4 3.1 copy-start.1
Sparse Core Ops, SparseCore 0:
  10.1 84.1 all-gather.7
  174.7 163.1 all-gather.5
  349.7 80.7 all-gather.9
  433.3 85.4 all-reduce.1

commit v8 on v7

--- a/solution.py
+++ b/solution.py
@@ -629,7 +629,7 @@
     )(*grads, *weights, gy)
 
 
-def weights_back_kernel(full_width, sub, x_ref, far0_ref, far1_ref, far2_ref, wq_ref, wk_ref, dq_ref, dk_ref, dv_ref, cos_ref, sin_ref, qg_ref, kg_ref, post_ref,
+def weights_back_kernel(full_width, sub, x_ref, far0_ref, far1_ref, wq_ref, wk_ref, dq_ref, dk_ref, dv_ref, cos_ref, sin_ref, qg_ref, kg_ref, post_ref,
                         dw_ref, exq_ref, exk_ref, exv_ref, gains_ref, post_out,
                         x_buf, wqk_ref, lin_ref, q16_ref, k16_ref, own, slots_tp, mid, slots_cp, done, total, gq_ref, gk_ref, my_gains,
                         x_sem, w_sem, pair_send, pair_recv, tp_send, tp_recv, cp_send, cp_recv, back_send, back_recv, ex_send, ex_recv):
@@ -638,7 +638,7 @@
     rows, head_dim = dq_ref.shape[1:]
     loads = []
     step = far0_ref.shape[0]
-    fars = ((far0_ref, pl.ds(0, step)), (far1_ref, pl.ds(step, step)), (far2_ref, pl.ds(2 * step, rows - 2 * step)))
+    fars = ((far0_ref, pl.ds(0, step)), (far1_ref, pl.ds(step, rows - step)))
     pieces = ((x_ref, 0, pl.ds(0, rows)),) + tuple((ref, 2, part) for ref, part in fars)
     for idx, (src, dist, part) in enumerate(pieces):
         load = pltpu.make_async_copy(src, x_buf.at[dist, part], x_sem.at[idx])
@@ -677,7 +677,7 @@
     sides = ((dq_ref, qg_ref, 0), (dk_ref, kg_ref, 1))
     for order, dist in enumerate((0, 2, 1, 3)):
         blk = flip(me, dist)
-        for load in (loads[0:1], loads[1:4], loads[4:5], loads[5:8])[order]:
+        for load in (loads[0:1], loads[1:3], loads[3:4], loads[4:6])[order]:
             if order < 2:
                 load.wait()
             else:
@@ -795,7 +795,7 @@
     lax.fori_loop(0, x_buf.shape[2] // block, weight_step, 0)
     for copy in copies:
         copy.wait()
-    for load in loads[4:]:
+    for load in loads[3:]:
         load.wait_send()
 
 
@@ -813,13 +813,13 @@
         functools.partial(weights_back_kernel, full_width, min(512, rows)),
         out_shape=(jax.ShapeDtypeStruct((3, d_model, head_dim), jnp.float32), ex, ex, ex,
                    jax.ShapeDtypeStruct((4, 2, head_dim), jnp.float32), jax.ShapeDtypeStruct((1, d_model), jnp.float32)),
-        in_specs=[any_spec] * 6 + [VMEM_SPEC] * 8,
+        in_specs=[any_spec] * 5 + [VMEM_SPEC] * 8,
         out_specs=tuple([VMEM_SPEC] * 6),
         scratch_shapes=[pltpu.VMEM((4, rows, d_model), jnp.bfloat16), pltpu.VMEM((2 * head_dim, d_model), jnp.bfloat16), pltpu.VMEM((4, rows, 2 * head_dim), jnp.float32),
                         pltpu.VMEM(dq.shape, jnp.bfloat16), pltpu.VMEM(dq.shape, jnp.bfloat16),
                         stat, slots, small, slots, small, stat,
                         pltpu.VMEM((1, head_dim), jnp.float32), pltpu.VMEM((1, head_dim), jnp.float32), pltpu.VMEM((2, head_dim), jnp.float32),
-                        dma((4,)), dma((2,)), dma((4,)), dma((4,)), dma((3,)), dma((3,)), dma((3,)), dma((3,)), dma((3,)), dma((3,)), dma((4, 3)), dma((4, 3))],
+                        dma((3,)), dma((2,)), dma((3,)), dma((3,)), dma((3,)), dma((3,)), dma((3,)), dma((3,)), dma((3,)), dma((3,)), dma((4, 3)), dma((4, 3))],
         compiler_params=pltpu.CompilerParams(collective_id=collective_id, has_side_effects=True, vmem_limit_bytes=VMEM_LIMIT),
         name="weights_back",
     )(x, *x_far, wq, wk, dq, dk, dv, cos_tab, sin_tab, q_gain, k_gain, grad_post)
@@ -868,13 +868,11 @@
         o_seq, wo_mine = lax.optimization_barrier((o_seq, wo_mine))
         wo_other = lax.ppermute(wo_mine, "cp", swap_core)
         o_heads, o_tokens = heads_to_tokens(2, o_seq.reshape(block_shape))
-        o_tokens, x_free = lax.optimization_barrier((o_tokens, x))
-        far1 = fetch(piece, piece)
         both, do_tokens, grad_post = post(o_tokens, wo_mine, wo_other, x, gy, post_norm_w[None, :])
         do_seq = tokens_to_heads(3, do_tokens)
         both, do_seq, x_free = lax.optimization_barrier((both, do_seq, x))
         both = lax.all_gather(both, "tp", tiled=True)
-        far2 = fetch(2 * piece, rows - 2 * piece)
+        far1 = fetch(piece, rows - piece)
 
         coarse_cos, coarse_sin = rope_tables(jnp.arange(0, cp_size * rows, 64, dtype=jnp.float32), head_dim)
         fine_cos, fine_sin = (jnp.concatenate([t, t], axis=1)[None] for t in rope_tables(jnp.arange(64, dtype=jnp.float32), head_dim))
@@ -886,7 +884,7 @@
         gains_head = tuple(lax.dynamic_slice_in_dim(w, cp_index, 1, axis=0) for w in (q_norm_w, k_norm_w))
         dq_seq, dk_seq, dv_seq = attend_back(q_seq, k_seq, v_seq, o_seq, do_seq.reshape(seq_shape), lse)
         dw, dq16, dk16, dv16, gains, grad_post = weights_back(
-            4, full_width, x, (far0, far1, far2), turned[0], turned[1],
+            4, full_width, x, (far0, far1), turned[0], turned[1],
             dq_seq.reshape(block_shape), dk_seq.reshape(block_shape), dv_seq.reshape(block_shape), seq_cos, seq_sin, *gains_head, grad_post)
         o_heads, dw = lax.optimization_barrier((o_heads, dw))
         grad_w_o = lax.psum(output_weights(o_heads, both), "cp")

time: 559 us -> 560 us (level)
    ppermute x3 -> x2, waiting for transfers between devices: 38.5 us -> 42.3 us  [fetch(): lax.ppermute(x_free[start:start + size], 'cp', [(dev, dev ^ 2) for dev in...]
    unnamed x22 -> x20, local copies, waits for them, and re-layouts: 22.2 us -> 21.8 us
  transfers between devices with their start and end apart: 8 -> 7, of which waited for: 2 -> 1; matrix products, arithmetic and copies ran while one was open for 6% -> 5% of each run, Pallas kernels for 74% -> 74%
where the time goes in v8:
time: 560 us; the launch traced here: 559 us
  Pallas kernels  458 us (82%)
  waiting for transfers between devices  42.4 us (8%)
  local copies, waits for them, and re-layouts  34.8 us (6%)
  between operations  13.9 us (2%)
  other arithmetic  6.33 us (1%)
    pallas_call x1, Pallas kernels, chain_sum(): pl.pallas_call(functools.partial(chain_kernel, size, n_chunk, 2, min(256,...  169 us
    pallas_call x1, Pallas kernels, weights_back(): pl.pallas_call(functools.partial(weights_back_kernel, full_width, min(512...  76.5 us
    pallas_call x1, Pallas kernels, front(): pl.pallas_call(functools.partial(front_kernel, full_width, min(256, rows)...  49.5 us
    pallas_call x1, Pallas kernels, attend_back(): pl.pallas_call(functools.partial(attend_back_kernel, block, head_dim ** (...  43.2 us
    ppermute x2, waiting for transfers between devices, fetch(): lax.ppermute(x_free[start:start + size], 'cp', [(dev, dev ^ 2) for dev in...  42.3 us
    pallas_call x1, Pallas kernels, heads_to_tokens(): pl.pallas_call(heads_to_tokens_kernel, out_shape=(jax.ShapeDtypeStruct(ar...  28.1 us
    pallas_call x1, Pallas kernels, tokens_to_heads(): pl.pallas_call(tokens_to_heads_kernel, out_shape=jax.ShapeDtypeStruct((he...  27.9 us
    pallas_call x1, Pallas kernels, attend(): pl.pallas_call(functools.partial(attend_kernel, block, head_dim ** (-0.5)...  27.6 us
  transfers between devices with their start and end apart: 7, of which 1 were waited for; matrix products, arithmetic and copies ran while one was open for 5% of the time, Pallas kernels for 74%

profile of v8, /device:TPU:0, one launch (start us, length us, event | category | flops | bytes accessed | tf_op | source)
XLA Modules:
  0.0 558.8 jit_solution(12069016572123627611)
XLA Ops:
  7.2 0.0 copy-start
  7.2 0.0 all-gather.8.cloned.1.call-start
  7.3 1.5 copy-done
  8.8 1.1 constant_dynamic-slice_fusion.2
  9.9 0.0 all-gather.8.cloned.1.call-update
  9.9 0.0 all-gather.6.cloned.1.call-start
  9.9 0.0 copy-start.3
  9.9 4.4 copy.21
  14.3 2.6 copy.22
  16.9 4.3 copy.23
  21.2 1.9 fusion
  23.1 1.3 pad_maximum_fusion
  24.4 49.5 %front.1 = (bf16[4,1024,128]{2,1,0:T(8,128)(2,1)}, bf16[4,1024,128]{2,1,0:T(8,128)(2,1)}, bf16[4,1024,128]{2,1,0:T(8,128)(2,1)}) custom-call(bf16[1024,2048]{1,0:T(8,128)(2,1)} %bitcast.48, bf16[512,2048]{1,0:T(8,128)(2,1)} %bitcast.53, bf16[512,2048]{1,0:T(8,128)(2,1)} %bitcast.56, bf16[512,2048]{1,0:T(8,128)(2,1)} %bitcast.62, ...), custom_call_target="tpu_custom_call" | custom-call | tf_op jit(solution)/shard_map/front/pallas_call | solution.py:250
  74.0 27.6 %attend.1 = (bf16[4096,128]{1,0:T(8,128)(2,1)}, f32[1,4096]{1,0:T(1,128)}) custom-call(bf16[4096,128]{1,0:T(8,128)(2,1)} %bitcast.84, bf16[4096,128]{1,0:T(8,128)(2,1)} %bitcast.86, bf16[4096,128]{1,0:T(8,128)(2,1)} %bitcast.88), custom_call_target="tpu_custom_call" | custom-call | flops 4294967296 | bytes 4194304 | tf_op jit(solution)/shard_map/attend/pallas_call | solution.py:303
  101.6 0.7 collective-permute-start
  102.3 28.1 %heads_to_tokens.1 = (bf16[4,1024,128]{2,1,0:T(8,128)(2,1)}, bf16[4,4,256,128]{3,2,1,0:T(8,128)(2,1)}) custom-call(bf16[4,1024,128]{2,1,0:T(8,128)(2,1)} %bitcast.72), custom_call_target="tpu_custom_call" | custom-call | tf_op jit(solution)/shard_map/heads_to_tokens/pallas_call | solution.py:108
  130.4 0.0 collective-permute-done.other_ref
  130.5 16.3 %post.1 = (bf16[256,4096]{1,0:T(8,128)(2,1)}, bf16[4,4,256,128]{3,2,1,0:T(8,128)(2,1)}, f32[1,2048]{1,0:T(1,128)}) custom-call(bf16[4,4,256,128]{3,2,1,0:T(8,128)(2,1)} %get-tuple-element.52.o_ref, bf16[4,256,2048]{2,1,0:T(8,128)(2,1)} %bitcast.68, bf16[4,256,2048]{2,1,0:T(8,128)(2,1)} %collective-permute-done.other_ref, bf16[1024,2048]{1,0:T(8,128)(2,1)} %bitcast.49, ...), custom_call_target="tpu_custom_call" | custom-call | flops 4294967296 | bytes 16777216 | tf_op jit(solution)/shard_map/post/pallas_call | solution.py:429
  146.8 27.9 %tokens_to_heads.1 = bf16[4,1024,128]{2,1,0:T(8,128)(2,1)} custom-call(bf16[4,4,256,128]{3,2,1,0:T(8,128)(2,1)} %get-tuple-element.55.in_ref), custom_call_target="tpu_custom_call" | custom-call | tf_op jit(solution)/shard_map/tokens_to_heads/pallas_call | solution.py:159
  174.6 0.0 all-gather.6.cloned.1.call-update
  174.7 0.2 all-gather.10.cloned.1.call-start
  174.9 4.0 slice.17
  178.9 0.3 collective-permute-start.2
  179.1 1.3 slice.16
  180.5 1.8 collective-permute-start.1
  182.3 0.3 broadcast_multiply_fusion
  182.6 0.1 maximum_bitcast_fusion.2
  182.7 0.1 maximum_bitcast_fusion.4
  182.8 2.6 multiply_add_fusion
  185.4 1.2 constant_dynamic-slice_fusion
  186.6 43.2 %attend_back.1 = (f32[4096,128]{1,0:T(8,128)}, f32[4096,128]{1,0:T(8,128)}, bf16[4096,128]{1,0:T(8,128)(2,1)}) custom-call(bf16[4096,128]{1,0:T(8,128)(2,1)} %bitcast.85, bf16[4096,128]{1,0:T(8,128)(2,1)} %bitcast.87, bf16[4096,128]{1,0:T(8,128)(2,1)} %bitcast.89, bf16[4096,128]{1,0:T(8,128)(2,1)} %get-tuple-element.51.o_ref, bf16[4096,128]{1,0:T(8,128)(2,1)} %bitcast.73, ...), custom_call_target="tpu_custom_call" | custom-call | flops 10737418240 | bytes 10485760 | tf_op jit(solution)/shard_map/attend_back/pallas_call | solution.py:367
  229.8 42.3 %collective-permute-done.1.far0_ref = bf16[256,2048]{1,0:T(8,128)(2,1)S(1)} collective-permute-done((bf16[256,2048]{1,0:T(8,128)(2,1)S(1)}, bf16[256,2048]{1,0:T(8,128)(2,1)S(1)}, u32[]{:S(2)}, u32[]{:S(2)}) %collective-permute-start.1) | collective-permute-done | bytes 1048608 | tf_op jit(solution)/shard_map/ppermute | solution.py:862
  272.1 0.0 collective-permute-done.2.far1_ref
  272.1 1.0 copy-done.4
  273.1 76.5 %weights_back.1 = (f32[3,2048,128]{2,1,0:T(8,128)}, bf16[4,1024,128]{2,1,0:T(8,128)(2,1)}, bf16[4,1024,128]{2,1,0:T(8,128)(2,1)}, bf16[4,1024,128]{2,1,0:T(8,128...) custom-call(bf16[1024,2048]{1,0:T(8,128)(2,1)} %bitcast.52, bf16[256,2048]{1,0:T(8,128)(2,1)} %copy-done.4, ...), custom_call_target="tpu_custom_call" | custom-call | tf_op jit(solution)/shard_map/weights_back/pallas_call | solution.py:812
  349.5 0.0 all-gather.10.cloned.1.call-update
  349.6 0.0 all-reduce.2.cloned.1.call-start
  349.6 0.0 all-gather.6.cloned.1.call-done.gp_ref
  349.6 6.4 %output_weights.1 = f32[4,128,2048]{2,1,0:T(8,128)} custom-call(bf16[4,1024,128]{2,1,0:T(8,128)(2,1)} %get-tuple-element.80.o_ref, bf16[1024,4096]{1,0:T(8,128)(2,1)} %all-gather.6.cloned.1.call-done.gp_ref), custom_call_target="tpu_custom_call" | custom-call | flops 2147483648 | bytes 25165824 | tf_op jit(solution)/shard_map/output_weights/pallas_call | solution.py:453
  356.1 0.0 all-reduce.2.cloned.1.call-update
  356.1 169.1 %chain_sum.1 = bf16[1024,2048]{1,0:T(8,128)(2,1)} custom-call(bf16[4,1024,128]{2,1,0:T(8,128)(2,1)} %get-tuple-element.71.dq_ref, bf16[4,1024,128]{2,1,0:T(8,128)(2,1)} %get-tuple-element.72.dk_ref, bf16[4,1024,128]{2,1,0:T(8,128)(2,1)} %get-tuple-element.73.dv_ref, bf16[512,2048]{1,0:T(8,128)(2,1)} %bitcast.55, bf16[512,2048]{1,0:T(8,128)(2,1)} %bitcast.58, ...), custom_call_target="tpu_custom_call" | custom-call | flops 99999997952 | bytes 33554432 | tf_op jit(solution)/shard_map/chain_sum/pallas_call | solution.py:620
  525.2 0.6 fusion.3
  525.8 4.8 slice_bitcast_fusion
  530.6 13.6 %spread.1 = (f32[2048,4,128]{2,1,0:T(4,128)}, f32[2048,4,128]{2,1,0:T(4,128)}, f32[2048,4,128]{2,1,0:T(4,128)}) custom-call(f32[4,3,2048,128]{3,2,1,0:T(8,128)} %bitcast.59), custom_call_target="tpu_custom_call" | custom-call | flops 3145728 | bytes 25165824 | tf_op jit(solution)/shard_map/spread/pallas_call | solution.py:474
  544.2 4.9 copy.27
  549.2 2.1 copy.28
  551.3 0.6 copy.29
  551.9 0.4 copy-done.1
  (15 shorter events, 0.0 us)
Async XLA Ops:
  7.2 1.6 copy-start
  7.2 94.4 %all-gather.8.cloned.1.call-start = ((), (), s32[]{:S(2)}) async-start(), calls=%async_computation.2 | async-start | bytes 5242880 | tf_op jit(solution)/shard_map/all_gather | solution.py:855
  9.9 339.8 %all-gather.6.cloned.1.call-start = ((), (), s32[]{:S(2)}) async-start(), calls=%async_computation | async-start | bytes 10485760 | tf_op jit(solution)/shard_map/all_gather | solution.py:874
  9.9 4.4 copy-start.3
  101.6 28.9 %collective-permute-start = (bf16[4,256,2048]{2,1,0:T(8,128)(2,1)}, bf16[4,256,2048]{2,1,0:T(8,128)(2,1)}, u32[]{:S(2)}, u32[]{:S(2)}) collective-permute-start(bf16[4,256,2048]{2,1,0:T(8,128)(2,1)} %bitcast.67), channel_id=1, source_target_pairs={{0,1},{1,0},{2,3},{3,2},{4,5},{5,4},{6,7},{7,6},{8,9},{9,8},{10,11... | collective-permute-start | bytes 12582920 | tf_op jit(solution)/shard_map/ppermute | solution.py:869
  174.7 355.9 %all-gather.10.cloned.1.call-start = ((), (), s32[]{:S(2)}) async-start(), calls=%async_computation.3 | async-start | bytes 15728640 | tf_op jit(solution)/shard_map/all_gather | solution.py:892
  178.9 93.2 %collective-permute-start.2 = (bf16[768,2048]{1,0:T(8,128)(2,1)}, bf16[768,2048]{1,0:T(8,128)(2,1)}, u32[]{:S(2)}, u32[]{:S(2)}) collective-permute-start(bf16[768,2048]{1,0:T(8,128)(2,1)} %slice.17), channel_id=1, source_target_pairs={{0,2},{1,3},{2,0},{3,1},{4,6},{5,7},{6,4},{7,5},{8,10},{9,11},{10,... | collective-permute-start | bytes 9437192 | tf_op jit(solution)/shard_map/ppermute | solution.py:862
  180.5 91.6 %collective-permute-start.1 = (bf16[256,2048]{1,0:T(8,128)(2,1)S(1)}, bf16[256,2048]{1,0:T(8,128)(2,1)S(1)}, u32[]{:S(2)}, u32[]{:S(2)}) collective-permute-start(bf16[256,2048]{1,0:T(8,128)(2,1)S(1)} %slice.16), channel_id=1, source_target_pairs={{0,2},{1,3},{2,0},{3,1},{4,6},{5,7},{6,4},{7,5},{8,10},{9,11},{10,... | collective-permute-start | bytes 3145736 | tf_op jit(solution)/shard_map/ppermute | solution.py:862
  272.1 1.0 copy-start.4
  349.6 194.7 %all-reduce.2.cloned.1.call-start = ((), (), s32[]{:S(2)}) async-start(), calls=%async_computation.1 | async-start | bytes 8388608 | tf_op jit(solution)/shard_map/psum | solution.py:890
  356.1 169.1 %copy-start.6 = (f32[4,2,128]{2,1,0:T(2,128)S(1)}, f32[4,2,128]{2,1,0:T(2,128)}, u32[]{:S(2)}) copy-start(f32[4,2,128]{2,1,0:T(2,128)} %get-tuple-element.81) | copy-start | bytes 12292
  544.2 4.9 copy-start.2
  549.2 2.1 copy-start.5
  549.2 3.1 copy-start.1
Sparse Core Ops, SparseCore 0:
  10.1 84.1 all-gather.7
  174.8 163.2 all-gather.5
  349.7 82.2 all-gather.9
  434.8 85.4 all-reduce.1
